TPU v7x, 32 devices: a whole 2x2x4 slice. The times are simulated.
32 devices in a mesh: wide: 16 (over z, y, core), narrow: 2 (over x).
Axes of the slice: x: 2, y: 2, z: 4, core: 2. Of those that a mesh axis runs over, the one named last changes fastest.
Arguments:
- tokens: bfloat16 [16384, 768], P('wide', 'narrow'), may hold values from -6 to 6
- lengths: int32 [16], P('wide'), may hold values from 1 to 1024, as said below
- qkv_weight: bfloat16 [768, 3, 768], P(None, None, 'narrow'), may hold values from -0.21875 to 0.21875
- qv_bias: bfloat16 [2, 768], P(None, 'narrow'), may hold values from -1 to 1
- proj_weight: bfloat16 [768, 768], P('narrow'), may hold values from -0.875 to 0.875
- proj_bias: bfloat16 [768], replicated, may hold values from -3 to 3
- up_weight: bfloat16 [768, 3072], P(None, 'narrow'), may hold values from -0.21875 to 0.21875
- up_bias: bfloat16 [3072], P('narrow'), may hold values from -3 to 3
- down_weight: bfloat16 [3072, 768], P('narrow'), may hold values from -0.109375 to 0.109375
- down_bias: bfloat16 [768], replicated, may hold values from -3 to 3
- first_gain: bfloat16 [768], replicated, may hold values from 0.099609375 to 1.8984375
- first_shift: bfloat16 [768], replicated, may hold values from -2 to 2
- second_gain: bfloat16 [768], replicated, may hold values from 0.099609375 to 1.8984375
- second_shift: bfloat16 [768], replicated, may hold values from -2 to 2
- cotangent: bfloat16 [16384, 768], P('wide', 'narrow'), may hold values from -6 to 6
Outputs:
- layer_out: bfloat16 [16384, 768], P('wide', 'narrow')
- input_grad: bfloat16 [16384, 768], P('wide', 'narrow')
- grad_qkv_weight: float32 [768, 3, 768], P(None, None, 'narrow')
- grad_qv_bias: float32 [2, 768], P(None, 'narrow')
- grad_proj_weight: float32 [768, 768], P('narrow')
- grad_proj_bias: float32 [768], replicated
- grad_up_weight: float32 [768, 3072], P(None, 'narrow')
- grad_up_bias: float32 [3072], P('narrow')
- grad_down_weight: float32 [3072, 768], P('narrow')
- grad_down_bias: float32 [768], replicated
- grad_first_gain: float32 [768], replicated
- grad_first_shift: float32 [768], replicated
- grad_second_gain: float32 [768], replicated
- grad_second_shift: float32 [768], replicated
Inputs may be any that keep to these rules, and one draw needn't show every extreme that they name: `lengths`: some sequence has exactly 1024 live tokens.
All inputs are finite; a program needn't handle non-finite values.
Results may differ from a plain program's by a relative error of at most 0.0097.
Values may be sent and summed in bfloat16 or wider, within the bound.
A program may use at most 192 MiB of HBM per device.

v0:
```python
import jax
import jax.numpy as jnp
from jax import lax
from jax.sharding import PartitionSpec as P

D = 768
HEADS = 12


EPS = 1e-05


def layer_norm(values, norm_gain, norm_shift):
    row_mean = jnp.mean(values, axis=-1, keepdims=True)
    centred = values - row_mean
    spread = jnp.mean(centred * centred, axis=-1, keepdims=True)
    return centred * lax.rsqrt(spread + EPS) * norm_gain + norm_shift


def gelu_tanh(values):
    return jax.nn.gelu(values, approximate=True)


def block_scores(block_q, key_rows, begin_row, length, score_scale):
    raw_scores = (
        jnp.einsum("qhe,khe->hqk", block_q, key_rows, preferred_element_type=jnp.float32)
        * score_scale
    )
    row_pos = begin_row + jnp.arange(block_q.shape[0], dtype=jnp.int32)
    key_pos = jnp.arange(key_rows.shape[0], dtype=jnp.int32)
    allowed = (key_pos[None, :] <= row_pos[:, None]) & (key_pos[None, :] < length)
    return jnp.where(allowed[None], raw_scores, -1e30)


def attend_forward(queries, key_rows, value_rows, lengths):
    seq_len = queries.shape[1]
    block_rows = min(512, seq_len)
    score_scale = queries.shape[3] ** (-0.5)
    starts = jnp.arange(seq_len // block_rows, dtype=jnp.int32) * block_rows

    def single_sequence(seq_items):
        seq_q, seq_k, seq_v, length = seq_items

        def one_block(begin_row):
            block_q = lax.dynamic_slice_in_dim(seq_q, begin_row, block_rows, 0)
            scores = block_scores(block_q, seq_k, begin_row, length, score_scale)
            row_peak = jnp.max(scores, axis=-1, keepdims=True)
            lifted = jnp.exp(scores - row_peak)
            row_total = jnp.sum(lifted, axis=-1, keepdims=True)
            weights = (lifted / row_total).astype(jnp.bfloat16)
            mixed_rows = jnp.einsum(
                "hqk,khe->qhe", weights, seq_v, preferred_element_type=jnp.float32
            )
            return (mixed_rows.astype(jnp.bfloat16), row_peak[..., 0] + jnp.log(row_total[..., 0]))

        return lax.map(one_block, starts)

    return lax.map(single_sequence, (queries, key_rows, value_rows, lengths))


def attend_backward(queries, key_rows, value_rows, grad_mixed, logsum, lengths):
    seq_len = queries.shape[1]
    block_rows = min(512, seq_len)
    score_scale = queries.shape[3] ** (-0.5)
    starts = jnp.arange(seq_len // block_rows, dtype=jnp.int32) * block_rows

    def single_sequence(seq_items):
        seq_q, seq_k, seq_v, seq_grad, seq_logsum, length = seq_items

        def one_block(running, block_items):
            key_acc, value_acc = running
            begin_row, block_logsum = block_items
            block_q = lax.dynamic_slice_in_dim(seq_q, begin_row, block_rows, 0)
            block_grad = lax.dynamic_slice_in_dim(seq_grad, begin_row, block_rows, 0)
            scores = block_scores(block_q, seq_k, begin_row, length, score_scale)
            weights = jnp.exp(scores - block_logsum[:, :, None])
            grad_probs = jnp.einsum(
                "qhe,khe->hqk", block_grad, seq_v, preferred_element_type=jnp.float32
            )
            center = jnp.sum(weights * grad_probs, axis=-1, keepdims=True)
            grad_scores = (weights * (grad_probs - center)).astype(jnp.bfloat16)
            grad_q = (
                jnp.einsum("hqk,khe->qhe", grad_scores, seq_k, preferred_element_type=jnp.float32)
                * score_scale
            )
            key_acc = (
                key_acc
                + jnp.einsum(
                    "hqk,qhe->khe", grad_scores, block_q, preferred_element_type=jnp.float32
                )
                * score_scale
            )
            value_acc = value_acc + jnp.einsum(
                "hqk,qhe->khe",
                weights.astype(jnp.bfloat16),
                block_grad,
                preferred_element_type=jnp.float32,
            )
            return ((key_acc, value_acc), grad_q)

        empty = jnp.zeros(seq_k.shape, jnp.float32)
        (key_grad, value_grad), query_grad = lax.scan(
            one_block, (empty, empty), (starts, seq_logsum)
        )
        return (query_grad.reshape(seq_k.shape), key_grad, value_grad)

    return lax.map(single_sequence, (queries, key_rows, value_rows, grad_mixed, logsum, lengths))


def on_device(
    tokens,
    lengths,
    qkv_weight,
    qv_bias,
    proj_weight,
    proj_bias,
    up_weight,
    up_bias,
    down_weight,
    down_bias,
    first_gain,
    first_shift,
    second_gain,
    second_shift,
    cotangent,
):
    whole_in, whole_cot = (
        lax.all_gather(tokens, "narrow", axis=1, tiled=True),
        lax.all_gather(cotangent, "narrow", axis=1, tiled=True),
    )
    rows_all = whole_in.shape[0]
    model_width = whole_in.shape[1]
    seq_count = lengths.shape[0]
    seq_len = rows_all // seq_count
    local_width = proj_weight.shape[0]
    head_dim = D // HEADS
    local_heads = local_width // head_dim
    column_width = tokens.shape[1]
    offset = lax.axis_index("narrow") * column_width
    flat_qkv = qkv_weight.reshape(model_width, 3 * local_width)
    input_batch = whole_in.astype(jnp.float32)
    normed, first_pull = jax.vjp(
        layer_norm, input_batch, first_gain.astype(jnp.float32), first_shift.astype(jnp.float32)
    )
    normed_low = normed.astype(jnp.bfloat16)
    projected = jnp.dot(normed_low, flat_qkv, preferred_element_type=jnp.float32)
    bias_wide = qv_bias.astype(jnp.float32)
    queries = (projected[:, :local_width] + bias_wide[0]).astype(jnp.bfloat16)
    key_rows = projected[:, local_width : 2 * local_width].astype(jnp.bfloat16)
    value_rows = (projected[:, 2 * local_width :] + bias_wide[1]).astype(jnp.bfloat16)
    split_shape = (seq_count, seq_len, local_heads, head_dim)
    queries = queries.reshape(split_shape)
    key_rows = key_rows.reshape(split_shape)
    value_rows = value_rows.reshape(split_shape)
    mixed_blocks, logsum = attend_forward(queries, key_rows, value_rows, lengths)
    mixed_rows = mixed_blocks.reshape(rows_all, local_width)
    attn_part = jnp.dot(mixed_rows, proj_weight, preferred_element_type=jnp.float32)
    attn_cols = lax.psum_scatter(attn_part, "narrow", scatter_dimension=1, tiled=True)
    proj_cols = lax.dynamic_slice_in_dim(proj_bias.astype(jnp.float32), offset, column_width, 0)
    middle_cols = tokens.astype(jnp.float32) + attn_cols + proj_cols
    middle = lax.all_gather(middle_cols, "narrow", axis=1, tiled=True)
    second, second_pull = jax.vjp(
        layer_norm, middle, second_gain.astype(jnp.float32), second_shift.astype(jnp.float32)
    )
    second_low = second.astype(jnp.bfloat16)
    hidden = jnp.dot(second_low, up_weight, preferred_element_type=jnp.float32) + up_bias.astype(
        jnp.float32
    )
    active, gelu_pull = jax.vjp(gelu_tanh, hidden)
    active_low = active.astype(jnp.bfloat16)
    ffn_part = jnp.dot(active_low, down_weight, preferred_element_type=jnp.float32)
    ffn_cols = lax.psum_scatter(
        ffn_part.astype(jnp.bfloat16), "narrow", scatter_dimension=1, tiled=True
    ).astype(jnp.float32)
    down_cols = lax.dynamic_slice_in_dim(down_bias.astype(jnp.float32), offset, column_width, 0)
    layer_out = (middle_cols + ffn_cols + down_cols).astype(jnp.bfloat16)
    positions = jnp.arange(seq_len, dtype=jnp.int32)
    valid_rows = (positions[None, :] < lengths[:, None]).reshape(rows_all, 1).astype(jnp.float32)
    grad_out = whole_cot.astype(jnp.float32) * valid_rows
    grad_low = grad_out.astype(jnp.bfloat16)
    grad_down = jnp.einsum("tf,td->fd", active_low, grad_low, preferred_element_type=jnp.float32)
    grad_down_bias = jnp.sum(grad_out, axis=0)
    grad_active = jnp.einsum("td,fd->tf", grad_low, down_weight, preferred_element_type=jnp.float32)
    (grad_hidden,) = gelu_pull(grad_active)
    hidden_low = grad_hidden.astype(jnp.bfloat16)
    grad_up = jnp.einsum("td,tf->df", second_low, hidden_low, preferred_element_type=jnp.float32)
    grad_up_bias = jnp.sum(hidden_low.astype(jnp.float32), axis=0)
    second_part = jnp.einsum("tf,df->td", hidden_low, up_weight, preferred_element_type=jnp.float32)
    grad_second = lax.psum(second_part, "narrow")
    middle_norm, grad_second_gain, grad_second_shift = second_pull(grad_second)
    grad_middle = grad_out + middle_norm
    grad_proj_bias = jnp.sum(grad_middle, axis=0)
    middle_low = grad_middle.astype(jnp.bfloat16)
    grad_proj = jnp.einsum("te,td->ed", mixed_rows, middle_low, preferred_element_type=jnp.float32)
    grad_mixed = jnp.einsum(
        "td,ed->te", middle_low, proj_weight, preferred_element_type=jnp.float32
    ).astype(jnp.bfloat16)
    query_grad, key_grad, value_grad = attend_backward(
        queries, key_rows, value_rows, grad_mixed.reshape(split_shape), logsum, lengths
    )
    grad_qkv_low = jnp.concatenate(
        [
            query_grad.reshape(rows_all, local_width),
            key_grad.reshape(rows_all, local_width),
            value_grad.reshape(rows_all, local_width),
        ],
        axis=1,
    ).astype(jnp.bfloat16)
    grad_qkv = jnp.einsum(
        "td,tc->dc", normed_low, grad_qkv_low, preferred_element_type=jnp.float32
    ).reshape(model_width, 3, local_width)
    qkv_wide = grad_qkv_low.astype(jnp.float32)
    grad_qv_bias = jnp.stack(
        [
            jnp.sum(qkv_wide[:, :local_width], axis=0),
            jnp.sum(qkv_wide[:, 2 * local_width :], axis=0),
        ]
    )
    normed_part = jnp.einsum(
        "tc,dc->td", grad_qkv_low, flat_qkv, preferred_element_type=jnp.float32
    )
    grad_normed = lax.psum(normed_part, "narrow")
    input_norm, grad_first_gain, grad_first_shift = first_pull(grad_normed)
    input_full = grad_middle + input_norm
    input_grad = lax.dynamic_slice_in_dim(input_full, offset, column_width, 1).astype(jnp.bfloat16)
    summed = lax.psum(
        (
            grad_qkv,
            grad_qv_bias,
            grad_proj,
            grad_proj_bias,
            grad_up,
            grad_up_bias,
            grad_down,
            grad_down_bias,
            grad_first_gain,
            grad_first_shift,
            grad_second_gain,
            grad_second_shift,
        ),
        "wide",
    )
    factor = 1.0 / (seq_count * lax.axis_size("wide"))
    return (
        layer_out,
        input_grad,
        summed[0] * factor,
        summed[1] * factor,
        summed[2] * factor,
        summed[3] * factor,
        summed[4] * factor,
        summed[5] * factor,
        summed[6] * factor,
        summed[7] * factor,
        summed[8] * factor,
        summed[9] * factor,
        summed[10] * factor,
        summed[11] * factor,
    )


def solution(mesh):
    placed = (
        P("wide", "narrow"),
        P("wide"),
        P(None, None, "narrow"),
        P(None, "narrow"),
        P("narrow", None),
        P(),
        P(None, "narrow"),
        P("narrow"),
        P("narrow", None),
        P(),
        P(),
        P(),
        P(),
        P(),
        P("wide", "narrow"),
    )
    return jax.shard_map(
        on_device,
        mesh=mesh,
        in_specs=placed,
        out_specs=(
            P("wide", "narrow"),
            P("wide", "narrow"),
            P(None, None, "narrow"),
            P(None, "narrow"),
            P("narrow", None),
            P(),
            P(None, "narrow"),
            P("narrow"),
            P("narrow", None),
            P(),
            P(),
            P(),
            P(),
            P(),
        ),
        check_vma=False,
    )
```

profile of v0, /device:TPU:0, one launch (start us, length us, event | category | flops | bytes accessed | tf_op | source)
XLA Modules:
  0.0 767.3 jit_solution(12685677447219709082)
XLA Ops:
  10.1 3.8 copy.44
  13.9 25.6 %all-gather.4.cloned.1.call-done = bf16[1024,768]{1,0:T(8,128)(2,1)} async-done(((bf16[1024,384]{1,0:T(8,128)(2,1)}), bf16[1024,768]{1,0:T(8,128)(2,1)}) %all-gather.4.cloned.1.call-update) | async-done | bytes 1572880 | tf_op jit(solution)/shard_map/all_gather | solution.py:128
  39.5 1.8 convert_reduce_fusion.1
  41.3 2.0 fusion.49
  43.4 4.0 fusion.72
  50.8 1.4 copy.46
  52.2 2.3 copy.45
  54.5 34.3 %while.47 = (s32[]{:T(128)}, bf16[2,512,6,64]{1,3,2,0:T(8,128)(2,1)}, f32[2,6,512]{2,1,0:T(8,128)S(1)}, s32[2]{0:T(128)S(1)}, s32[]{:T(128)}, /*index=5*/bf16[10...) while((s32[]{:T(128)}, ...), condition=%wide.region_5.6_spmd, body=%wide.region_2.5_spmd.sunk | while | flops 844298752 | bytes 51767564 | solution.py:56
  58.7 3.9 fusion.121
  62.7 3.6 fusion.122
  66.3 4.4 fusion.123
  75.9 3.9 fusion.121
  79.8 3.6 fusion.122
  83.5 4.4 fusion.123
  88.8 2.0 copy.48
  91.8 2.7 fusion.79
  95.0 43.1 %reduce-scatter.5.cloned.1.call-done = f32[1024,384]{1,0:T(8,128)} async-done(((f32[1024,768]{1,0:T(8,128)}), f32[1024,384]{1,0:T(8,128)}) %reduce-scatter.5.cloned.1.call-update) | async-done | bytes 1572880 | tf_op jit(solution)/shard_map/reduce_scatter | solution.py:158
  138.1 2.9 add_add_fusion.3
  142.5 43.7 %all-gather.6.cloned.1.call-done = f32[1024,768]{1,0:T(8,128)} async-done(((f32[1024,384]{1,0:T(8,128)}), f32[1024,768]{1,0:T(8,128)}) %all-gather.6.cloned.1.call-update) | async-done | bytes 3145744 | tf_op jit(solution)/shard_map/all_gather | solution.py:161
  186.1 2.1 reduce_sum.171
  188.3 2.5 multiply_reduce_fusion.3
  191.1 6.5 fusion.75
  197.6 17.2 %all-gather.8.cloned.1.call-done = bf16[1024,768]{1,0:T(8,128)(2,1)} async-done(((bf16[1024,384]{1,0:T(8,128)(2,1)}), bf16[1024,768]{1,0:T(8,128)(2,1)}) %all-gather.8.cloned.1.call-update) | async-done | bytes 1572880 | tf_op jit(solution)/shard_map/all_gather | solution.py:129
  214.8 9.4 %convert_reduce_fusion = (f32[1536]{0:T(1024)}, bf16[1024,1536]{1,0:T(8,128)(2,1)S(1)}) fusion(f32[1024,1536]{1,0:T(8,128)} %fusion.75, f32[1536]{0:T(1024)S(1)} %convert_element_type.115, bf16[1536,768]{1,0:T(8,128)(2,1)S(1)} %copy-done, bf16[1024,768]{1,0:T(8,128)(2,1)} %all-gather.8.cloned.1.call-done, f32[1024]{0:T(1024)S(1)} %fusion.65), kind=kOutput, calls=%fused_computation.56 | convolution fusion | flops 2454452736 | bytes 13385728 | tf_op jit(solution)/shard_map/td,fd->tf/dot_general | solution.py:183
  224.1 1.7 copy-done.71
  225.8 4.3 fusion.80
  230.2 8.0 %convolution_convert_fusion = bf16[1024,768]{1,0:T(8,128)(2,1)} fusion(bf16[1536,768]{1,0:T(8,128)(2,1)S(1)} %copy-done, f32[1024,1536]{1,0:T(8,128)} %fusion.75, f32[1536]{0:T(1024)S(1)} %convert_element_type.115), kind=kOutput, calls=%fused_computation.85 | convolution fusion | flops 2432434176 | bytes 10229760 | tf_op jit(solution)/shard_map/dot_general | solution.py:171
  238.2 2.6 copy.53
  240.9 75.2 %all-reduce.6.cloned.1.call-done = f32[1024,768]{1,0:T(8,128)} async-done(((f32[1024,768]{1,0:T(8,128)}), f32[1024,768]{1,0:T(8,128)}) %all-reduce.6.cloned.1.call-update) | async-done | bytes 3145744 | tf_op jit(solution)/shard_map/psum | solution.py:189
  316.1 4.4 multiply_reduce_fusion.1
  320.8 1.4 fusion.78
  323.6 1.7 copy-done.7
  325.3 1.7 convolution_convert_fusion.1
  327.0 58.0 %while.48 = (s32[]{:T(128)}, f32[1024,6,64]{0,2,1:T(8,128)S(1)}, f32[1024,6,64]{0,2,1:T(8,128)}, bf16[2,512,6,64]{1,3,2,0:T(8,128)(2,1)}, s32[2]{0:T(128)S(1)}, ...) while((s32[]{:T(128)}, f32[1024,6,64]{0,2,1:T(8,128)S(1)}, ...), condition=%wide.region_15.16_spmd.clone, body=%wide.region_13.15_spmd.clone.sunk | while | flops 2063661568 | bytes 135891392 | solution.py:102
  331.4 3.1 fusion.133
  334.6 3.5 bitcast_add_fusion.5
  338.1 7.4 multiply_reduce_fusion.5
  345.5 6.9 multiply_convert_fusion.5
  352.4 2.0 fusion.135
  354.5 1.4 bitcast_add_fusion.4
  360.2 3.1 fusion.133
  363.4 3.5 bitcast_add_fusion.5
  366.9 7.4 multiply_reduce_fusion.5
  374.3 6.9 multiply_convert_fusion.5
  381.3 2.0 fusion.135
  383.3 1.5 bitcast_add_fusion.4
  385.0 2.1 copy.49
  389.4 4.0 fusion.70
  393.5 1.8 copy-done.6
  395.3 6.6 fusion.74
  401.9 9.2 %fusion.59 = f32[1536,768]{1,0:T(8,128)} fusion(bf16[1024,768]{1,0:T(8,128)(2,1)S(1)} %copy-done.32, f32[1024]{0:T(1024)S(1)} %copy-done.57, f32[1024,1536]{1,0:T(8,128)} %fusion.75, f32[1536]{0:T(1024)S(1)} %copy-done.59), kind=kOutput, calls=%fused_computation.102 | convolution fusion | flops 2434007040 | bytes 12593152 | tf_op jit(solution)/shard_map/tf,td->fd/dot_general | solution.py:181
  411.2 1.8 fusion.56
  413.7 4.1 fusion.69
  418.5 2.3 copy.54
  420.8 2.2 fusion.68
  425.7 53.7 %all-reduce.8.cloned.1.call-done = f32[1024,768]{1,0:T(8,128)} async-done(((f32[1024,768]{1,0:T(8,128)}), f32[1024,768]{1,0:T(8,128)}) %all-reduce.8.cloned.1.call-update) | async-done | bytes 3145744 | tf_op jit(solution)/shard_map/psum | solution.py:222
  479.4 3.0 fusion.48
  482.5 64.5 %all-reduce = (f32[2,384]{1,0:T(2,128)S(1)}, f32[768]{0:T(1024)S(1)}, f32[1536]{0:T(1024)S(1)}, f32[768]{0:T(1024)S(1)}, f32[768]{0:T(1024)S(1)}, /*index=5*/f32...) all-reduce(f32[2,384]{1,0:T(2,128)S(1)} %pad_maximum_fusion.1, ...), channel_id=1, replica_groups=mesh['wide'=16,'narrow'=2] {'wide'}, use_global_device_ids=true, to_apply=%region_22.23 | all-reduce | flops 6912 | bytes 55296 | tf_op jit(solution)/shard_map/psum | solution.py:226
  547.6 3.1 fusion.77
  554.3 187.6 %all-reduce.10.cloned.1.call-done = (f32[768,3,384]{0,2,1:T(8,128)}, f32[384,768]{1,0:T(8,128)}, f32[768,1536]{1,0:T(8,128)}, f32[1536,768]{1,0:T(8,128)}) async-done(((f32[768,3,384]{0,2,1:T(8,128)}, f32[384,768]{1,0:T(8,128)}, f32[768,1536]{1,0:T(8,128)}, f32[1536,768]{1,0:T(8,128)}), (f32[768,3,384]{0,2,1:T(8,128)}, f32[384,768]{1,0:T(8,128)}, f32[768,1536]{1,0:T(8,128)}, ...) | async-done | bytes 14155792 | tf_op jit(solution)/shard_map/psum | solution.py:226
  741.9 4.1 broadcast_multiply_fusion.2
  746.0 5.2 copy.51
  752.3 5.1 broadcast_multiply_fusion.1
  757.5 2.5 broadcast_multiply_fusion
  (247 shorter events, 33.3 us)
Async XLA Ops:
  7.2 207.6 %copy-start = (bf16[1536,768]{1,0:T(8,128)(2,1)S(1)}, bf16[1536,768]{1,0:T(8,128)(2,1)}, u32[]{:S(2)}) copy-start(bf16[1536,768]{1,0:T(8,128)(2,1)} %param.27) | copy-start | bytes 7077892
  7.2 32.3 %all-gather.4.cloned.1.call-start = ((), (), s32[]{:S(2)}) async-start(), calls=%async_computation.2 | async-start | bytes 2359296 | tf_op jit(solution)/shard_map/all_gather | solution.py:128
  7.9 130.2 %reduce-scatter.5.cloned.1.call-start = ((), (), s32[]{:S(2)}) async-start(), calls=%async_computation.3 | async-start | bytes 4718592 | tf_op jit(solution)/shard_map/reduce_scatter | solution.py:158
  9.4 34.0 %copy-start.42 = (f32[768]{0:T(1024)}, f32[768]{0:T(1024)S(1)}, u32[]{:S(2)}) copy-start(f32[768]{0:T(1024)S(1)} %convert_element_type.105) | copy-start | bytes 9220
  10.1 33.3 %copy-start.62 = (f32[768]{0:T(1024)}, f32[768]{0:T(1024)S(1)}, u32[]{:S(2)}) copy-start(f32[768]{0:T(1024)S(1)} %convert_element_type.106) | copy-start | bytes 9220
  39.5 3.9 copy-start.11
  41.3 6.1 copy-start.38
  43.3 4.0 copy-start.50
  43.4 4.0 copy-start.44
  62.6 3.7 copy-start.9
  62.7 3.7 copy-start.36
  79.8 3.7 copy-start.9
  79.8 3.7 copy-start.36
  88.8 3.0 copy-start.25
  91.8 3.1 copy-start.68
  94.6 91.6 %all-gather.6.cloned.1.call-start = ((), (), s32[]{:S(2)}) async-start(), calls=%async_computation.4 | async-start | bytes 4718592 | tf_op jit(solution)/shard_map/all_gather | solution.py:161
  95.0 47.3 %copy-start.66 = (bf16[768]{0:T(1024)(128)(2,1)S(1)}, bf16[768]{0:T(1024)(128)(2,1)}, u32[]{:S(2)}) copy-start(bf16[768]{0:T(1024)(128)(2,1)} %param.31) | copy-start | bytes 4612
  95.0 47.3 %copy-start.67 = (bf16[768]{0:T(1024)(128)(2,1)S(1)}, bf16[768]{0:T(1024)(128)(2,1)}, u32[]{:S(2)}) copy-start(bf16[768]{0:T(1024)(128)(2,1)} %param.32) | copy-start | bytes 4612
  95.0 47.4 %copy-start.61 = (bf16[1536]{0:T(1024)(128)(2,1)S(1)}, bf16[1536]{0:T(1024)(128)(2,1)}, u32[]{:S(2)}) copy-start(bf16[1536]{0:T(1024)(128)(2,1)} %param.26) | copy-start | bytes 9220
  141.1 73.7 %all-gather.8.cloned.1.call-start = ((), (), s32[]{:S(2)}) async-start(), calls=%async_computation.5 | async-start | bytes 2359296 | tf_op jit(solution)/shard_map/all_gather | solution.py:129
  141.7 174.4 %all-reduce.6.cloned.1.call-start = ((), (), s32[]{:S(2)}) async-start(), calls=%async_computation.6 | async-start | bytes 6291456 | tf_op jit(solution)/shard_map/psum | solution.py:189
  142.4 178.1 %copy-start.46 = (f32[768]{0:T(1024)}, f32[768]{0:T(1024)S(1)}, u32[]{:S(2)}) copy-start(f32[768]{0:T(1024)S(1)} %convert_element_type.112) | copy-start | bytes 9220
  142.4 48.4 %copy-start.64 = (f32[768]{0:T(1024)}, f32[768]{0:T(1024)S(1)}, u32[]{:S(2)}) copy-start(f32[768]{0:T(1024)S(1)} %convert_element_type.113) | copy-start | bytes 9220
  142.4 87.8 %copy-start.58 = (f32[1536]{0:T(1024)}, f32[1536]{0:T(1024)S(1)}, u32[]{:S(2)}) copy-start(f32[1536]{0:T(1024)S(1)} %convert_element_type.115) | copy-start | bytes 18436
  142.5 179.8 %copy-start.56 = (f32[1024]{0:T(1024)}, f32[1024]{0:T(1024)S(1)}, u32[]{:S(2)}) copy-start(f32[1024]{0:T(1024)S(1)} %fusion.65) | copy-start | bytes 12292
  188.2 2.8 copy-start.4
  188.3 132.3 %copy-start.40 = (f32[1024]{0:T(1024)}, f32[1024]{0:T(1024)S(1)}, u32[]{:S(2)}) copy-start(f32[1024]{0:T(1024)S(1)} %broadcast_multiply_fusion.11) | copy-start | bytes 12292
  191.1 129.4 %copy-start.48 = (f32[1024]{0:T(1024)}, f32[1024]{0:T(1024)S(1)}, u32[]{:S(2)}) copy-start(f32[1024]{0:T(1024)S(1)} %fusion.67) | copy-start | bytes 12292
  214.8 11.0 %copy-start.70 = (bf16[768,1536]{1,0:T(8,128)(2,1)S(1)}, bf16[768,1536]{1,0:T(8,128)(2,1)}, u32[]{:S(2)}) copy-start(bf16[768,1536]{1,0:T(8,128)(2,1)} %param.25) | copy-start | bytes 7077892
  230.1 188.4 %reduce-scatter.7.cloned.1.call-start = ((), (), s32[]{:S(2)}) async-start(), calls=%async_computation.8 | async-start | bytes 2359296
  240.8 238.6 %all-reduce.8.cloned.1.call-start = ((), (), s32[]{:S(2)}) async-start(), calls=%async_computation.7 | async-start | bytes 6291456 | tf_op jit(solution)/shard_map/psum | solution.py:222
  316.1 4.4 copy-start.5
  316.1 4.7 copy-start.14
  322.3 3.0 copy-start.26
  323.6 3.4 copy-start.2
  331.4 3.2 copy-start.15
  331.4 3.2 copy-start.28
  334.5 3.5 copy-start.10
  338.1 7.4 copy-start.29
  345.5 6.9 copy-start.34
  360.2 3.1 copy-start.15
  360.2 3.1 copy-start.28
  363.3 3.5 copy-start.10
  366.9 7.4 copy-start.29
  374.3 6.9 copy-start.34
  389.4 4.1 copy-start.41
  389.4 4.1 copy-start.47
  389.4 4.1 copy-start.49
  389.4 4.1 copy-start.65
  393.4 8.4 %copy-start.57 = (f32[1024]{0:T(1024)S(1)}, f32[1024]{0:T(1024)}, u32[]{:S(2)}) copy-start(f32[1024]{0:T(1024)} %copy-done.56) | copy-start | bytes 12292
  393.4 8.4 %copy-start.59 = (f32[1536]{0:T(1024)S(1)}, f32[1536]{0:T(1024)}, u32[]{:S(2)}) copy-start(f32[1536]{0:T(1024)} %copy-done.58) | copy-start | bytes 18436
  393.4 348.5 %all-reduce.10.cloned.1.call-start = ((), (), s32[]{:S(2)}) async-start(), calls=%async_computation.9 | async-start | bytes 28311552 | tf_op jit(solution)/shard_map/psum | solution.py:226
  395.3 6.6 copy-start.32
  401.9 9.2 %copy-start.8 = (f32[1024,768]{1,0:T(8,128)S(1)}, f32[1024,768]{1,0:T(8,128)}, u32[]{:S(2)}) copy-start(f32[1024,768]{1,0:T(8,128)} %copy-done.7) | copy-start | bytes 9437188
  401.9 9.2 %copy-start.17 = (bf16[48,8,2,512]{3,1,2,0:T(8,128)(2,1)S(1)}, bf16[48,8,2,512]{3,1,2,0:T(8,128)(2,1)}, u32[]{:S(2)}) copy-start(bf16[48,8,2,512]{3,1,2,0:T(8,128)(2,1)} %copy-done.16) | copy-start | bytes 2359300
  425.7 56.7 %copy-start.52 = (f32[768]{0:T(1024)S(1)}, f32[768]{0:T(1024)}, u32[]{:S(2)}) copy-start(f32[768]{0:T(1024)} %get-tuple-element.261) | copy-start | bytes 9220
  425.7 56.7 %copy-start.53 = (f32[768]{0:T(1024)S(1)}, f32[768]{0:T(1024)}, u32[]{:S(2)}) copy-start(f32[768]{0:T(1024)} %get-tuple-element.267) | copy-start | bytes 9220
  425.7 56.7 %copy-start.54 = (f32[768]{0:T(1024)S(1)}, f32[768]{0:T(1024)}, u32[]{:S(2)}) copy-start(f32[768]{0:T(1024)} %get-tuple-element.321) | copy-start | bytes 9220
  425.7 56.8 %copy-start.55 = (f32[768]{0:T(1024)S(1)}, f32[768]{0:T(1024)}, u32[]{:S(2)}) copy-start(f32[768]{0:T(1024)} %get-tuple-element.333) | copy-start | bytes 9220
  425.7 56.8 %copy-start.60 = (f32[1536]{0:T(1024)S(1)}, f32[1536]{0:T(1024)}, u32[]{:S(2)}) copy-start(f32[1536]{0:T(1024)} %get-tuple-element.334) | copy-start | bytes 18436
  425.7 121.9 %copy-start.51 = (f32[1024]{0:T(1024)S(1)}, f32[1024]{0:T(1024)}, u32[]{:S(2)}) copy-start(f32[1024]{0:T(1024)} %copy-done.50) | copy-start | bytes 12292
  746.0 5.3 copy-start.33
  752.3 5.1 slice-start
  752.3 5.1 slice-start.1
  (28 other events, 48.8 us)
Sparse Core Ops, SparseCore 0:
  9.5 29.8 all-gather.3
  94.7 43.4 reduce-scatter.4
  141.2 44.8 all-gather.5
  187.5 27.1 all-gather.7
  230.2 85.8 all-reduce.5
  318.2 26.1 reduce-scatter.6
  393.5 85.8 all-reduce.7
  485.1 256.7 all-reduce.9
where the time goes:
time: 777 us; the launch traced here: 767 us
  waiting for transfers between devices  447 us (58%)
  matrix products  114 us (15%)
  other arithmetic  76.5 us (10%)
  blocking collectives  64.5 us (8%)
  local copies, waits for them, and re-layouts  40 us (5%)
  between operations  16 us (2%)
  loops' own time  8.56 us (1%)
    psum x1, waiting for transfers between devices, on_device(): lax.psum((grad_qkv, grad_qv_bias, grad_proj, grad_proj_bias, grad_up, gra...  188 us
    psum x1, waiting for transfers between devices, on_device(): grad_second = lax.psum(second_part, 'narrow')  75.2 us
    psum x1, blocking collectives, on_device(): lax.psum((grad_qkv, grad_qv_bias, grad_proj, grad_proj_bias, grad_up, gra...  64.5 us
    psum x1, waiting for transfers between devices, on_device(): grad_normed = lax.psum(normed_part, 'narrow')  53.7 us
    all_gather x1, waiting for transfers between devices, on_device(): middle = lax.all_gather(middle_cols, 'narrow', axis=1, tiled=True)  43.7 us
    reduce_scatter x1, waiting for transfers between devices, on_device(): lax.psum_scatter(attn_part, 'narrow', scatter_dimension=1, tiled=True)  43.1 us
    unnamed x134, local copies, waits for them, and re-layouts  25.6 us
    all_gather x1, waiting for transfers between devices, on_device(): lax.all_gather(tokens, 'narrow', axis=1, tiled=True)  25.6 us
  transfers between devices with their start and end apart: 8, of which 7 were waited for; matrix products, arithmetic and copies ran while one was open for 17% of the time, Pallas kernels for 0%

commit v1 on v0

v1 whole, which is shorter than its diff:
```python
import functools

import jax
import jax.numpy as jnp
from jax import lax
from jax.experimental import pallas as pl
from jax.experimental.pallas import tpu as pltpu
from jax.sharding import PartitionSpec as P

EPS = 1e-05
HEAD = 64
F32, BF16 = jnp.float32, jnp.bfloat16
NT = (((1,), (1,)), ((), ()))
TN = (((0,), (0,)), ((), ()))
GELU_A, GELU_B = 0.7978845608028654, 0.044715
VMEM_LIMIT = 56 * 1024 * 1024


def dot(a, b):
    return jnp.dot(a, b, preferred_element_type=F32)


def dot_nt(a, b):
    return lax.dot_general(a, b, NT, preferred_element_type=F32)


def dot_tn(a, b):
    return lax.dot_general(a, b, TN, preferred_element_type=F32)


def params(**more):
    return pltpu.CompilerParams(vmem_limit_bytes=VMEM_LIMIT, **more)


def cost(flops, size, trans=0):
    return pl.CostEstimate(flops=int(flops), bytes_accessed=int(size), transcendentals=int(trans))


def lane_part(which, width):
    return pl.ds(pl.multiple_of(which * width, 128), width)


def norm_rows(x):
    mean = jnp.mean(x, axis=-1, keepdims=True)
    cen = x - mean
    var = jnp.mean(cen * cen, axis=-1, keepdims=True)
    r = lax.rsqrt(var + EPS)
    return cen * r, r


def add_rows(ref, first, value):
    total = jnp.sum(value, axis=0, keepdims=True)

    @pl.when(first)
    def _():
        ref[...] = total

    @pl.when(jnp.logical_not(first))
    def _():
        ref[...] += total


def rows_spec(rows, cols, base=0):
    return pl.BlockSpec((rows, cols), lambda i, *_: (i + base, 0))


def whole_spec(shape):
    zeros = (0,) * len(shape)
    return pl.BlockSpec(shape, lambda i, *_: zeros)


def qkv_body(n_ref, own, got, w, bias, gain, shift, xf, low, q, k, v):
    n = n_ref[0]
    cw = own.shape[1]
    xf[:, lane_part(n, cw)] = own[...]
    xf[:, lane_part(1 - n, cw)] = got[...]
    xhat, _ = norm_rows(xf[...].astype(F32))
    y = (xhat * gain[...] + shift[...]).astype(BF16)
    low[...] = y
    q[...] = (dot(y, w[0]) + bias[0:1, :]).astype(BF16) * jnp.asarray(HEAD**-0.5, BF16)
    k[...] = dot(y, w[1]).astype(BF16)
    v[...] = (dot(y, w[2]) + bias[1:2, :]).astype(BF16)


def qkv_call(n, own, got, w, bias, gain, shift, block=256):
    rows, cw = own.shape
    d, lw = w.shape[1], w.shape[2]
    sd = jax.ShapeDtypeStruct
    return pl.pallas_call(
        qkv_body,
        out_shape=(sd((rows, d), BF16), sd((rows, d), BF16)) + (sd((rows, lw), BF16),) * 3,
        grid_spec=pltpu.PrefetchScalarGridSpec(
            num_scalar_prefetch=1,
            grid=(rows // block,),
            in_specs=[rows_spec(block, cw), rows_spec(block, cw)]
            + [whole_spec(a.shape) for a in (w, bias, gain, shift)],
            out_specs=[rows_spec(block, d)] * 2 + [rows_spec(block, lw)] * 3,
        ),
        compiler_params=params(),
        cost_estimate=cost(2 * rows * d * 3 * lw, 2 * (rows * d * 5 + w.size)),
        name="norm_qkv",
    )(n, own, got, w, bias, gain, shift)


def three(x):
    hi = x.astype(BF16).astype(F32)
    mid = (x - hi).astype(BF16).astype(F32)
    return hi, mid, x - hi - mid


def lanes_of(par):
    lane = lax.broadcasted_iota(jnp.int32, (1, 2 * HEAD), 1)
    mine = (lane // HEAD) == par
    return lane, mine, (1 - par) * HEAD


def place(lane, mine, at, base, terms):
    out = jnp.where(mine, base, 0.0)
    for i, term in enumerate(terms):
        out = jnp.where(lane == at + i, term, out)
    return out


def fwd_body(len_ref, q, k, v, o, qa_out, ka, va, *, r0, bq):
    par = pl.program_id(0) % 2
    lane, mine, at = lanes_of(par)
    keys = k.shape[0]
    kpos = lax.broadcasted_iota(jnp.int32, (keys, 1), 0)
    kbias = jnp.where(kpos < len_ref[0], 0.0, -1e30)
    ka[...] = place(lane, mine, at, k[...].astype(F32), [kbias]).astype(BF16)
    va[...] = place(lane, mine, at, v[...].astype(F32), [1.0]).astype(BF16)
    tri = lax.broadcasted_iota(jnp.int32, (bq, bq), 1) <= lax.broadcasted_iota(jnp.int32, (bq, bq), 0)
    for i in range(q.shape[0] // bq):
        nk = r0 + (i + 1) * bq
        rows = pl.ds(i * bq, bq)
        qf = q[rows, :].astype(F32)
        qa = place(lane, mine, at, qf, [1.0])
        s = dot_nt(qa.astype(BF16), ka[0:nk, :])
        edge = jnp.where(tri, s[:, nk - bq :], -1e30)
        m = jnp.max(edge, axis=1, keepdims=True)
        if nk > bq:
            m = jnp.maximum(m, jnp.max(s[:, : nk - bq], axis=1, keepdims=True))
        pv = dot(jnp.exp(edge - m).astype(BF16), va[nk - bq : nk, :])
        if nk > bq:
            pv += dot(jnp.exp(s[:, : nk - bq] - m).astype(BF16), va[0 : nk - bq, :])
        total = jnp.sum(jnp.where(lane == at, pv, 0.0), axis=1, keepdims=True)
        out = (pv / total).astype(BF16).astype(F32)
        old = o[rows, :].astype(F32)
        o[rows, :] = jnp.where(mine, out, jnp.where(par == 0, 0.0, old)).astype(BF16)
        lse = m + jnp.log(total)
        qa_out[0, rows, :] = place(lane, mine, at, qf, [1.0, *three(lse)]).astype(BF16)


def attend_forward(length, q, k, v, r0, rows, bq=256):
    width = q.shape[1]
    heads, pair = width // HEAD, 2 * HEAD
    keys = r0 + rows
    half = lambda h, *_: (0, h // 2)
    sd = jax.ShapeDtypeStruct
    work = 4 * heads * rows * (keys - rows // 2) * HEAD
    return pl.pallas_call(
        functools.partial(fwd_body, r0=r0, bq=bq),
        out_shape=(sd((rows, width), BF16), sd((heads, rows, pair), BF16)),
        grid_spec=pltpu.PrefetchScalarGridSpec(
            num_scalar_prefetch=1,
            grid=(heads,),
            in_specs=[
                pl.BlockSpec((rows, pair), lambda h, *_: (r0 // rows, h // 2)),
                pl.BlockSpec((keys, pair), half),
                pl.BlockSpec((keys, pair), half),
            ],
            out_specs=[
                pl.BlockSpec((rows, pair), half),
                pl.BlockSpec((1, rows, pair), lambda h, *_: (h, 0, 0)),
            ],
            scratch_shapes=[pltpu.VMEM((keys, pair), BF16)] * 2,
        ),
        compiler_params=params(),
        cost_estimate=cost(4 * work, 2 * rows * width * 6, work // 256),
        name="attend_fwd",
    )(length, q, k, v)


def bwd_body(len_ref, qa, k, v, do, o, dq, dk, dv, ka, va, dk_acc, dv_acc, *, r0, bq):
    par = pl.program_id(0) % 2
    lane, mine, at = lanes_of(par)
    keys = k.shape[0]
    kpos = lax.broadcasted_iota(jnp.int32, (keys, 1), 0)
    kbias = jnp.where(kpos < len_ref[0], 0.0, -1e30)
    ka[...] = place(lane, mine, at, k[...].astype(F32), [kbias, -1.0, -1.0, -1.0]).astype(BF16)
    va[...] = place(lane, mine, at, v[...].astype(F32), [-1.0, -1.0, -1.0]).astype(BF16)
    dk_acc[...] = jnp.zeros_like(dk_acc)
    dv_acc[...] = jnp.zeros_like(dv_acc)
    tri = lax.broadcasted_iota(jnp.int32, (bq, bq), 0) <= lax.broadcasted_iota(jnp.int32, (bq, bq), 1)

    def put(ref, rows, new):
        old = ref[rows, :].astype(F32)
        ref[rows, :] = jnp.where(mine, new, jnp.where(par == 0, 0.0, old)).astype(BF16)

    for i in range(qa.shape[1] // bq):
        rows = pl.ds(i * bq, bq)
        qb = qa[0, rows, :]
        df = do[rows, :].astype(F32)
        delta = jnp.sum(jnp.where(mine, df * o[rows, :].astype(F32), 0.0), axis=1, keepdims=True)
        db = place(lane, mine, at, df, three(delta)).astype(BF16)
        dqs = None
        for j in range((r0 + i * bq) // bq + 1):
            cols = pl.ds(j * bq, bq)
            kb, vb = ka[cols, :], va[cols, :]
            s = dot_nt(kb, qb)
            if j * bq == r0 + i * bq:
                s = jnp.where(tri, s, -1e30)
            p = jnp.exp(s)
            ds = (p * dot_nt(vb, db)).astype(BF16)
            dv_acc[cols, :] += dot(p.astype(BF16), db)
            dk_acc[cols, :] += dot(ds, qb)
            part = dot_tn(ds, kb)
            dqs = part if dqs is None else dqs + part
        put(dq, rows, dqs * HEAD**-0.5)
    put(dk, pl.ds(0, keys), dk_acc[...])
    put(dv, pl.ds(0, keys), dv_acc[...])


def attend_backward(length, qa, k, v, do, o, r0, rows, bq=256):
    width = k.shape[1]
    heads, pair = width // HEAD, 2 * HEAD
    keys = r0 + rows
    half = lambda h, *_: (0, h // 2)
    sd = jax.ShapeDtypeStruct
    work = 4 * heads * rows * (keys - rows // 2) * HEAD
    return pl.pallas_call(
        functools.partial(bwd_body, r0=r0, bq=bq),
        out_shape=(sd((rows, width), BF16), sd((keys, width), BF16), sd((keys, width), BF16)),
        grid_spec=pltpu.PrefetchScalarGridSpec(
            num_scalar_prefetch=1,
            grid=(heads,),
            in_specs=[
                pl.BlockSpec((1, rows, pair), lambda h, *_: (h, 0, 0)),
                pl.BlockSpec((keys, pair), half),
                pl.BlockSpec((keys, pair), half),
                pl.BlockSpec((rows, pair), half),
                pl.BlockSpec((rows, pair), half),
            ],
            out_specs=[
                pl.BlockSpec((rows, pair), half),
                pl.BlockSpec((keys, pair), half),
                pl.BlockSpec((keys, pair), half),
            ],
            scratch_shapes=[pltpu.VMEM((keys, pair), BF16)] * 2 + [pltpu.VMEM((keys, pair), F32)] * 2,
        ),
        compiler_params=params(),
        cost_estimate=cost(10 * work, 2 * rows * width * 9, work // 256),
        name="attend_bwd",
    )(length, qa, k, v, do, o)


def mlp_body(
    s_ref, xf, mo, mr, pwo, pwr, pb, gain, shift, up, ub, down, db, co, cr,
    mid, second, active, gh, cf, lo, send, gs, sum_ub, sum_db,
    *, r0,
):
    n, length = s_ref[0], s_ref[1]
    i = pl.program_id(0)
    rows, cw = co.shape
    m = xf[...].astype(F32) + (dot(mo[...], pwo[...]) + dot(mr[...], pwr[...])) + pb[...]
    mid[...] = m
    xhat, _ = norm_rows(m)
    sec = (xhat * gain[...] + shift[...]).astype(BF16)
    second[...] = sec
    hid = dot(sec, up[...]) + ub[...]
    sq = hid * hid
    t = jnp.tanh(GELU_A * (hid + GELU_B * (sq * hid)))
    half = 0.5 * (1.0 + t)
    act = (hid * half).astype(BF16)
    active[...] = act
    slope = half + (0.5 * hid) * (1.0 - t * t) * (GELU_A + (3.0 * GELU_A * GELU_B) * sq)
    mine, other = lane_part(n, cw), lane_part(1 - n, cw)
    lo[...] = mid[:, mine] + dot(act, down[:, mine]) + db[:, mine]
    send[...] = dot(act, down[:, other]).astype(BF16)
    pos = r0 + i * rows + lax.broadcasted_iota(jnp.int32, (rows, 1), 0)
    live = (pos < length).astype(F32)
    cf[:, mine] = (co[...].astype(F32) * live).astype(BF16)
    cf[:, other] = (cr[...].astype(F32) * live).astype(BF16)
    cot = cf[...]
    ghid = (dot_nt(cot, down[...]) * slope).astype(BF16)
    gh[...] = ghid
    gs[...] = dot_nt(ghid, up[...]).astype(BF16)
    add_rows(sum_ub, i == 0, ghid.astype(F32))
    add_rows(sum_db, i == 0, cot.astype(F32))


def mlp_call(scal, xf, mo, mr, pwo, pwr, pb, gain, shift, up, ub, down, db, co, cr, r0, block=256):
    rows, lw = mo.shape
    d, f = up.shape
    cw = co.shape[1]
    b0 = r0 // block
    sd = jax.ShapeDtypeStruct
    return pl.pallas_call(
        functools.partial(mlp_body, r0=r0),
        out_shape=(
            sd((rows, d), F32), sd((rows, d), BF16), sd((rows, f), BF16), sd((rows, f), BF16),
            sd((rows, d), BF16), sd((rows, cw), F32), sd((rows, cw), BF16), sd((rows, d), BF16),
            sd((1, f), F32), sd((1, d), F32),
        ),
        grid_spec=pltpu.PrefetchScalarGridSpec(
            num_scalar_prefetch=1,
            grid=(rows // block,),
            in_specs=[rows_spec(block, d, b0), rows_spec(block, lw), rows_spec(block, lw)]
            + [whole_spec(a.shape) for a in (pwo, pwr, pb, gain, shift, up, ub, down, db)]
            + [rows_spec(block, cw, b0), rows_spec(block, cw, b0)],
            out_specs=[
                rows_spec(block, d), rows_spec(block, d), rows_spec(block, f), rows_spec(block, f),
                rows_spec(block, d), rows_spec(block, cw), rows_spec(block, cw), rows_spec(block, d),
                whole_spec((1, f)), whole_spec((1, d)),
            ],
        ),
        compiler_params=params(),
        cost_estimate=cost(2 * rows * d * (d + 4 * f), 2 * (rows * d * 8 + rows * f * 2 + 2 * d * f), rows * f),
        name="mlp",
    )(scal, xf, mo, mr, pwo, pwr, pb, gain, shift, up, ub, down, db, co, cr)


def mid_body(s_ref, go, gr, mid, cf, gain, pwo, low, gm_own, gmix, sum_gain, sum_shift, sum_pb):
    n = s_ref[0]
    i = pl.program_id(0)
    cw = gm_own.shape[1]
    g = go[...].astype(F32) + gr[...].astype(F32)
    xhat, r = norm_rows(mid[...])
    gg = g * gain[...]
    m1 = jnp.mean(gg, axis=-1, keepdims=True)
    m2 = jnp.mean(gg * xhat, axis=-1, keepdims=True)
    gm = cf[...].astype(F32) + r * (gg - m1 - xhat * m2)
    mid[...] = gm
    gm_own[...] = mid[:, lane_part(n, cw)]
    gl = gm.astype(BF16)
    low[...] = gl
    gmix[...] = dot_nt(gl, pwo[...]).astype(BF16)
    add_rows(sum_gain, i == 0, g * xhat)
    add_rows(sum_shift, i == 0, g)
    add_rows(sum_pb, i == 0, gm)


def mid_call(scal, go, gr, mid, cf, gain, pwo, block=256):
    rows, d = mid.shape
    lw = pwo.shape[0]
    cw = d // 2
    sd = jax.ShapeDtypeStruct
    return pl.pallas_call(
        mid_body,
        out_shape=(
            sd((rows, d), BF16), sd((rows, cw), F32), sd((rows, lw), BF16),
            sd((1, d), F32), sd((1, d), F32), sd((1, d), F32),
        ),
        grid_spec=pltpu.PrefetchScalarGridSpec(
            num_scalar_prefetch=1,
            grid=(rows // block,),
            in_specs=[rows_spec(block, d)] * 4 + [whole_spec(gain.shape), whole_spec(pwo.shape)],
            out_specs=[rows_spec(block, d), rows_spec(block, cw), rows_spec(block, lw)] + [whole_spec((1, d))] * 3,
        ),
        compiler_params=params(),
        cost_estimate=cost(2 * rows * d * lw, rows * d * 16),
        name="mid_bwd",
    )(scal, go, gr, mid, cf, gain, pwo)


def part_body(s_ref, dq, dk, dv, w, xf, gain, keep, send, stats, tmp):
    n = s_ref[0]
    cw = keep.shape[1]
    for c in range(2):
        g = dot_nt(dq[...], w[0, c * cw : (c + 1) * cw, :])
        g += dot_nt(dk[...], w[1, c * cw : (c + 1) * cw, :])
        g += dot_nt(dv[...], w[2, c * cw : (c + 1) * cw, :])
        tmp[:, c * cw : (c + 1) * cw] = g
    keep[...] = tmp[:, lane_part(n, cw)]
    send[...] = tmp[:, lane_part(1 - n, cw)].astype(BF16)
    xhat, _ = norm_rows(xf[...].astype(F32))
    gg = tmp[...] * gain[...]
    m1 = jnp.mean(gg, axis=-1, keepdims=True)
    m2 = jnp.mean(gg * xhat, axis=-1, keepdims=True)
    lane = lax.broadcasted_iota(jnp.int32, (1, 128), 1)
    both = jnp.where(lane == 0, m1, jnp.where(lane == 1, m2, 0.0))
    stats[...] = both.T[0:8, :]


def part_call(scal, dq, dk, dv, w, xf, gain, block=256):
    rows, d = xf.shape
    lw = dq.shape[1]
    cw = d // 2
    sd = jax.ShapeDtypeStruct
    return pl.pallas_call(
        part_body,
        out_shape=(sd((rows, cw), F32), sd((rows, cw), BF16), sd((8, rows), F32)),
        grid_spec=pltpu.PrefetchScalarGridSpec(
            num_scalar_prefetch=1,
            grid=(rows // block,),
            in_specs=[rows_spec(block, lw)] * 3 + [whole_spec(w.shape), rows_spec(block, d), whole_spec(gain.shape)],
            out_specs=[
                rows_spec(block, cw), rows_spec(block, cw),
                pl.BlockSpec((8, block), lambda i, *_: (0, i)),
            ],
            scratch_shapes=[pltpu.VMEM((block, d), F32)],
        ),
        compiler_params=params(),
        cost_estimate=cost(6 * rows * d * lw, rows * d * 8),
        name="qkv_bwd",
    )(scal, dq, dk, dv, w, xf, gain)


def in_body(s_ref, keep, got, st_own, st_got, xf, gm, gain, out, sum_gain, sum_shift):
    n = s_ref[0]
    i = pl.program_id(0)
    cw = keep.shape[1]
    x = xf[...].astype(F32)
    mean = jnp.mean(x, axis=-1, keepdims=True)
    cen = x - mean
    r = lax.rsqrt(jnp.mean(cen * cen, axis=-1, keepdims=True) + EPS)
    xhat = (xf[:, lane_part(n, cw)].astype(F32) - mean) * r
    st = (st_own[...] + st_got[...]).T
    g = keep[...] + got[...].astype(F32)
    gg = g * gain[:, lane_part(n, cw)]
    out[...] = (gm[...] + r * (gg - st[:, 0:1] - xhat * st[:, 1:2])).astype(BF16)
    add_rows(sum_gain, i == 0, g * xhat)
    add_rows(sum_shift, i == 0, g)


def in_call(scal, keep, got, st_own, st_got, xf, gm, gain, block=256):
    rows, d = xf.shape
    cw = d // 2
    sd = jax.ShapeDtypeStruct
    stat = pl.BlockSpec((8, block), lambda i, *_: (0, i))
    return pl.pallas_call(
        in_body,
        out_shape=(sd((rows, cw), BF16), sd((1, cw), F32), sd((1, cw), F32)),
        grid_spec=pltpu.PrefetchScalarGridSpec(
            num_scalar_prefetch=1,
            grid=(rows // block,),
            in_specs=[rows_spec(block, cw)] * 2 + [stat, stat, rows_spec(block, d), rows_spec(block, cw), whole_spec(gain.shape)],
            out_specs=[rows_spec(block, cw), whole_spec((1, cw)), whole_spec((1, cw))],
        ),
        compiler_params=params(),
        cost_estimate=cost(rows * d * 16, rows * d * 8),
        name="in_bwd",
    )(scal, keep, got, st_own, st_got, xf, gm, gain)


def on_device(
    tokens, lengths, qkv_weight, qv_bias, proj_weight, proj_bias, up_weight, up_bias,
    down_weight, down_bias, first_gain, first_shift, second_gain, second_shift, cotangent,
):
    rows, cw = tokens.shape
    n = lax.axis_index("narrow").astype(jnp.int32)
    n1 = n.reshape(1)
    scal = jnp.concatenate([n1, lengths.astype(jnp.int32)])
    swap = lambda a: lax.ppermute(a, "narrow", [(0, 1), (1, 0)])
    row = lambda a: a.astype(F32).reshape(1, -1)
    w3 = jnp.transpose(qkv_weight, (1, 0, 2))
    gain1, shift1, gain2, shift2 = map(row, (first_gain, first_shift, second_gain, second_shift))

    got_tokens = swap(tokens)
    got_cot = swap(cotangent)
    got_proj = swap(proj_weight)
    xf, low, q, k, v = qkv_call(n1, tokens, got_tokens, w3, qv_bias.astype(F32), gain1, shift1)
    mixed, qa = attend_forward(lengths, q, k, v, 0, rows)
    got_mixed = swap(mixed)
    mid, second, active, gh, cf, lo, send, gs, sum_ub, sum_db = mlp_call(
        scal, xf, mixed, got_mixed, proj_weight, got_proj, row(proj_bias), gain2, shift2,
        up_weight, row(up_bias), down_weight, row(down_bias), cotangent, got_cot, 0,
    )
    got_gs = swap(gs)
    layer_out = (lo + swap(send).astype(F32)).astype(BF16)
    grad_down = dot_tn(active, cf)
    grad_up = dot_tn(second, gh)
    mlow, gm_own, gmix, sum_g2, sum_s2, sum_pb = mid_call(n1, gs, got_gs, mid, cf, gain2, proj_weight)
    dq, dk, dv = attend_backward(lengths, qa, k, v, gmix, mixed, 0, rows)
    keep, nsend, stats = part_call(n1, dq, dk, dv, w3, xf, gain1)
    input_grad, sum_g1, sum_s1 = in_call(n1, keep, swap(nsend), stats, swap(stats), xf, gm_own, gain1)
    grad_proj = dot_tn(mixed, mlow)
    grad_qkv = jnp.stack([dot_tn(low, a) for a in (dq, dk, dv)])
    bias_sums = jnp.concatenate([jnp.sum(a.astype(F32), axis=0) for a in (dq, dv)])

    spread = lambda a: lax.dynamic_update_slice(jnp.zeros((2 * cw,), F32), a.reshape(-1), (n * cw,))
    both = jnp.concatenate([spread(sum_g1), spread(sum_s1)])
    both = both + swap(both)
    small = jnp.concatenate(
        [both] + [a.reshape(-1) for a in (sum_g2, sum_s2, sum_pb, sum_db, sum_ub, bias_sums)]
    )
    d = 2 * cw
    pad = -small.shape[0] % (16 * d)
    small = jnp.pad(small, (0, pad)).reshape(-1, d)
    proj_small = jnp.concatenate([grad_proj.astype(BF16), small.astype(BF16)], axis=0)
    s_down, s_up, s_proj, s_qkv = lax.psum(
        (grad_down.astype(BF16), grad_up.astype(BF16), proj_small, grad_qkv.astype(BF16)), "wide"
    )
    factor = 1.0 / (lengths.shape[0] * lax.axis_size("wide"))
    fin = lambda a: a.astype(F32) * factor
    flat = fin(s_proj[grad_proj.shape[0] :]).reshape(-1)
    lw, ff = proj_weight.shape[0], up_weight.shape[1]
    cuts = [d, d, d, d, d, d, ff, lw, lw]
    pieces, at = [], 0
    for c in cuts:
        pieces.append(flat[at : at + c])
        at += c
    g1, s1, g2, s2, pb, dbs, ubs, qb, vb = pieces
    return (
        layer_out, input_grad, jnp.transpose(fin(s_qkv), (1, 0, 2)), jnp.stack([qb, vb]),
        fin(s_proj[: grad_proj.shape[0]]), pb, fin(s_up), ubs, fin(s_down), dbs, g1, s1, g2, s2,
    )


def solution(mesh):
    split = P("wide", "narrow")
    none3, cols, rows1 = P(None, None, "narrow"), P(None, "narrow"), P("narrow", None)
    return jax.shard_map(
        on_device,
        mesh=mesh,
        in_specs=(
            split, P("wide"), none3, cols, rows1, P(), cols, P("narrow"), rows1, P(), P(), P(), P(), P(), split,
        ),
        out_specs=(
            split, split, none3, cols, rows1, P(), cols, P("narrow"), rows1, P(), P(), P(), P(), P(),
        ),
        check_vma=False,
    )
```

time: 777 us -> 387 us (0.50); the launches traced: 767 us -> 386 us
  waiting for transfers between devices: 447 us -> 223 us
  matrix products: 114 us -> 15.6 us
  Pallas kernels: 0 us -> 86.3 us
  blocking collectives: 64.5 us -> 0 us
  other arithmetic: 76.5 us -> 21.1 us
  local copies, waits for them, and re-layouts: 40 us -> 15.2 us
  starting transfers between devices: 0.67 us -> 10 us
  loops' own time: 8.56 us -> 0 us
    psum x3 -> x1, waiting for transfers between devices: 316 us -> 136 us  [on_device(): lax.psum((grad_down.astype(BF16), grad_up.astype(BF16), proj_small, grad_...]
    dot_general x26 -> x6, matrix products: 114 us -> 15.6 us  [dot_tn(): return lax.dot_general(a, b, TN, preferred_element_type=F32)]
    ppermute x0 -> x9, waiting for transfers between devices: none -> 86.9 us  [on_device(): swap = lambda a: lax.ppermute(a, 'narrow', [(0, 1), (1, 0)])]
    all_gather x3 -> x0, waiting for transfers between devices: 86.4 us -> none  [the longest x1 43.7 us: on_device(): middle = lax.all_gather(middle_cols, 'narrow', axis=1, tiled=True)]
    pallas_call x0 -> x7, Pallas kernels: none -> 86.3 us  [the longest x1 22.5 us: mlp_call(): pl.pallas_call(functools.partial(mlp_body, r0=r0), out_shape=(sd((rows, d...]
    psum x1 -> x0, blocking collectives: 64.5 us -> none  [on_device(): lax.psum((grad_qkv, grad_qv_bias, grad_proj, grad_proj_bias, grad_up, gra...]
    reduce_scatter x1 -> x0, waiting for transfers between devices: 43.1 us -> none  [on_device(): lax.psum_scatter(attn_part, 'narrow', scatter_dimension=1, tiled=True)]
    reduce_sum x12 -> x2, other arithmetic: 29.2 us -> 0.35 us  [on_device(): jnp.sum(a.astype(F32), axis=0)]
  transfers between devices with their start and end apart: 8 -> 10, of which waited for: 7 -> 7; matrix products, arithmetic and copies ran while one was open for 17% -> 6% of each run, Pallas kernels for 0% -> 5%
where the time goes in v1:
time: 387 us; the launch traced here: 386 us
  waiting for transfers between devices  223 us (58%)
  Pallas kernels  86.3 us (22%)
  other arithmetic  21.1 us (5%)
  matrix products  15.6 us (4%)
  local copies, waits for them, and re-layouts  15.2 us (4%)
  between operations  14.9 us (4%)
  starting transfers between devices  10 us (3%)
    psum x1, waiting for transfers between devices, on_device(): lax.psum((grad_down.astype(BF16), grad_up.astype(BF16), proj_small, grad_...  136 us
    ppermute x9, waiting for transfers between devices, on_device(): swap = lambda a: lax.ppermute(a, 'narrow', [(0, 1), (1, 0)])  86.9 us
    pallas_call x1, Pallas kernels, mlp_call(): pl.pallas_call(functools.partial(mlp_body, r0=r0), out_shape=(sd((rows, d...  22.5 us
    pallas_call x1, Pallas kernels, attend_backward(): pl.pallas_call(functools.partial(bwd_body, r0=r0, bq=bq), out_shape=(sd((...  21.6 us
    dot_general x6, matrix products, dot_tn(): return lax.dot_general(a, b, TN, preferred_element_type=F32)  15.6 us
    pallas_call x1, Pallas kernels, attend_forward(): pl.pallas_call(functools.partial(fwd_body, r0=r0, bq=bq), out_shape=(sd((...  14 us
    mul x4, other arithmetic, on_device(): fin = lambda a: a.astype(F32) * factor  10 us
    ppermute x9, starting transfers between devices, on_device(): swap = lambda a: lax.ppermute(a, 'narrow', [(0, 1), (1, 0)])  10 us
  transfers between devices with their start and end apart: 10, of which 7 were waited for; matrix products, arithmetic and copies ran while one was open for 6% of the time, Pallas kernels for 5%

profile of v1, /device:TPU:0, one launch (start us, length us, event | category | flops | bytes accessed | tf_op | source)
XLA Modules:
  0.0 386.4 jit_solution(11084447591811373950)
XLA Ops:
  7.2 3.0 collective-permute-start
  10.3 1.3 reshape.128.gain
  11.6 1.3 convert_element_type.53.bias
  12.9 1.3 reshape.130.shift
  14.8 14.1 %collective-permute-done.got = bf16[1024,384]{1,0:T(8,128)(2,1)S(1)} collective-permute-done((bf16[1024,384]{1,0:T(8,128)(2,1)}, bf16[1024,384]{1,0:T(8,128)(2,1)S(1)}, u32[]{:S(2)}, u32[]{:S(2)}) %collective-permute-start) | collective-permute-done | bytes 786464 | tf_op jit(solution)/shard_map/ppermute | solution.py:454
  28.9 0.9 copy-done.22
  29.7 6.8 %norm_qkv.1 = (bf16[1024,768]{1,0:T(8,128)(2,1)}, bf16[1024,768]{1,0:T(8,128)(2,1)}, bf16[1024,384]{1,0:T(8,128)(2,1)}, bf16[1024,384]{1,0:T(8,128)(2,1)}, bf16[1024,384]{1,0:T(8,128)(2,1)}) custom-call(s32[1]{0:T(128)} %bitcast.n_ref.s_ref, bf16[1024,384]{1,0:T(8,128)(2,1)} %own.1, bf16[1024,384]{1,0:T(8,128)(2,1)} %copy-done.22, ...), custom_call_target="tpu_custom_call" | custom-call | flops 1811939328 | bytes 9633792 | tf_op jit(solution)/shard_map/norm_qkv/pallas_call | solution.py:89
  36.7 14.0 %attend_fwd.1 = (bf16[1024,384]{1,0:T(8,128)(2,1)}, bf16[6,1024,128]{2,1,0:T(8,128)(2,1)}) custom-call(s32[1]{0:T(128)S(6)} %copy.43.len_ref, bf16[1024,384]{1,0:T(8,128)(2,1)} %get-tuple-element.47.q, bf16[1024,384]{1,0:T(8,128)(2,1)} %get-tuple-element.48.k, bf16[1024,384]{1,0:T(8,128)(2,1)} %get-tuple-element.49.v), custom_call_target="tpu_custom_call" | custom-call | flops 3221225472 | bytes 4718592 | tf_op jit(solution)/shard_map/attend_fwd/pallas_call | solution.py:161
  50.7 2.0 collective-permute-start.1
  52.8 0.6 reshape.134.gain
  53.4 0.6 reshape.138.ub
  54.0 0.6 reshape.132.pb
  54.6 0.6 reshape.136.shift
  55.1 0.6 reshape.140.db
  55.7 0.6 pad_add_fusion.s_ref
  56.3 25.1 %collective-permute-done.2.pwr = bf16[384,768]{1,0:T(8,128)(2,1)S(1)} collective-permute-done((bf16[384,768]{1,0:T(8,128)(2,1)S(1)}, bf16[384,768]{1,0:T(8,128)(2,1)S(1)}, u32[]{:S(2)}, u32[]{:S(2)}) %collective-permute-start.2) | collective-permute-done | bytes 589856 | tf_op jit(solution)/shard_map/ppermute | solution.py:454
  81.4 0.8 copy-done.23
  82.2 0.3 copy-done.20
  82.5 0.3 copy-done.21
  82.7 22.5 %mlp.1 = (f32[1024,768]{1,0:T(8,128)}, bf16[1024,768]{1,0:T(8,128)(2,1)}, bf16[1024,1536]{1,0:T(8,128)(2,1)}, bf16[1024,1536]{1,0:T(8,128)(2,1)}, bf16[1024,768]...) custom-call(s32[2]{0:T(128)} %pad_add_fusion.s_ref, ...), custom_call_target="tpu_custom_call" | custom-call | flops 10871635968 | bytes 23592960 | tf_op jit(solution)/shard_map/mlp/pallas_call | solution.py:298
  105.2 1.6 collective-permute-start.5
  106.9 0.7 convert_reduce_fusion.1
  107.6 0.7 convert_reduce_fusion
  108.3 6.6 %convolution_convert_fusion = bf16[1536,768]{1,0:T(8,128)(2,1)} fusion(bf16[1024,1536]{1,0:T(8,128)(2,1)} %get-tuple-element.77, bf16[1024,768]{1,0:T(8,128)(2,1)} %get-tuple-element.56.cf), kind=kOutput, calls=%fused_computation.3 | convolution fusion | flops 2417098752 | bytes 7077888 | tf_op jit(solution)/shard_map/dot_general | solution.py:28
  114.9 4.0 %convolution_convert_fusion.1 = bf16[768,1536]{1,0:T(8,128)(2,1)} fusion(bf16[1024,768]{1,0:T(8,128)(2,1)S(1)} %copy-done.26, bf16[1024,1536]{1,0:T(8,128)(2,1)S(1)} %copy-done.24), kind=kOutput, calls=%fused_computation.4 | convolution fusion | flops 2417098752 | bytes 7077888 | tf_op jit(solution)/shard_map/dot_general | solution.py:28
  118.9 20.5 %collective-permute-done.5.gr = bf16[1024,768]{1,0:T(8,128)(2,1)S(1)} collective-permute-done((bf16[1024,768]{1,0:T(8,128)(2,1)}, bf16[1024,768]{1,0:T(8,128)(2,1)S(1)}, u32[]{:S(2)}, u32[]{:S(2)}) %collective-permute-start.5) | collective-permute-done | bytes 1572896 | tf_op jit(solution)/shard_map/ppermute | solution.py:454
  139.4 1.1 copy-done.2
  140.5 8.4 %mid_bwd.1 = (bf16[1024,768]{1,0:T(8,128)(2,1)}, f32[1024,384]{1,0:T(8,128)}, bf16[1024,384]{1,0:T(8,128)(2,1)}, f32[1,768]{1,0:T(1,128)}, f32[1,768]{1,0:T(1,128)}, /*index=5*/f32[1,768]{1,0:T(1,128)}) custom-call(s32[1]{0:T(128)} %bitcast.n_ref.s_ref, bf16[1024,768]{1,0:T(8,128)(2,1)} %get-tuple-element.54.go, bf16[1024,768]{1,0:T(8,128)(2,1)} %copy-done.2, ...), custom_call_target="tpu_custom_call" | custom-call | flops 603979776 | bytes 12582912 | tf_op jit(solution)/shard_map/mid_bwd/pallas_call | solution.py:348
  148.9 21.6 %attend_bwd.1 = (bf16[1024,384]{1,0:T(8,128)(2,1)}, bf16[1024,384]{1,0:T(8,128)(2,1)}, bf16[1024,384]{1,0:T(8,128)(2,1)}) custom-call(s32[1]{0:T(128)S(6)} %copy.43.len_ref, bf16[6,1024,128]{2,1,0:T(8,128)(2,1)} %get-tuple-element.53.qa, bf16[1024,384]{1,0:T(8,128)(2,1)} %get-tuple-element.48.k, bf16[1024,384]{1,0:T(8,128)(2,1)} %get-tuple-element.49.v, ...), custom_call_target="tpu_custom_call" | custom-call | flops 8053063680 | bytes 7077888 | tf_op jit(solution)/shard_map/attend_bwd/pallas_call | solution.py:231
  170.5 2.2 fusion
  172.8 1.0 fusion.1
  173.8 7.6 %qkv_bwd.1 = (f32[1024,384]{1,0:T(8,128)}, bf16[1024,384]{1,0:T(8,128)(2,1)}, f32[8,1024]{1,0:T(8,128)}) custom-call(s32[1]{0:T(128)} %bitcast.n_ref.s_ref, bf16[1024,384]{1,0:T(8,128)(2,1)} %get-tuple-element.58.dq, bf16[1024,384]{1,0:T(8,128)(2,1)} %get-tuple-element.59.dk, bf16[1024,384]{1,0:T(8,128)(2,1)} %get-tuple-element.60.dv, ...), custom_call_target="tpu_custom_call" | custom-call | flops 1811939328 | bytes 6291456 | tf_op jit(solution)/shard_map/qkv_bwd/pallas_call | solution.py:390
  181.4 1.1 collective-permute-start.6
  182.5 1.0 collective-permute-start.7
  183.5 1.0 fusion.2
  184.5 1.4 pad_maximum_fusion
  185.9 0.4 copy-done.4
  186.4 0.3 copy-done.7
  186.7 0.8 convolution_convert_fusion.2
  187.6 10.9 %collective-permute-done.7.st_got = f32[8,1024]{1,0:T(8,128)S(1)} collective-permute-done((f32[8,1024]{1,0:T(8,128)}, f32[8,1024]{1,0:T(8,128)S(1)}, u32[]{:S(2)}, u32[]{:S(2)}) %collective-permute-start.7) | collective-permute-done | bytes 32800 | tf_op jit(solution)/shard_map/ppermute | solution.py:454
  198.5 0.6 copy-done.10
  199.1 0.3 copy-done.8
  199.4 5.3 %in_bwd.1 = (bf16[1024,384]{1,0:T(8,128)(2,1)}, f32[1,384]{1,0:T(1,128)}, f32[1,384]{1,0:T(1,128)}) custom-call(s32[1]{0:T(128)} %bitcast.n_ref.s_ref, f32[1024,384]{1,0:T(8,128)} %get-tuple-element.61.keep, bf16[1024,384]{1,0:T(8,128)(2,1)} %copy-done.8, f32[8,1024]{1,0:T(8,128)} %get-tuple-element.63.st_own, f32[8,1024]{1,0:T(8,128)} %copy-done.10, ...), custom_call_target="tpu_custom_call" | custom-call | flops 12582912 | bytes 6291456 | tf_op jit(solution)/shard_map/in_bwd/pallas_call | solution.py:431
  204.7 0.7 reduce.2
  205.4 0.7 reduce.3
  206.1 0.3 dynamic_update_slice.6
  206.6 0.6 collective-permute-start.8
  207.5 2.8 collective-permute-done.8
  210.3 0.3 dynamic-update-slice
  211.4 0.2 dynamic-update-slice.5
  212.1 0.9 pad_maximum_fusion.1
  213.0 1.1 copy-done.19
  214.1 0.5 collective-permute-start.4
  214.6 13.6 %collective-permute-done.4 = bf16[1024,384]{1,0:T(8,128)(2,1)S(1)} collective-permute-done((bf16[1024,384]{1,0:T(8,128)(2,1)S(1)}, bf16[1024,384]{1,0:T(8,128)(2,1)S(1)}, u32[]{:S(2)}, u32[]{:S(2)}) %collective-permute-start.4) | collective-permute-done | bytes 786464 | tf_op jit(solution)/shard_map/ppermute | solution.py:454
  228.2 1.1 add_convert_fusion
  229.3 136.3 %all-reduce.4.cloned.1.call-done = (bf16[3,768,384]{2,1,0:T(8,128)(2,1)}, bf16[400,768]{1,0:T(8,128)(2,1)}, bf16[768,1536]{1,0:T(8,128)(2,1)}, bf16[1536,768]{1,0:T(8,128)(2,1)}) async-done(((bf16[3,768,384]{2,1,0:T(8,128)(2,1)}, bf16[400,768]{1,0:T(8,128)(2,1)}, bf16[768,1536]{1,0:T(8,128)(2,1)}, bf16[1536,768]{1,0:T(8,128)(2,1)}), (bf16[3,768,384]{2,1,0:T(8,128)(2,1)}, bf16[400,768]{1,0:T(8,128)(2,1)}, ...) | async-done | bytes 7102480 | tf_op jit(solution)/shard_map/psum | solution.py:491
  365.6 0.7 convert_multiply_fusion.3
  366.3 2.2 convert_multiply_fusion.2
  368.5 0.6 slice_reduce_fusion
  369.1 4.3 %convert_multiply_fusion = f32[1536,768]{1,0:T(8,128)} fusion(bf16[1536,768]{1,0:T(8,128)(2,1)} %get-tuple-element.87), kind=kLoop, calls=%fused_computation | loop fusion | flops 2359296 | bytes 7077888 | tf_op jit(solution)/shard_map/mul | solution.py:495
  373.5 2.8 convert_multiply_fusion.1
  376.3 2.0 multiply_bitcast_fusion
  378.3 0.6 slice.61
  378.9 0.6 pad_maximum_fusion.3
  (76 shorter events, 2.2 us)
Async XLA Ops:
  7.2 358.4 %all-reduce.4.cloned.1.call-start = ((), (), s32[]{:S(2)}) async-start(), calls=%async_computation | async-start | bytes 14204928 | tf_op jit(solution)/shard_map/psum | solution.py:491
  7.2 21.6 %collective-permute-start = (bf16[1024,384]{1,0:T(8,128)(2,1)}, bf16[1024,384]{1,0:T(8,128)(2,1)S(1)}, u32[]{:S(2)}, u32[]{:S(2)}) collective-permute-start(bf16[1024,384]{1,0:T(8,128)(2,1)} %own.1), channel_id=1, source_target_pairs={{0,1},{1,0},{2,3},{3,2},{4,5},{5,4},{6,7},{7,6},{8,9},{9,8},{10,11... | collective-permute-start | bytes 2359304 | tf_op jit(solution)/shard_map/ppermute | solution.py:454
  10.3 71.2 %collective-permute-start.3 = (bf16[1024,384]{1,0:T(8,128)(2,1)}, bf16[1024,384]{1,0:T(8,128)(2,1)S(1)}, u32[]{:S(2)}, u32[]{:S(2)}) collective-permute-start(bf16[1024,384]{1,0:T(8,128)(2,1)} %co.1), channel_id=1, source_target_pairs={{0,1},{1,0},{2,3},{3,2},{4,5},{5,4},{6,7},{7,6},{8,9},{9,8},{10,11... | collective-permute-start | bytes 2359304 | tf_op jit(solution)/shard_map/ppermute | solution.py:454
  28.9 0.9 copy-start.22
  36.6 16.1 %copy-start.9 = (bf16[384,768]{1,0:T(8,128)(2,1)S(1)}, bf16[384,768]{1,0:T(8,128)(2,1)}, u32[]{:S(2)}) copy-start(bf16[384,768]{1,0:T(8,128)(2,1)} %pwo.3) | copy-start | bytes 1769476
  36.6 16.2 %copy-start.15 = (bf16[768]{0:T(1024)(128)(2,1)S(1)}, bf16[768]{0:T(1024)(128)(2,1)}, u32[]{:S(2)}) copy-start(bf16[768]{0:T(1024)(128)(2,1)} %param.27) | copy-start | bytes 4612
  36.6 16.8 %copy-start.11 = (bf16[1536]{0:T(1024)(128)(2,1)S(1)}, bf16[1536]{0:T(1024)(128)(2,1)}, u32[]{:S(2)}) copy-start(bf16[1536]{0:T(1024)(128)(2,1)} %param.22) | copy-start | bytes 9220
  36.6 17.4 %copy-start.16 = (bf16[768]{0:T(1024)(128)(2,1)S(1)}, bf16[768]{0:T(1024)(128)(2,1)}, u32[]{:S(2)}) copy-start(bf16[768]{0:T(1024)(128)(2,1)} %param.20) | copy-start | bytes 4612
  36.6 17.9 %copy-start.17 = (bf16[768]{0:T(1024)(128)(2,1)S(1)}, bf16[768]{0:T(1024)(128)(2,1)}, u32[]{:S(2)}) copy-start(bf16[768]{0:T(1024)(128)(2,1)} %param.28) | copy-start | bytes 4612
  36.6 18.5 %copy-start.18 = (bf16[768]{0:T(1024)(128)(2,1)S(1)}, bf16[768]{0:T(1024)(128)(2,1)}, u32[]{:S(2)}) copy-start(bf16[768]{0:T(1024)(128)(2,1)} %param.24) | copy-start | bytes 4612
  50.7 30.7 %collective-permute-start.1 = (bf16[1024,384]{1,0:T(8,128)(2,1)}, bf16[1024,384]{1,0:T(8,128)(2,1)S(1)}, u32[]{:S(2)}, u32[]{:S(2)}) collective-permute-start(bf16[1024,384]{1,0:T(8,128)(2,1)} %get-tuple-element.50.mo.o), channel_id=1, source_target_pairs={{0,1},{1,0},{2,3},{3,2},{4,5},{5,4},{6,7},{7,6},{8,9},{9,8},{10,11... | collective-permute-start | bytes 2359304 | tf_op jit(solution)/shard_map/ppermute | solution.py:454
  52.7 28.7 %collective-permute-start.2 = (bf16[384,768]{1,0:T(8,128)(2,1)S(1)}, bf16[384,768]{1,0:T(8,128)(2,1)S(1)}, u32[]{:S(2)}, u32[]{:S(2)}) collective-permute-start(bf16[384,768]{1,0:T(8,128)(2,1)S(1)} %copy-done.9), channel_id=1, source_target_pairs={{0,1},{1,0},{2,3},{3,2},{4,5},{5,4},{6,7},{7,6},{8,9},{9,8},{10,11... | collective-permute-start | bytes 1769480 | tf_op jit(solution)/shard_map/ppermute | solution.py:454
  81.4 0.8 copy-start.23
  81.4 1.1 copy-start.20
  81.4 1.3 copy-start.21
  105.2 34.1 %collective-permute-start.5 = (bf16[1024,768]{1,0:T(8,128)(2,1)}, bf16[1024,768]{1,0:T(8,128)(2,1)S(1)}, u32[]{:S(2)}, u32[]{:S(2)}) collective-permute-start(bf16[1024,768]{1,0:T(8,128)(2,1)} %get-tuple-element.54.go), channel_id=1, source_target_pairs={{0,1},{1,0},{2,3},{3,2},{4,5},{5,4},{6,7},{7,6},{8,9},{9,8},{10,11... | collective-permute-start | bytes 4718600 | tf_op jit(solution)/shard_map/ppermute | solution.py:454
  108.3 6.6 %copy-start.24 = (bf16[1024,1536]{1,0:T(8,128)(2,1)S(1)}, bf16[1024,1536]{1,0:T(8,128)(2,1)}, u32[]{:S(2)}) copy-start(bf16[1024,1536]{1,0:T(8,128)(2,1)} %get-tuple-element.76) | copy-start | bytes 9437188
  108.3 6.6 %copy-start.26 = (bf16[1024,768]{1,0:T(8,128)(2,1)S(1)}, bf16[1024,768]{1,0:T(8,128)(2,1)}, u32[]{:S(2)}) copy-start(bf16[1024,768]{1,0:T(8,128)(2,1)} %get-tuple-element.75) | copy-start | bytes 4718596
  139.4 1.1 copy-start.2
  148.9 21.6 %copy-start.27 = (bf16[1024,768]{1,0:T(8,128)(2,1)S(1)}, bf16[1024,768]{1,0:T(8,128)(2,1)}, u32[]{:S(2)}) copy-start(bf16[1024,768]{1,0:T(8,128)(2,1)} %get-tuple-element.66) | copy-start | bytes 4718596
  170.5 2.2 copy-start.25
  173.8 9.7 %copy-start.5 = (bf16[1024,384]{1,0:T(8,128)(2,1)S(1)}, bf16[1024,384]{1,0:T(8,128)(2,1)}, u32[]{:S(2)}) copy-start(bf16[1024,384]{1,0:T(8,128)(2,1)} %get-tuple-element.60.dv) | copy-start | bytes 2359300
  181.4 17.1 %collective-permute-start.6 = (bf16[1024,384]{1,0:T(8,128)(2,1)}, bf16[1024,384]{1,0:T(8,128)(2,1)S(1)}, u32[]{:S(2)}, u32[]{:S(2)}) collective-permute-start(bf16[1024,384]{1,0:T(8,128)(2,1)} %get-tuple-element.62), channel_id=1, source_target_pairs={{0,1},{1,0},{2,3},{3,2},{4,5},{5,4},{6,7},{7,6},{8,9},{9,8},{10,11... | collective-permute-start | bytes 2359304 | tf_op jit(solution)/shard_map/ppermute | solution.py:454
  182.5 16.0 %collective-permute-start.7 = (f32[8,1024]{1,0:T(8,128)}, f32[8,1024]{1,0:T(8,128)S(1)}, u32[]{:S(2)}, u32[]{:S(2)}) collective-permute-start(f32[8,1024]{1,0:T(8,128)} %get-tuple-element.63.st_own), channel_id=1, source_target_pairs={{0,1},{1,0},{2,3},{3,2},{4,5},{5,4},{6,7},{7,6},{8,9},{9,8},{10,11... | collective-permute-start | bytes 98312 | tf_op jit(solution)/shard_map/ppermute | solution.py:454
  184.5 1.9 copy-start.4
  184.5 2.2 copy-start.7
  185.9 1.6 copy-start.13
  185.9 1.6 copy-start.14
  198.5 0.6 copy-start.10
  198.5 0.9 copy-start.8
  199.4 7.8 %copy-start.12 = (f32[1,768]{1,0:T(1,128)S(1)}, f32[1,768]{1,0:T(1,128)}, u32[]{:S(2)}) copy-start(f32[1,768]{1,0:T(1,128)} %get-tuple-element.70) | copy-start | bytes 9220
  199.4 7.8 %copy-start.6 = (bf16[1024,384]{1,0:T(8,128)(2,1)S(1)}, bf16[1024,384]{1,0:T(8,128)(2,1)}, u32[]{:S(2)}) copy-start(bf16[1024,384]{1,0:T(8,128)(2,1)} %get-tuple-element.58.dq) | copy-start | bytes 2359300
  206.6 3.7 collective-permute-start.8
  213.0 1.1 copy-start.19
  213.0 15.3 %copy-start.3 = (f32[1024,384]{1,0:T(8,128)S(1)}, f32[1024,384]{1,0:T(8,128)}, u32[]{:S(2)}) copy-start(f32[1024,384]{1,0:T(8,128)} %get-tuple-element.51) | copy-start | bytes 4718596
  214.1 14.1 %collective-permute-start.4 = (bf16[1024,384]{1,0:T(8,128)(2,1)S(1)}, bf16[1024,384]{1,0:T(8,128)(2,1)S(1)}, u32[]{:S(2)}, u32[]{:S(2)}) collective-permute-start(bf16[1024,384]{1,0:T(8,128)(2,1)S(1)} %copy-done.19), channel_id=1, source_target_pairs={{0,1},{1,0},{2,3},{3,2},{4,5},{5,4},{6,7},{7,6},{8,9},{9,8},{10,11... | collective-permute-start | bytes 2359304 | tf_op jit(solution)/shard_map/ppermute | solution.py:454
  369.1 4.3 %copy-start = (bf16[768,1536]{1,0:T(8,128)(2,1)S(1)}, bf16[768,1536]{1,0:T(8,128)(2,1)}, u32[]{:S(2)}) copy-start(bf16[768,1536]{1,0:T(8,128)(2,1)} %get-tuple-element.86) | copy-start | bytes 7077892
  373.5 2.8 copy-start.1
Sparse Core Ops, SparseCore 0:
  213.1 152.4 all-reduce.3

commit v2 on v1

--- a/solution.py
+++ b/solution.py
@@ -443,6 +443,126 @@
     )(scal, keep, got, st_own, st_got, xf, gm, gain)
 
 
+def bit_of(index, bit):
+    return (index // (1 << bit)) % 2
+
+
+def flip(index, bit):
+    return index + (1 - 2 * bit_of(index, bit)) * (1 << bit)
+
+
+def greet(peers):
+    barrier = pltpu.get_barrier_semaphore()
+    for peer in peers:
+        pl.semaphore_signal(barrier, inc=1, device_id=peer)
+    pl.semaphore_wait(barrier, len(peers))
+
+
+class Chain:
+    def __init__(self, order, src, dst, box, part, send_sem, recv_sem, me):
+        self.order, self.src, self.dst, self.box, self.part = order, src, dst, box, part
+        self.send_sem, self.recv_sem, self.me = send_sem, recv_sem, me
+        self.base, self.size, self.at = 0, src.shape[0], 0
+        self.copy = None
+
+    def _start(self, step, bit, src, dst):
+        self.copy = pltpu.make_async_remote_copy(
+            src_ref=src,
+            dst_ref=dst,
+            send_sem=self.send_sem.at[step],
+            recv_sem=self.recv_sem.at[step],
+            device_id={"wide": flip(self.me, bit)},
+            device_id_type=pl.DeviceIdType.MESH,
+        )
+        self.copy.start()
+
+    def scatter_start(self, step):
+        bit = self.order[step]
+        half = self.size // 2
+        mine = bit_of(self.me, bit)
+        source = self.src if step == 0 else self.part
+        self.keep = self.base + mine * half
+        give = self.base + (1 - mine) * half
+        self._start(step, bit, source.at[pl.ds(give, half)], self.box.at[pl.ds(self.at, half)])
+
+    def scatter_end(self, step):
+        half = self.size // 2
+        source = self.src if step == 0 else self.part
+        target = self.dst if step == len(self.order) - 1 else self.part
+        self.copy.wait()
+
+        def add(i, carry):
+            got = self.box[self.at + i].astype(F32) + source[self.keep + i].astype(F32)
+            target[self.keep + i] = got.astype(BF16)
+            return carry
+
+        lax.fori_loop(0, half, add, 0)
+        self.at += half
+        self.base, self.size = self.keep, half
+
+    def gather_start(self, step):
+        bit = self.order[len(self.order) - 1 - step]
+        region = self.dst.at[pl.ds(self.base, self.size)]
+        self._start(len(self.order) + step, bit, region, region)
+
+    def gather_end(self, step):
+        bit = self.order[len(self.order) - 1 - step]
+        self.copy.wait()
+        self.base = self.base - bit_of(self.me, bit) * self.size
+        self.size *= 2
+
+
+def sum_body(*refs, orders):
+    k = len(orders)
+    srcs, dsts = refs[:k], refs[k : 2 * k]
+    boxes, parts, send_sem, recv_sem = refs[2 * k : 3 * k], refs[3 * k : 4 * k], refs[4 * k], refs[4 * k + 1]
+    me = lax.axis_index("wide")
+    steps = len(orders[0])
+    greet([{"wide": flip(me, bit)} for bit in range(steps)])
+    chains = [
+        Chain(orders[i], srcs[i], dsts[i], boxes[i], parts[i], send_sem.at[i], recv_sem.at[i], me) for i in range(k)
+    ]
+    for chain in chains:
+        chain.scatter_start(0)
+    for step in range(steps):
+        for chain in chains:
+            chain.scatter_end(step)
+            if step + 1 < steps:
+                chain.scatter_start(step + 1)
+            else:
+                chain.gather_start(0)
+    for step in range(steps):
+        for chain in chains:
+            chain.gather_end(step)
+            if step + 1 < steps:
+                chain.gather_start(step + 1)
+
+
+def orders_for(wide):
+    steps = wide.bit_length() - 1
+    first = list(range(steps))
+    second = [0] + first[2:] + first[1:2]
+    return first, second
+
+
+def sum_call(arrays, orders, ident):
+    steps = len(orders[0])
+    vmem = pl.BlockSpec(memory_space=pltpu.VMEM)
+    k = len(arrays)
+    size = sum(a.size for a in arrays)
+    return pl.pallas_call(
+        functools.partial(sum_body, orders=orders),
+        out_shape=tuple(jax.ShapeDtypeStruct(a.shape, BF16) for a in arrays),
+        in_specs=[vmem] * k,
+        out_specs=(vmem,) * k,
+        scratch_shapes=[pltpu.VMEM(a.shape, BF16) for a in arrays] * 2
+        + [pltpu.SemaphoreType.DMA((k, 2 * steps)), pltpu.SemaphoreType.DMA((k, 2 * steps))],
+        compiler_params=params(collective_id=ident, has_side_effects=True),
+        cost_estimate=cost(size * 2, size * 8),
+        name="sum_wide",
+    )(*arrays)
+
+
 def on_device(
     tokens, lengths, qkv_weight, qv_bias, proj_weight, proj_bias, up_weight, up_bias,
     down_weight, down_bias, first_gain, first_shift, second_gain, second_shift, cotangent,
@@ -475,26 +595,31 @@
     keep, nsend, stats = part_call(n1, dq, dk, dv, w3, xf, gain1)
     input_grad, sum_g1, sum_s1 = in_call(n1, keep, swap(nsend), stats, swap(stats), xf, gm_own, gain1)
     grad_proj = dot_tn(mixed, mlow)
-    grad_qkv = jnp.stack([dot_tn(low, a) for a in (dq, dk, dv)])
+    grad_qkv = [dot_tn(low, a) for a in (dq, dk, dv)]
     bias_sums = jnp.concatenate([jnp.sum(a.astype(F32), axis=0) for a in (dq, dv)])
 
-    spread = lambda a: lax.dynamic_update_slice(jnp.zeros((2 * cw,), F32), a.reshape(-1), (n * cw,))
+    d, ff, lw = 2 * cw, up_weight.shape[1], proj_weight.shape[0]
+    wide = lax.axis_size("wide")
+    spread = lambda a: lax.dynamic_update_slice(jnp.zeros((d,), F32), a.reshape(-1), (n * cw,))
     both = jnp.concatenate([spread(sum_g1), spread(sum_s1)])
     both = both + swap(both)
     small = jnp.concatenate(
         [both] + [a.reshape(-1) for a in (sum_g2, sum_s2, sum_pb, sum_db, sum_ub, bias_sums)]
     )
-    d = 2 * cw
-    pad = -small.shape[0] % (16 * d)
-    small = jnp.pad(small, (0, pad)).reshape(-1, d)
-    proj_small = jnp.concatenate([grad_proj.astype(BF16), small.astype(BF16)], axis=0)
-    s_down, s_up, s_proj, s_qkv = lax.psum(
-        (grad_down.astype(BF16), grad_up.astype(BF16), proj_small, grad_qkv.astype(BF16)), "wide"
-    )
-    factor = 1.0 / (lengths.shape[0] * lax.axis_size("wide"))
+    small = jnp.pad(small, (0, -small.shape[0] % (wide * 16 * 128))).reshape(wide, -1, 128).astype(BF16)
+    grad_proj = jnp.stack([grad_proj[:, :cw], grad_proj[:, cw:]])
+    arrays = [grad_down, grad_up, grad_qkv[0], grad_qkv[1], grad_qkv[2], grad_proj]
+    arrays = [a.astype(BF16).reshape(wide, -1, a.shape[-1]) for a in arrays] + [small]
+    first, second_order = orders_for(wide)
+    orders = [first, second_order, first, second_order, first, first, first]
+    sums = sum_call(arrays, orders, 1)
+    factor = 1.0 / (lengths.shape[0] * wide)
     fin = lambda a: a.astype(F32) * factor
-    flat = fin(s_proj[grad_proj.shape[0] :]).reshape(-1)
-    lw, ff = proj_weight.shape[0], up_weight.shape[1]
+    s_down, s_up = fin(sums[0]).reshape(-1, d), fin(sums[1]).reshape(-1, ff)
+    s_qkv = jnp.stack([fin(a).reshape(-1, lw) for a in sums[2:5]])
+    s_proj = fin(sums[5]).reshape(2, lw, cw)
+    s_proj = jnp.concatenate([s_proj[0], s_proj[1]], axis=1)
+    flat = fin(sums[6]).reshape(-1)
     cuts = [d, d, d, d, d, d, ff, lw, lw]
     pieces, at = [], 0
     for c in cuts:
@@ -502,8 +627,8 @@
         at += c
     g1, s1, g2, s2, pb, dbs, ubs, qb, vb = pieces
     return (
-        layer_out, input_grad, jnp.transpose(fin(s_qkv), (1, 0, 2)), jnp.stack([qb, vb]),
-        fin(s_proj[: grad_proj.shape[0]]), pb, fin(s_up), ubs, fin(s_down), dbs, g1, s1, g2, s2,
+        layer_out, input_grad, jnp.transpose(s_qkv, (1, 0, 2)), jnp.stack([qb, vb]),
+        s_proj, pb, s_up, ubs, s_down, dbs, g1, s1, g2, s2,
     )
 
 

time: 387 us -> 345 us (0.89)
  waiting for transfers between devices: 223 us -> 86.3 us
  Pallas kernels: 86.3 us -> 196 us
  between operations: 14.9 us -> 1.59 us
  other arithmetic: 21.1 us -> 17.2 us
    psum x1 -> x0, waiting for transfers between devices: 136 us -> none  [on_device(): lax.psum((grad_down.astype(BF16), grad_up.astype(BF16), proj_small, grad_...]
    pallas_call x0 -> x1, Pallas kernels: none -> 110 us  [sum_call(): pl.pallas_call(functools.partial(sum_body, orders=orders), out_shape=tupl...]
    mul x4 -> x7, other arithmetic: 10 us -> 7.82 us  [on_device(): fin = lambda a: a.astype(F32) * factor]
    unnamed x63 -> x71, local copies, waits for them, and re-layouts: 7.74 us -> 8.64 us
  transfers between devices with their start and end apart: 10 -> 9, of which waited for: 7 -> 6; matrix products, arithmetic and copies ran while one was open for 6% -> 8% of each run, Pallas kernels for 5% -> 6%
where the time goes in v2:
time: 345 us; the launch traced here: 344 us
  Pallas kernels  196 us (57%)
  waiting for transfers between devices  86.3 us (25%)
  other arithmetic  17.2 us (5%)
  matrix products  16.9 us (5%)
  local copies, waits for them, and re-layouts  16.8 us (5%)
  starting transfers between devices  10 us (3%)
    pallas_call x1, Pallas kernels, sum_call(): pl.pallas_call(functools.partial(sum_body, orders=orders), out_shape=tupl...  110 us
    ppermute x9, waiting for transfers between devices, on_device(): swap = lambda a: lax.ppermute(a, 'narrow', [(0, 1), (1, 0)])  86.3 us
    pallas_call x1, Pallas kernels, mlp_call(): pl.pallas_call(functools.partial(mlp_body, r0=r0), out_shape=(sd((rows, d...  22.5 us
    pallas_call x1, Pallas kernels, attend_backward(): pl.pallas_call(functools.partial(bwd_body, r0=r0, bq=bq), out_shape=(sd((...  21.4 us
    dot_general x6, matrix products, dot_tn(): return lax.dot_general(a, b, TN, preferred_element_type=F32)  16.9 us
    pallas_call x1, Pallas kernels, attend_forward(): pl.pallas_call(functools.partial(fwd_body, r0=r0, bq=bq), out_shape=(sd((...  14 us
    ppermute x9, starting transfers between devices, on_device(): swap = lambda a: lax.ppermute(a, 'narrow', [(0, 1), (1, 0)])  10 us
    unnamed x71, local copies, waits for them, and re-layouts  8.64 us
  transfers between devices with their start and end apart: 9, of which 6 were waited for; matrix products, arithmetic and copies ran while one was open for 8% of the time, Pallas kernels for 6%

profile of v2, /device:TPU:0, one launch (start us, length us, event | category | flops | bytes accessed | tf_op | source)
XLA Modules:
  0.0 344.4 jit_solution(4249423752538129036)
XLA Ops:
  0.6 3.0 collective-permute-start
  4.4 1.3 convert_element_type.68.bias
  5.7 1.3 reshape.157.gain
  6.9 1.3 reshape.159.shift
  8.2 14.1 %collective-permute-done.got = bf16[1024,384]{1,0:T(8,128)(2,1)S(1)} collective-permute-done((bf16[1024,384]{1,0:T(8,128)(2,1)}, bf16[1024,384]{1,0:T(8,128)(2,1)S(1)}, u32[]{:S(2)}, u32[]{:S(2)}) %collective-permute-start) | collective-permute-done | bytes 786464 | tf_op jit(solution)/shard_map/ppermute | solution.py:574
  22.3 0.9 copy-done.26
  23.2 6.9 %norm_qkv.1 = (bf16[1024,768]{1,0:T(8,128)(2,1)}, bf16[1024,768]{1,0:T(8,128)(2,1)}, bf16[1024,384]{1,0:T(8,128)(2,1)}, bf16[1024,384]{1,0:T(8,128)(2,1)}, bf16[1024,384]{1,0:T(8,128)(2,1)}) custom-call(s32[1]{0:T(128)} %bitcast.n_ref.s_ref, bf16[1024,384]{1,0:T(8,128)(2,1)} %own.1, bf16[1024,384]{1,0:T(8,128)(2,1)} %copy-done.26, ...), custom_call_target="tpu_custom_call" | custom-call | flops 1811939328 | bytes 9633792 | tf_op jit(solution)/shard_map/norm_qkv/pallas_call | solution.py:89
  30.1 14.0 %attend_fwd.1 = (bf16[1024,384]{1,0:T(8,128)(2,1)}, bf16[6,1024,128]{2,1,0:T(8,128)(2,1)}) custom-call(s32[1]{0:T(128)S(6)} %copy.39.len_ref, bf16[1024,384]{1,0:T(8,128)(2,1)} %get-tuple-element.54.q, bf16[1024,384]{1,0:T(8,128)(2,1)} %get-tuple-element.55.k, bf16[1024,384]{1,0:T(8,128)(2,1)} %get-tuple-element.56.v), custom_call_target="tpu_custom_call" | custom-call | flops 3221225472 | bytes 4718592 | tf_op jit(solution)/shard_map/attend_fwd/pallas_call | solution.py:161
  44.1 2.0 collective-permute-start.1
  46.2 0.6 reshape.161.pb
  46.8 0.6 reshape.163.gain
  47.4 0.6 reshape.165.shift
  48.0 0.6 reshape.167.ub
  48.6 0.6 reshape.169.db
  49.2 0.6 pad_add_fusion.s_ref
  49.8 25.1 %collective-permute-done.2.pwr = bf16[384,768]{1,0:T(8,128)(2,1)S(1)} collective-permute-done((bf16[384,768]{1,0:T(8,128)(2,1)S(1)}, bf16[384,768]{1,0:T(8,128)(2,1)S(1)}, u32[]{:S(2)}, u32[]{:S(2)}) %collective-permute-start.2) | collective-permute-done | bytes 589856 | tf_op jit(solution)/shard_map/ppermute | solution.py:574
  74.9 0.8 copy-done.27
  75.7 0.2 copy-done.24
  75.9 0.2 copy-done.25
  76.2 22.5 %mlp.1 = (f32[1024,768]{1,0:T(8,128)}, bf16[1024,768]{1,0:T(8,128)(2,1)}, bf16[1024,1536]{1,0:T(8,128)(2,1)}, bf16[1024,1536]{1,0:T(8,128)(2,1)}, bf16[1024,768]...) custom-call(s32[2]{0:T(128)} %pad_add_fusion.s_ref, ...), custom_call_target="tpu_custom_call" | custom-call | flops 10871635968 | bytes 23592960 | tf_op jit(solution)/shard_map/mlp/pallas_call | solution.py:298
  98.7 1.6 collective-permute-start.4
  100.3 0.5 collective-permute-start.5
  100.8 6.6 %convolution_convert_fusion.1 = bf16[1536,768]{1,0:T(8,128)(2,1)} fusion(bf16[1024,1536]{1,0:T(8,128)(2,1)} %get-tuple-element.73, bf16[1024,768]{1,0:T(8,128)(2,1)} %get-tuple-element.63.cf), kind=kOutput, calls=%fused_computation.4 | convolution fusion | flops 2417098752 | bytes 7077888 | tf_op jit(solution)/shard_map/dot_general | solution.py:28
  107.5 3.9 %convolution_convert_fusion = bf16[768,1536]{1,0:T(8,128)(2,1)} fusion(bf16[1024,768]{1,0:T(8,128)(2,1)S(1)} %copy-done.30, bf16[1024,1536]{1,0:T(8,128)(2,1)S(1)} %copy-done.28), kind=kOutput, calls=%fused_computation.3 | convolution fusion | flops 2417098752 | bytes 7077888 | tf_op jit(solution)/shard_map/dot_general | solution.py:28
  111.4 7.9 %collective-permute-done.4 = bf16[1024,384]{1,0:T(8,128)(2,1)S(1)} collective-permute-done((bf16[1024,384]{1,0:T(8,128)(2,1)}, bf16[1024,384]{1,0:T(8,128)(2,1)S(1)}, u32[]{:S(2)}, u32[]{:S(2)}) %collective-permute-start.4) | collective-permute-done | bytes 786464 | tf_op jit(solution)/shard_map/ppermute | solution.py:574
  119.3 1.1 add_convert_fusion
  120.4 29.2 %collective-permute-done.5.gr = bf16[1024,768]{1,0:T(8,128)(2,1)S(1)} collective-permute-done((bf16[1024,768]{1,0:T(8,128)(2,1)}, bf16[1024,768]{1,0:T(8,128)(2,1)S(1)}, u32[]{:S(2)}, u32[]{:S(2)}) %collective-permute-start.5) | collective-permute-done | bytes 1572896 | tf_op jit(solution)/shard_map/ppermute | solution.py:574
  149.6 1.1 copy-done.2
  150.8 8.4 %mid_bwd.1 = (bf16[1024,768]{1,0:T(8,128)(2,1)}, f32[1024,384]{1,0:T(8,128)}, bf16[1024,384]{1,0:T(8,128)(2,1)}, f32[1,768]{1,0:T(1,128)}, f32[1,768]{1,0:T(1,128)}, /*index=5*/f32[1,768]{1,0:T(1,128)}) custom-call(s32[1]{0:T(128)} %bitcast.n_ref.s_ref, bf16[1024,768]{1,0:T(8,128)(2,1)} %get-tuple-element.61.go, bf16[1024,768]{1,0:T(8,128)(2,1)} %copy-done.2, ...), custom_call_target="tpu_custom_call" | custom-call | flops 603979776 | bytes 12582912 | tf_op jit(solution)/shard_map/mid_bwd/pallas_call | solution.py:348
  159.2 21.4 %attend_bwd.1 = (bf16[1024,384]{1,0:T(8,128)(2,1)}, bf16[1024,384]{1,0:T(8,128)(2,1)}, bf16[1024,384]{1,0:T(8,128)(2,1)}) custom-call(s32[1]{0:T(128)S(6)} %copy.39.len_ref, bf16[6,1024,128]{2,1,0:T(8,128)(2,1)} %get-tuple-element.60.qa, bf16[1024,384]{1,0:T(8,128)(2,1)} %get-tuple-element.55.k, bf16[1024,384]{1,0:T(8,128)(2,1)} %get-tuple-element.56.v, ...), custom_call_target="tpu_custom_call" | custom-call | flops 8053063680 | bytes 7077888 | tf_op jit(solution)/shard_map/attend_bwd/pallas_call | solution.py:231
  180.6 7.6 %qkv_bwd.1 = (f32[1024,384]{1,0:T(8,128)}, bf16[1024,384]{1,0:T(8,128)(2,1)}, f32[8,1024]{1,0:T(8,128)}) custom-call(s32[1]{0:T(128)} %bitcast.n_ref.s_ref, bf16[1024,384]{1,0:T(8,128)(2,1)} %get-tuple-element.65.dq, bf16[1024,384]{1,0:T(8,128)(2,1)} %get-tuple-element.66.dk, bf16[1024,384]{1,0:T(8,128)(2,1)} %get-tuple-element.67.dv, ...), custom_call_target="tpu_custom_call" | custom-call | flops 1811939328 | bytes 6291456 | tf_op jit(solution)/shard_map/qkv_bwd/pallas_call | solution.py:390
  188.2 1.1 collective-permute-start.6
  189.4 0.9 collective-permute-start.7
  190.4 1.8 convolution_convert_fusion.5
  192.2 0.8 convolution_convert_fusion.2
  193.1 0.9 pad_maximum_fusion.1
  194.0 0.4 copy-done.29
  194.3 1.8 convolution_convert_fusion.4
  196.2 1.9 convolution_convert_fusion.3
  198.1 7.3 %collective-permute-done.7.st_got = f32[8,1024]{1,0:T(8,128)S(1)} collective-permute-done((f32[8,1024]{1,0:T(8,128)}, f32[8,1024]{1,0:T(8,128)S(1)}, u32[]{:S(2)}, u32[]{:S(2)}) %collective-permute-start.7) | collective-permute-done | bytes 32800 | tf_op jit(solution)/shard_map/ppermute | solution.py:574
  205.3 0.6 copy-done.13
  205.9 0.3 copy-done.8
  206.2 5.3 %in_bwd.1 = (bf16[1024,384]{1,0:T(8,128)(2,1)}, f32[1,384]{1,0:T(1,128)}, f32[1,384]{1,0:T(1,128)}) custom-call(s32[1]{0:T(128)} %bitcast.n_ref.s_ref, f32[1024,384]{1,0:T(8,128)} %get-tuple-element.68.keep, bf16[1024,384]{1,0:T(8,128)(2,1)} %copy-done.8, f32[8,1024]{1,0:T(8,128)} %get-tuple-element.70.st_own, f32[8,1024]{1,0:T(8,128)} %copy-done.13, ...), custom_call_target="tpu_custom_call" | custom-call | flops 12582912 | bytes 6291456 | tf_op jit(solution)/shard_map/in_bwd/pallas_call | solution.py:431
  211.5 0.7 reduce.3
  212.2 0.7 reduce.2
  212.9 0.3 dynamic_update_slice.7
  213.4 0.6 collective-permute-start.8
  214.4 2.7 collective-permute-done.8
  217.1 0.3 dynamic-update-slice
  217.4 0.2 dynamic-update-slice.1
  218.2 0.2 dynamic-update-slice.5
  218.9 0.6 pad.5
  219.5 109.6 %sum_wide.1 = (bf16[16,96,768]{2,1,0:T(8,128)(2,1)}, bf16[16,48,1536]{2,1,0:T(8,128)(2,1)}, bf16[16,48,384]{2,1,0:T(8,128)(2,1)}, bf16[16,48,384]{2,1,0:T(8,128)...) custom-call(bf16[16,96,768]{2,1,0:T(8,128)(2,1)} %bitcast.41, ...), custom_call_target="tpu_custom_call" | custom-call | flops 7143424 | bytes 28573696 | tf_op jit(solution)/shard_map/sum_wide/pallas_call | solution.py:553
  329.1 0.9 convert_multiply_fusion.6
  330.0 0.6 fusion.1
  330.6 0.6 slice.63
  331.2 1.2 convert_multiply_fusion.3
  332.7 0.9 copy-done.10
  333.7 1.6 copy-done.1
  335.3 2.8 convert_multiply_fusion.1
  338.1 2.6 convert_multiply_fusion
  340.7 0.6 pad_maximum_fusion.3
  341.3 1.1 pad_maximum_fusion
  342.4 2.0 maximum_bitcast_fusion
  (84 shorter events, 2.3 us)
Async XLA Ops:
  0.6 21.6 %collective-permute-start = (bf16[1024,384]{1,0:T(8,128)(2,1)}, bf16[1024,384]{1,0:T(8,128)(2,1)S(1)}, u32[]{:S(2)}, u32[]{:S(2)}) collective-permute-start(bf16[1024,384]{1,0:T(8,128)(2,1)} %own.1), channel_id=1, source_target_pairs={{0,1},{1,0},{2,3},{3,2},{4,5},{5,4},{6,7},{7,6},{8,9},{9,8},{10,11... | collective-permute-start | bytes 2359304 | tf_op jit(solution)/shard_map/ppermute | solution.py:574
  3.7 71.2 %collective-permute-start.3 = (bf16[1024,384]{1,0:T(8,128)(2,1)}, bf16[1024,384]{1,0:T(8,128)(2,1)S(1)}, u32[]{:S(2)}, u32[]{:S(2)}) collective-permute-start(bf16[1024,384]{1,0:T(8,128)(2,1)} %co.1), channel_id=1, source_target_pairs={{0,1},{1,0},{2,3},{3,2},{4,5},{5,4},{6,7},{7,6},{8,9},{9,8},{10,11... | collective-permute-start | bytes 2359304 | tf_op jit(solution)/shard_map/ppermute | solution.py:574
  22.3 0.9 copy-start.26
  30.0 16.1 %copy-start.9 = (bf16[384,768]{1,0:T(8,128)(2,1)S(1)}, bf16[384,768]{1,0:T(8,128)(2,1)}, u32[]{:S(2)}) copy-start(bf16[384,768]{1,0:T(8,128)(2,1)} %pwo.3) | copy-start | bytes 1769476
  30.0 16.2 %copy-start.20 = (bf16[768]{0:T(1024)(128)(2,1)S(1)}, bf16[768]{0:T(1024)(128)(2,1)}, u32[]{:S(2)}) copy-start(bf16[768]{0:T(1024)(128)(2,1)} %param.20) | copy-start | bytes 4612
  30.0 16.8 %copy-start.21 = (bf16[768]{0:T(1024)(128)(2,1)S(1)}, bf16[768]{0:T(1024)(128)(2,1)}, u32[]{:S(2)}) copy-start(bf16[768]{0:T(1024)(128)(2,1)} %param.27) | copy-start | bytes 4612
  30.1 17.3 %copy-start.22 = (bf16[768]{0:T(1024)(128)(2,1)S(1)}, bf16[768]{0:T(1024)(128)(2,1)}, u32[]{:S(2)}) copy-start(bf16[768]{0:T(1024)(128)(2,1)} %param.28) | copy-start | bytes 4612
  30.1 17.9 %copy-start.15 = (bf16[1536]{0:T(1024)(128)(2,1)S(1)}, bf16[1536]{0:T(1024)(128)(2,1)}, u32[]{:S(2)}) copy-start(bf16[1536]{0:T(1024)(128)(2,1)} %param.22) | copy-start | bytes 9220
  30.1 18.5 %copy-start.23 = (bf16[768]{0:T(1024)(128)(2,1)S(1)}, bf16[768]{0:T(1024)(128)(2,1)}, u32[]{:S(2)}) copy-start(bf16[768]{0:T(1024)(128)(2,1)} %param.24) | copy-start | bytes 4612
  44.1 30.7 %collective-permute-start.1 = (bf16[1024,384]{1,0:T(8,128)(2,1)}, bf16[1024,384]{1,0:T(8,128)(2,1)S(1)}, u32[]{:S(2)}, u32[]{:S(2)}) collective-permute-start(bf16[1024,384]{1,0:T(8,128)(2,1)} %get-tuple-element.57.mo.o), channel_id=1, source_target_pairs={{0,1},{1,0},{2,3},{3,2},{4,5},{5,4},{6,7},{7,6},{8,9},{9,8},{10,11... | collective-permute-start | bytes 2359304 | tf_op jit(solution)/shard_map/ppermute | solution.py:574
  46.2 28.7 %collective-permute-start.2 = (bf16[384,768]{1,0:T(8,128)(2,1)S(1)}, bf16[384,768]{1,0:T(8,128)(2,1)S(1)}, u32[]{:S(2)}, u32[]{:S(2)}) collective-permute-start(bf16[384,768]{1,0:T(8,128)(2,1)S(1)} %copy-done.9), channel_id=1, source_target_pairs={{0,1},{1,0},{2,3},{3,2},{4,5},{5,4},{6,7},{7,6},{8,9},{9,8},{10,11... | collective-permute-start | bytes 1769480 | tf_op jit(solution)/shard_map/ppermute | solution.py:574
  74.8 0.9 copy-start.27
  74.8 1.1 copy-start.24
  74.8 1.3 copy-start.25
  98.7 20.7 %collective-permute-start.4 = (bf16[1024,384]{1,0:T(8,128)(2,1)}, bf16[1024,384]{1,0:T(8,128)(2,1)S(1)}, u32[]{:S(2)}, u32[]{:S(2)}) collective-permute-start(bf16[1024,384]{1,0:T(8,128)(2,1)} %get-tuple-element.59), channel_id=1, source_target_pairs={{0,1},{1,0},{2,3},{3,2},{4,5},{5,4},{6,7},{7,6},{8,9},{9,8},{10,11... | collective-permute-start | bytes 2359304 | tf_op jit(solution)/shard_map/ppermute | solution.py:574
  100.3 49.3 %collective-permute-start.5 = (bf16[1024,768]{1,0:T(8,128)(2,1)}, bf16[1024,768]{1,0:T(8,128)(2,1)S(1)}, u32[]{:S(2)}, u32[]{:S(2)}) collective-permute-start(bf16[1024,768]{1,0:T(8,128)(2,1)} %get-tuple-element.61.go), channel_id=1, source_target_pairs={{0,1},{1,0},{2,3},{3,2},{4,5},{5,4},{6,7},{7,6},{8,9},{9,8},{10,11... | collective-permute-start | bytes 4718600 | tf_op jit(solution)/shard_map/ppermute | solution.py:574
  100.7 6.6 %copy-start.17 = (f32[1,768]{1,0:T(1,128)S(1)}, f32[1,768]{1,0:T(1,128)}, u32[]{:S(2)}) copy-start(f32[1,768]{1,0:T(1,128)} %get-tuple-element.83) | copy-start | bytes 9220
  100.8 6.7 %copy-start.14 = (f32[1,1536]{1,0:T(1,128)S(1)}, f32[1,1536]{1,0:T(1,128)}, u32[]{:S(2)}) copy-start(f32[1,1536]{1,0:T(1,128)} %get-tuple-element.84) | copy-start | bytes 18436
  100.8 6.7 %copy-start.28 = (bf16[1024,1536]{1,0:T(8,128)(2,1)S(1)}, bf16[1024,1536]{1,0:T(8,128)(2,1)}, u32[]{:S(2)}) copy-start(bf16[1024,1536]{1,0:T(8,128)(2,1)} %get-tuple-element.75) | copy-start | bytes 9437188
  100.8 6.7 %copy-start.30 = (bf16[1024,768]{1,0:T(8,128)(2,1)S(1)}, bf16[1024,768]{1,0:T(8,128)(2,1)}, u32[]{:S(2)}) copy-start(bf16[1024,768]{1,0:T(8,128)(2,1)} %get-tuple-element.74) | copy-start | bytes 4718596
  107.5 11.9 %copy-start.4 = (f32[1024,384]{1,0:T(8,128)S(1)}, f32[1024,384]{1,0:T(8,128)}, u32[]{:S(2)}) copy-start(f32[1024,384]{1,0:T(8,128)} %get-tuple-element.58) | copy-start | bytes 4718596
  149.6 1.1 copy-start.2
  180.6 9.7 %copy-start.6 = (bf16[1024,384]{1,0:T(8,128)(2,1)S(1)}, bf16[1024,384]{1,0:T(8,128)(2,1)}, u32[]{:S(2)}) copy-start(bf16[1024,384]{1,0:T(8,128)(2,1)} %get-tuple-element.65.dq) | copy-start | bytes 2359300
  180.6 9.7 %copy-start.31 = (bf16[1024,768]{1,0:T(8,128)(2,1)S(1)}, bf16[1024,768]{1,0:T(8,128)(2,1)}, u32[]{:S(2)}) copy-start(bf16[1024,768]{1,0:T(8,128)(2,1)} %get-tuple-element.76) | copy-start | bytes 4718596
  188.2 17.1 %collective-permute-start.6 = (bf16[1024,384]{1,0:T(8,128)(2,1)}, bf16[1024,384]{1,0:T(8,128)(2,1)S(1)}, u32[]{:S(2)}, u32[]{:S(2)}) collective-permute-start(bf16[1024,384]{1,0:T(8,128)(2,1)} %get-tuple-element.69), channel_id=1, source_target_pairs={{0,1},{1,0},{2,3},{3,2},{4,5},{5,4},{6,7},{7,6},{8,9},{9,8},{10,11... | collective-permute-start | bytes 2359304 | tf_op jit(solution)/shard_map/ppermute | solution.py:574
  189.4 16.0 %collective-permute-start.7 = (f32[8,1024]{1,0:T(8,128)}, f32[8,1024]{1,0:T(8,128)S(1)}, u32[]{:S(2)}, u32[]{:S(2)}) collective-permute-start(f32[8,1024]{1,0:T(8,128)} %get-tuple-element.70.st_own), channel_id=1, source_target_pairs={{0,1},{1,0},{2,3},{3,2},{4,5},{5,4},{6,7},{7,6},{8,9},{9,8},{10,11... | collective-permute-start | bytes 98312 | tf_op jit(solution)/shard_map/ppermute | solution.py:574
  190.3 1.9 copy-start.3
  190.3 1.9 copy-start.7
  193.0 1.3 copy-start.29
  194.3 1.8 copy-start.5
  196.2 1.9 copy-start.18
  196.2 1.9 copy-start.19
  205.3 0.6 copy-start.13
  205.3 0.9 copy-start.8
  206.2 7.8 %copy-start.16 = (f32[1,768]{1,0:T(1,128)S(1)}, f32[1,768]{1,0:T(1,128)}, u32[]{:S(2)}) copy-start(f32[1,768]{1,0:T(1,128)} %get-tuple-element.80) | copy-start | bytes 9220
  213.4 3.7 %collective-permute-start.8 = (f32[1536]{0:T(1024)S(1)}, f32[1536]{0:T(1024)S(1)}, u32[]{:S(2)}, u32[]{:S(2)}) collective-permute-start(f32[1536]{0:T(1024)S(1)} %pad_maximum_fusion.2), channel_id=1, source_target_pairs={{0,1},{1,0},{2,3},{3,2},{4,5},{5,4},{6,7},{7,6},{8,9},{9,8},{10,11... | collective-permute-start | bytes 18440 | tf_op jit(solution)/shard_map/ppermute | solution.py:574
  329.1 3.4 copy-start.12
  331.2 1.3 copy-start.11
  332.5 1.1 copy-start.10
  333.6 1.7 copy-start.1
  335.3 2.8 copy-start

commit v3 on v1

v3 whole, which is shorter than its diff:
```python
import functools

import jax
import jax.numpy as jnp
from jax import lax
from jax.experimental import pallas as pl
from jax.experimental.pallas import tpu as pltpu
from jax.sharding import PartitionSpec as P

EPS = 1e-05
HEAD = 64
F32, BF16 = jnp.float32, jnp.bfloat16
NT = (((1,), (1,)), ((), ()))
TN = (((0,), (0,)), ((), ()))
GELU_A, GELU_B = 0.7978845608028654, 0.044715
VMEM_LIMIT = 63 * 1024 * 1024


def dot(a, b):
    return jnp.dot(a, b, preferred_element_type=F32)


def dot_nt(a, b):
    return lax.dot_general(a, b, NT, preferred_element_type=F32)


def dot_tn(a, b):
    return lax.dot_general(a, b, TN, preferred_element_type=F32)


def params(**more):
    return pltpu.CompilerParams(vmem_limit_bytes=VMEM_LIMIT, **more)


def cost(flops, size, trans=0):
    return pl.CostEstimate(flops=int(flops), bytes_accessed=int(size), transcendentals=int(trans))


def lane_part(which, width):
    return pl.ds(pl.multiple_of(which * width, 128), width)


def norm_rows(x):
    mean = jnp.mean(x, axis=-1, keepdims=True)
    cen = x - mean
    var = jnp.mean(cen * cen, axis=-1, keepdims=True)
    r = lax.rsqrt(var + EPS)
    return cen * r, r


def rows_spec(rows, cols, base=0):
    return pl.BlockSpec((rows, cols), lambda i, *_: (i + base, 0))


def whole_spec(shape):
    zeros = (0,) * len(shape)
    return pl.BlockSpec(shape, lambda i, *_: zeros)


MESH = pl.DeviceIdType.MESH


def bit_of(index, bit):
    return (index // (1 << bit)) % 2


def flip(index, bit):
    return index + (1 - 2 * bit_of(index, bit)) * (1 << bit)


def greet(peers):
    barrier = pltpu.get_barrier_semaphore()
    for peer in peers:
        pl.semaphore_signal(barrier, inc=1, device_id=peer, device_id_type=MESH)
    pl.semaphore_wait(barrier, len(peers))


def remote(src, dst, sems, at, peer):
    return pltpu.make_async_remote_copy(
        src_ref=src, dst_ref=dst, send_sem=sems[0].at[at], recv_sem=sems[1].at[at],
        device_id=peer, device_id_type=MESH,
    )


def block_rows(start, size, unit=16):
    return pl.ds(start if isinstance(start, int) else pl.multiple_of(start, unit), size)


class Chain:
    def __init__(self, me, order, rows):
        self.me, self.steps, self.splits = me, [], []
        base, size, box = 0, rows, 0
        for bit in order:
            if size % 32 == 0:
                half = size // 2
                mine = bit_of(me, bit)
                keep, give = base + mine * half, base + (1 - mine) * half
                self.splits.append((bit, base, keep, half))
            else:
                half, keep, give = size, base, base
            self.steps.append((bit, keep, give, half, box))
            base, size, box = keep, half, box + half
        self.base, self.size, self.box_rows = base, size, box
        self.first = self.steps[0][1]

    def scatter(self, src, box, part, own, sems, at, cols):
        self.src, self.box, self.part, self.own = src, box, part, own
        self.sems, self.at, self.cols = sems, at, cols
        return self

    def _source(self, step):
        if step == 0:
            return self.src, 0
        return self.part, self.first

    def _scatter_copy(self, step):
        bit, _, give, half, box = self.steps[step]
        source, off = self._source(step)
        return remote(
            source.at[block_rows(give - off, half), self.cols],
            self.box.at[pl.ds(box, half), self.cols],
            self.sems, self.at + step, {"wide": flip(self.me, bit)},
        )

    def scatter_start(self, step):
        self._scatter_copy(step).start()

    def scatter_end(self, step):
        self._scatter_copy(step).wait()
        _, keep, _, half, box = self.steps[step]
        source, off = self._source(step)
        last = step == len(self.steps) - 1
        target, out = (self.own, keep) if last else (self.part, self.first)
        unit = next(u for u in (96, 64, 48, 32, 16) if half % u == 0)

        def add(i, carry):
            at = i * unit
            got = self.box[block_rows(box + at, unit), self.cols].astype(F32)
            mine = source[block_rows(keep - off + at, unit), self.cols].astype(F32)
            target[block_rows(keep - out + at, unit), self.cols] = (got + mine).astype(BF16)
            return carry

        lax.fori_loop(0, half // unit, add, 0)

    def gather(self, own, dst, sems, at, cols):
        self.own, self.dst, self.gsems, self.gat, self.gcols = own, dst, sems, at, cols
        return self

    def gather_open(self):
        self.dst[block_rows(self.base, self.size), self.gcols] = self.own[:, self.gcols]

    def gather_copy_open(self, sem, at):
        region = self.dst.at[block_rows(self.base, self.size), self.gcols]
        return pltpu.make_async_copy(self.own.at[:, self.gcols], region, sem.at[at])

    def _gather_copy(self, step):
        bit, _, keep, half = self.splits[len(self.splits) - 1 - step]
        region = self.dst.at[block_rows(keep, half), self.gcols]
        return remote(region, region, self.gsems, self.gat + step, {"wide": flip(self.me, bit)})

    def gather_start(self, step):
        if step < len(self.splits):
            self._gather_copy(step).start()

    def gather_end(self, step):
        if step < len(self.splits):
            self._gather_copy(step).wait()


def bits(wide):
    return wide.bit_length() - 1


def order_of(wide, kind):
    steps = list(range(bits(wide)))
    return steps if kind == 0 else [0] + steps[2:] + steps[1:2]


def thirds(cols):
    w = cols // 3
    return [(0, pl.ds(0, w)), (0, pl.ds(w, w)), (1, pl.ds(2 * w, w))]


def wide_peers(me, wide):
    return [{"wide": flip(me, b)} for b in range(bits(wide))]


def vmem():
    return pl.BlockSpec(memory_space=pltpu.VMEM)


def anywhere():
    return pl.BlockSpec(memory_space=pl.ANY)


def sems(*counts):
    return [pltpu.SemaphoreType.DMA((c,)) for c in counts]


def qkv_body(own_hbm, own, w, bias, gain, shift, xf, low, q, k, v, got, send_sem, recv_sem):
    n = lax.axis_index("narrow")
    i = pl.program_id(0)
    rows, cw = own.shape
    peer = {"narrow": 1 - n}

    def copy(at):
        block = block_rows(at * rows, rows)
        return remote(own_hbm.at[block], got.at[block], (send_sem, recv_sem), at, peer)

    @pl.when(i == 0)
    def _():
        greet([peer])
        for at in range(got.shape[0] // rows):
            copy(at).start()

    xf[:, lane_part(n, cw)] = own[...]
    copy(i).wait()
    xf[:, lane_part(1 - n, cw)] = got[block_rows(i * rows, rows), :]
    xhat, _ = norm_rows(xf[...].astype(F32))
    y = (xhat * gain[...] + shift[...]).astype(BF16)
    low[...] = y
    q[...] = (dot(y, w[0]) + bias[0:1, :]).astype(BF16) * jnp.asarray(HEAD**-0.5, BF16)
    k[...] = dot(y, w[1]).astype(BF16)
    v[...] = (dot(y, w[2]) + bias[1:2, :]).astype(BF16)


def qkv_call(own, w, bias, gain, shift, block=256):
    rows, cw = own.shape
    d, lw = w.shape[1], w.shape[2]
    sd = jax.ShapeDtypeStruct
    return pl.pallas_call(
        qkv_body,
        out_shape=(sd((rows, d), BF16), sd((rows, d), BF16)) + (sd((rows, lw), BF16),) * 3,
        grid_spec=pltpu.PrefetchScalarGridSpec(
            num_scalar_prefetch=0,
            grid=(rows // block,),
            in_specs=[anywhere(), rows_spec(block, cw)] + [whole_spec(a.shape) for a in (w, bias, gain, shift)],
            out_specs=[rows_spec(block, d)] * 2 + [rows_spec(block, lw)] * 3,
            scratch_shapes=[pltpu.VMEM((rows, cw), BF16)] + sems(rows // block, rows // block),
        ),
        compiler_params=params(collective_id=1, has_side_effects=True),
        cost_estimate=cost(2 * rows * d * 3 * lw, 2 * (rows * d * 5 + w.size)),
        name="norm_qkv",
    )(own, own, w, bias, gain, shift)


def three(x):
    hi = x.astype(BF16).astype(F32)
    mid = (x - hi).astype(BF16).astype(F32)
    return hi, mid, x - hi - mid


def lanes_of(par):
    lane = lax.broadcasted_iota(jnp.int32, (1, 2 * HEAD), 1)
    mine = (lane // HEAD) == par
    return lane, mine, (1 - par) * HEAD


def place(lane, mine, at, base, terms):
    out = jnp.where(mine, base, 0.0)
    for i, term in enumerate(terms):
        out = jnp.where(lane == at + i, term, out)
    return out


def fwd_body(
    len_ref, q, k, v, pw, o, qa_out, o_got, pw_got, ka, va, send_sem, recv_sem, *, bq
):
    head = pl.program_id(0)
    par, pair = head % 2, head // 2
    lane, mine, at = lanes_of(par)
    n, me = lax.axis_index("narrow"), lax.axis_index("wide")
    peer, core = {"narrow": 1 - n}, {"wide": flip(me, 0)}
    pairs = pl.num_programs(0) // 2
    both = (send_sem, recv_sem)
    cols = lane_part(pair, 2 * HEAD)
    part = block_rows((me % 2) * (pw.shape[0] // 2), pw.shape[0] // 2)
    npairs = o.shape[1] // (2 * HEAD)
    weights = remote(pw.at[part], pw_got.at[part], both, npairs, peer)
    shared = remote(pw_got.at[part], pw_got.at[part], both, npairs + 1, core)

    @pl.when(head == 0)
    def _():
        greet([peer, core])
        weights.start()

    keys = k.shape[0]
    kpos = lax.broadcasted_iota(jnp.int32, (keys, 1), 0)
    kbias = jnp.where(kpos < len_ref[0], 0.0, -1e30)
    ka[...] = place(lane, mine, at, k[...].astype(F32), [kbias]).astype(BF16)
    va[...] = place(lane, mine, at, v[...].astype(F32), [1.0]).astype(BF16)
    tri = lax.broadcasted_iota(jnp.int32, (bq, bq), 1) <= lax.broadcasted_iota(jnp.int32, (bq, bq), 0)
    for i in range(q.shape[0] // bq):
        nk = (i + 1) * bq
        rows = pl.ds(i * bq, bq)
        qf = q[rows, :].astype(F32)
        qa = place(lane, mine, at, qf, [1.0])
        s = dot_nt(qa.astype(BF16), ka[0:nk, :])
        edge = jnp.where(tri, s[:, nk - bq :], -1e30)
        m = jnp.max(edge, axis=1, keepdims=True)
        if nk > bq:
            m = jnp.maximum(m, jnp.max(s[:, : nk - bq], axis=1, keepdims=True))
        pv = dot(jnp.exp(edge - m).astype(BF16), va[nk - bq : nk, :])
        if nk > bq:
            pv += dot(jnp.exp(s[:, : nk - bq] - m).astype(BF16), va[0 : nk - bq, :])
        total = jnp.sum(jnp.where(lane == at, pv, 0.0), axis=1, keepdims=True)
        out = (pv / total).astype(BF16).astype(F32)
        old = o[rows, cols].astype(F32)
        o[rows, cols] = jnp.where(mine, out, jnp.where(par == 0, 0.0, old)).astype(BF16)
        lse = m + jnp.log(total)
        qa_out[0, rows, :] = place(lane, mine, at, qf, [1.0, *three(lse)]).astype(BF16)

    def mixed(j):
        c = pl.ds(j * 2 * HEAD, 2 * HEAD)
        return remote(o.at[:, c], o_got.at[:, c], both, j, peer)

    for j in range(npairs):

        @pl.when(head == 2 * j + 1)
        def _():
            mixed(j).start()

    @pl.when(head == 3)
    def _():
        weights.wait()
        shared.start()

    @pl.when(head == 2 * npairs - 1)
    def _():
        shared.wait()
        for j in range(npairs):
            mixed(j).wait()


def attend_forward(length, q, k, v, pw, bq=256):
    rows, width = q.shape
    heads, pair = width // HEAD, 2 * HEAD
    half = lambda h, *_: (0, h // 2)
    sd = jax.ShapeDtypeStruct
    work = 2 * heads * rows * rows * HEAD
    return pl.pallas_call(
        functools.partial(fwd_body, bq=bq),
        out_shape=(
            sd((rows, width), BF16), sd((heads, rows, pair), BF16), sd((rows, width), BF16), sd(pw.shape, BF16),
        ),
        grid_spec=pltpu.PrefetchScalarGridSpec(
            num_scalar_prefetch=1,
            grid=(heads,),
            in_specs=[pl.BlockSpec((rows, pair), half)] * 3 + [anywhere()],
            out_specs=[vmem(), pl.BlockSpec((1, rows, pair), lambda h, *_: (h, 0, 0)), anywhere(), anywhere()],
            scratch_shapes=[pltpu.VMEM((rows, pair), BF16)] * 2 + sems(heads // 2 + 2, heads // 2 + 2),
        ),
        compiler_params=params(collective_id=2, has_side_effects=True),
        cost_estimate=cost(4 * work, 2 * rows * width * 6, work // 256),
        name="attend_fwd",
    )(length, q, k, v, pw)


def mlp_body(
    len_ref, xf, mo, mr, pwo, pwr, pb, gain, shift, ub, db, up_hbm, down_hbm, cot,
    lo, lo_send, gmix, gm, gup, down_own, gp_own, gp_other, sum_ub, sum_db, sum_g, sum_s, sum_pb,
    up, down, cot_got, cf, mid, second, active, slope, gh, gs_send, gs_got, gs_own, gdown, box, part,
    glow, gmix_send, load_sem, nsend, nrecv, wsend, wrecv,
    *, wide,
):
    n, me = lax.axis_index("narrow"), lax.axis_index("wide")
    peer = {"narrow": 1 - n}
    rows, cw = cot.shape
    d, f = up.shape
    half, block = rows // 2, min(256, rows // 2)
    each = half // block
    mine, other = lane_part(n, cw), lane_part(1 - n, cw)
    narrow, across = (nsend, nrecv), (wsend, wrecv)
    loads = [
        pltpu.make_async_copy(up_hbm, up, load_sem.at[0]),
        pltpu.make_async_copy(down_hbm, down, load_sem.at[1]),
    ]
    for load in loads:
        load.start()
    greet([peer] + wide_peers(me, wide))

    def cot_copy(side, j):
        r = block_rows(side * half + j * block, block)
        return (cot.at[r], cot_got.at[r])

    for a, side in enumerate((n, 1 - n)):
        for j in range(each):
            src, dst = cot_copy(side, j)
            remote(src, dst, narrow, a * each + j, peer).start()

    def forward(i, carry):
        r = block_rows(i * block, block)
        m = xf[r, :].astype(F32) + (dot(mo[r, :], pwo[...]) + dot(mr[r, :], pwr[...])) + pb[...]
        mid[r, :] = m
        xhat, _ = norm_rows(m)
        sec = (xhat * gain[...] + shift[...]).astype(BF16)
        second[r, :] = sec
        hid = dot(sec, up[...]) + ub[...]
        sq = hid * hid
        t = jnp.tanh(GELU_A * (hid + GELU_B * (sq * hid)))
        hf = 0.5 * (1.0 + t)
        act = (hid * hf).astype(BF16)
        active[r, :] = act
        slope[r, :] = hf + (0.5 * hid) * (1.0 - t * t) * (GELU_A + (3.0 * GELU_A * GELU_B) * sq)
        lo[r, :] = mid[r, mine] + dot(act, down[:, mine]) + db[:, mine]
        lo_send[r, :] = dot(act, down[:, other]).astype(BF16)
        return carry

    for load in loads:
        load.wait()
    lax.fori_loop(0, rows // block, forward, 0)

    def backward(side, j, a):
        src, dst = cot_copy(side, j)
        remote(src, dst, narrow, a * each + j, peer).wait()
        at = side * half + j * block
        r = block_rows(at, block)
        pos = at + lax.broadcasted_iota(jnp.int32, (block, 1), 0)
        live = (pos < len_ref[0]).astype(F32)
        cf[r, mine] = (cot[r, :].astype(F32) * live).astype(BF16)
        cf[r, other] = (cot_got[r, :].astype(F32) * live).astype(BF16)
        ghid = (dot_nt(cf[r, :], down[...]) * slope[r, :]).astype(BF16)
        gh[r, :] = ghid
        return dot_nt(ghid, up[...]), ghid

    def gs_copy(j):
        r = pl.ds(j * block, block)
        return remote(gs_send.at[r], gs_got.at[r], narrow, 2 * each + j, peer)

    sum_ub[...] = jnp.zeros_like(sum_ub)

    def for_peer(j, carry):
        g, ghid = backward(1 - n, j, 0)
        r = block_rows(j * block, block)
        gs_send[r, :] = g.astype(BF16)
        remote(gs_send.at[r], gs_got.at[r], narrow, 2 * each + j, peer).start()
        sum_ub[...] += jnp.sum(ghid.astype(F32), axis=0, keepdims=True)
        return carry

    def for_own(j, carry):
        g, ghid = backward(n, j, 1)
        gs_own[block_rows(j * block, block), :] = g
        sum_ub[...] += jnp.sum(ghid.astype(F32), axis=0, keepdims=True)
        return carry

    lax.fori_loop(0, each, for_peer, 0)
    lax.fori_loop(0, each, for_own, 0)

    chains = []
    for a, (kind, cols) in enumerate(thirds(d)):
        chain = Chain(me, order_of(wide, kind), f)
        chains.append(chain.scatter(gdown, box, part, down_own, across, a * bits(wide), cols))

    def weight_down(i, carry):
        c = block_rows(i * 256, 256, 256)
        gdown[c, :] = dot_tn(active[:, c], cf[...]).astype(BF16)
        return carry

    def weight_up(i, carry):
        c = block_rows(i * 256, 256, 256)
        gup[c, :] = dot_tn(second[:, c], gh[...]).astype(BF16)
        return carry

    lax.fori_loop(0, f // 256, weight_down, 0)
    for chain in chains:
        chain.scatter_start(0)
    lax.fori_loop(0, d // 256, weight_up, 0)

    def advance(step):
        for chain in chains:
            chain.scatter_end(step)
            if step + 1 < bits(wide):
                chain.scatter_start(step + 1)

    advance(0)
    for j in range(each):
        gs_copy(j).wait()
    for ref in (sum_g, sum_s, sum_pb, sum_db):
        ref[...] = jnp.zeros_like(ref)

    def gmix_copy(j):
        r = block_rows(n * half + j * block, block)
        return remote(gmix_send.at[block_rows(j * block, block)], gmix.at[r], narrow, 3 * each + j, peer)

    def back_norm(j, carry):
        r, rh = block_rows(n * half + j * block, block), block_rows(j * block, block)
        g = gs_own[rh, :] + gs_got[rh, :].astype(F32)
        xhat, scale = norm_rows(mid[r, :])
        gg = g * gain[...]
        m1 = jnp.mean(gg, axis=-1, keepdims=True)
        m2 = jnp.mean(gg * xhat, axis=-1, keepdims=True)
        c = cf[r, :].astype(F32)
        grad = c + scale * (gg - m1 - xhat * m2)
        gm[rh, :] = grad
        gl = grad.astype(BF16)
        glow[rh, :] = gl
        gmix_send[rh, :] = dot_nt(gl, pwr[...]).astype(BF16)
        gmix_copy(j).start()
        gmix[r, :] = dot_nt(gl, pwo[...]).astype(BF16)
        sum_g[...] += jnp.sum(g * xhat, axis=0, keepdims=True)
        sum_s[...] += jnp.sum(g, axis=0, keepdims=True)
        sum_pb[...] += jnp.sum(grad, axis=0, keepdims=True)
        sum_db[...] += jnp.sum(c, axis=0, keepdims=True)
        return carry

    lax.fori_loop(0, each, back_norm, 0)
    for step in range(1, bits(wide)):
        advance(step)
        if step == 1:
            own_rows = block_rows(n * half, half)
            lw = mo.shape[1]
            for src, dst in ((mo, gp_own), (mr, gp_other)):
                total = dot_tn(src[own_rows, :], glow[...]).astype(BF16)
                dst[0:lw, :] = total[:, :cw]
                dst[lw : 2 * lw, :] = total[:, cw:]

    def received(j):
        r = block_rows((1 - n) * half + j * block, block)
        return remote(gmix_send.at[block_rows(j * block, block)], gmix.at[r], narrow, 3 * each + j, peer)

    for j in range(each):
        gmix_copy(j).wait()


def mlp_call(length, xf, mo, mr, pwo, pwr, pb, gain, shift, up, ub, down, db, cot, wide):
    rows, d = xf.shape
    f, lw, cw = up.shape[1], mo.shape[1], cot.shape[1]
    half = rows // 2
    chain = Chain(0, order_of(wide, 0), f)
    sd, vm = jax.ShapeDtypeStruct, pltpu.VMEM
    each = half // min(256, half)
    return pl.pallas_call(
        functools.partial(mlp_body, wide=wide),
        out_shape=(
            sd((rows, cw), F32), sd((rows, cw), BF16), sd((rows, lw), BF16), sd((half, d), F32),
            sd((d, f), BF16), sd((chain.size, d), BF16), sd((2 * lw, cw), BF16), sd((2 * lw, cw), BF16),
            sd((1, f), F32), sd((1, d), F32), sd((1, d), F32), sd((1, d), F32), sd((1, d), F32),
        ),
        in_specs=[pl.BlockSpec(memory_space=pltpu.SMEM)] + [vmem()] * 10 + [anywhere(), anywhere(), vmem()],
        out_specs=(vmem(),) * 13,
        scratch_shapes=[
            vm((d, f), BF16), vm((f, d), BF16), vm((rows, cw), BF16), vm((rows, d), BF16), vm((rows, d), F32),
            vm((rows, d), BF16), vm((rows, f), BF16), vm((rows, f), F32), vm((rows, f), BF16),
            vm((half, d), BF16), vm((half, d), BF16), vm((half, d), F32), vm((f, d), BF16),
            vm((chain.box_rows, d), BF16), vm((f // 2, d), BF16), vm((half, d), BF16), vm((half, lw), BF16),
        ]
        + sems(2, 4 * each, 4 * each, 3 * bits(wide), 3 * bits(wide)),
        compiler_params=params(collective_id=3, has_side_effects=True),
        cost_estimate=cost(2 * rows * d * (d + 6 * f), 2 * (rows * d * 8 + 2 * d * f), rows * f),
        name="mlp",
    )(length, xf, mo, mr, pwo, pwr, pb, gain, shift, ub, db, up, down, cot)


def bwd_body(
    len_ref, qa, k, v, do, o, lo_send, gup, down_own, gp_own, gp_other,
    dq, dk, dv, lo_got, gdown, up_own, gp_sum,
    ka, va, dk_acc, dv_acc, up_box, up_part, own_box, own_part, other_box, other_part,
    own_shard, other_shard, peer_shard, open_sem, nsend, nrecv, wsend, wrecv, *, bq, wide,
):
    head = pl.program_id(0)
    heads = 2 * (lo_got.shape[1] // (2 * HEAD))
    n, me = lax.axis_index("narrow"), lax.axis_index("wide")
    peer = {"narrow": 1 - n}
    narrow, across = (nsend, nrecv), (wsend, wrecv)
    steps = bits(wide)
    scatters, gathers = [], []
    for a, (kind, cols) in enumerate(thirds(gup.shape[1])):
        chain = Chain(me, order_of(wide, kind), gup.shape[0])
        scatters.append(chain.scatter(gup, up_box, up_part, up_own, across, a * steps, cols))
    cw = gp_own.shape[1]
    for a, (src, box, part, own) in enumerate(
        ((gp_own, own_box, own_part, own_shard), (gp_other, other_box, other_part, other_shard))
    ):
        chain = Chain(me, order_of(wide, 0), gp_own.shape[0])
        scatters.append(chain.scatter(src, box, part, own, across, (3 + a) * steps, pl.ds(0, cw)))
    for a, (kind, cols) in enumerate(thirds(gdown.shape[1])):
        chain = Chain(me, order_of(wide, kind), gdown.shape[0])
        gathers.append(chain.gather(down_own, gdown, across, (5 + a) * steps, cols))
    layer = remote(lo_send, lo_got, narrow, 0, peer)
    shard = remote(other_shard, peer_shard, narrow, 1, peer)

    @pl.when(head == 0)
    def _():
        greet([peer] + wide_peers(me, wide))
        layer.start()
        for chain in scatters:
            chain.scatter_start(0)
        opens = [chain.gather_copy_open(open_sem, a) for a, chain in enumerate(gathers)]
        for opened in opens:
            opened.start()
        for opened, chain in zip(opens, gathers):
            opened.wait()
            chain.gather_start(0)

    par = head % 2
    lane, mine, at = lanes_of(par)
    keys = k.shape[0]
    kpos = lax.broadcasted_iota(jnp.int32, (keys, 1), 0)
    kbias = jnp.where(kpos < len_ref[0], 0.0, -1e30)
    ka[...] = place(lane, mine, at, k[...].astype(F32), [kbias, -1.0, -1.0, -1.0]).astype(BF16)
    va[...] = place(lane, mine, at, v[...].astype(F32), [-1.0, -1.0, -1.0]).astype(BF16)
    dk_acc[...] = jnp.zeros_like(dk_acc)
    dv_acc[...] = jnp.zeros_like(dv_acc)
    tri = lax.broadcasted_iota(jnp.int32, (bq, bq), 0) <= lax.broadcasted_iota(jnp.int32, (bq, bq), 1)

    def put(ref, rows, new):
        old = ref[rows, :].astype(F32)
        ref[rows, :] = jnp.where(mine, new, jnp.where(par == 0, 0.0, old)).astype(BF16)

    for i in range(qa.shape[1] // bq):
        rows = pl.ds(i * bq, bq)
        qb = qa[0, rows, :]
        df = do[rows, :].astype(F32)
        delta = jnp.sum(jnp.where(mine, df * o[rows, :].astype(F32), 0.0), axis=1, keepdims=True)
        db = place(lane, mine, at, df, three(delta)).astype(BF16)
        dqs = None
        for j in range(i + 1):
            cols = pl.ds(j * bq, bq)
            kb, vb = ka[cols, :], va[cols, :]
            s = dot_nt(kb, qb)
            if j == i:
                s = jnp.where(tri, s, -1e30)
            p = jnp.exp(s)
            ds = (p * dot_nt(vb, db)).astype(BF16)
            dv_acc[cols, :] += dot(p.astype(BF16), db)
            dk_acc[cols, :] += dot(ds, qb)
            part = dot_tn(ds, kb)
            dqs = part if dqs is None else dqs + part
        put(dq, rows, dqs * HEAD**-0.5)
    put(dk, pl.ds(0, keys), dk_acc[...])
    put(dv, pl.ds(0, keys), dv_acc[...])

    def advance(step):
        for chain in scatters:
            chain.scatter_end(step)
            if step + 1 < steps:
                chain.scatter_start(step + 1)
        for chain in gathers:
            chain.gather_end(step)
            chain.gather_start(step + 1)
        if step == steps - 1:
            shard.start()

    for step in range(steps):

        @pl.when(head == min(heads - 1, (step * heads) // steps + (1 if step else 0)))
        def _():
            advance(step)

    @pl.when(head == heads - 1)
    def _():
        shard.wait()
        gp_sum[...] = (own_shard[...].astype(F32) + peer_shard[...].astype(F32)).astype(BF16)
        layer.wait()


def attend_backward(length, qa, k, v, do, o, lo_send, gup, down_own, gp_own, gp_other, wide, bq=256):
    rows, width = k.shape
    heads, pair = width // HEAD, 2 * HEAD
    half = lambda h, *_: (0, h // 2)
    sd, vm = jax.ShapeDtypeStruct, pltpu.VMEM
    work = 2 * heads * rows * rows * HEAD
    d, f = gup.shape
    up_chain = Chain(0, order_of(wide, 0), d)
    gp_rows, cw = gp_own.shape
    gp_chain = Chain(0, order_of(wide, 0), gp_rows)
    pairs = [pl.BlockSpec((rows, pair), half)]
    steps = bits(wide)
    return pl.pallas_call(
        functools.partial(bwd_body, bq=bq, wide=wide),
        out_shape=(
            (sd((rows, width), BF16),) * 3
            + (sd(lo_send.shape, BF16), sd((f, d), BF16), sd((up_chain.size, f), BF16), sd((gp_chain.size, cw), BF16))
        ),
        grid_spec=pltpu.PrefetchScalarGridSpec(
            num_scalar_prefetch=1,
            grid=(heads,),
            in_specs=[pl.BlockSpec((1, rows, pair), lambda h, *_: (h, 0, 0))] + pairs * 4 + [vmem()] * 5,
            out_specs=pairs * 3 + [anywhere()] * 2 + [vmem()] * 2,
            scratch_shapes=[vm((rows, pair), BF16)] * 2 + [vm((rows, pair), F32)] * 2
            + [vm((up_chain.box_rows, f), BF16), vm((d // 2, f), BF16)]
            + [vm((gp_chain.box_rows, cw), BF16), vm((gp_rows // 2, cw), BF16)] * 2
            + [vm((gp_chain.size, cw), BF16)] * 3
            + sems(3, 2, 2, 8 * steps, 8 * steps),
        ),
        compiler_params=params(collective_id=4, has_side_effects=True),
        cost_estimate=cost(10 * work, 2 * rows * width * 9, work // 256),
        name="attend_bwd",
    )(length, qa, k, v, do, o, lo_send, gup, down_own, gp_own, gp_other)


def last_body(
    dq, dk, dv, low_hbm, w_hbm, xf_hbm, gm, gain, up_own, gp_sum, s_ub, s_db, s_g2, s_s2, s_pb,
    ig, gup, gp, gq, gk, gv, small,
    low, w, xf, gn_send, gn_got, gn_own, ig_own, ig_send, src, box, part, own, vec, vec_box,
    load_sem, nsend, nrecv, wsend, wrecv, *, wide,
):
    n, me = lax.axis_index("narrow"), lax.axis_index("wide")
    peer = {"narrow": 1 - n}
    narrow, across = (nsend, nrecv), (wsend, wrecv)
    steps = bits(wide)
    rows, lw = dq.shape
    d = gain.shape[1]
    cw = d // 2
    half, block = rows // 2, min(256, rows // 2)
    each = half // block
    loads = [
        pltpu.make_async_copy(a, b, load_sem.at[i])
        for i, (a, b) in enumerate(((low_hbm, low), (w_hbm, w), (xf_hbm, xf)))
    ]
    for load in loads:
        load.start()
    greet([peer] + wide_peers(me, wide))
    gathers = []
    for a, (kind, cols) in enumerate(thirds(gup.shape[1])):
        chain = Chain(me, order_of(wide, kind), gup.shape[0])
        gathers.append(chain.gather(up_own, gup, across, a * steps, cols))
    chain = Chain(me, order_of(wide, 0), gp.shape[0])
    gathers.append(chain.gather(gp_sum, gp, across, 3 * steps, pl.ds(0, cw)))
    for chain in gathers:
        chain.gather_open()
        chain.gather_start(0)

    grads, outs = (dq, dk, dv), (gq, gk, gv)
    scatters = []
    for c in range(3):
        chain = Chain(me, order_of(wide, 1 if c == 1 else 0), d)
        chain.scatter(src.at[c], box.at[c], part.at[c], own.at[c], across, (4 + c) * steps, pl.ds(0, lw))
        scatters.append(chain.gather(own.at[c], outs[c], across, (7 + c) * steps, pl.ds(0, lw)))

    def scatter_step(step):
        for chain in scatters:
            chain.scatter_end(step)
            if step + 1 < steps:
                chain.scatter_start(step + 1)
            else:
                chain.gather_open()
                chain.gather_start(0)

    def gather_step(chains, step):
        for chain in chains:
            chain.gather_end(step)
            chain.gather_start(step + 1)

    loads[0].wait()
    for c in range(3):
        src[c] = dot_tn(low[...], grads[c][...]).astype(BF16)
        scatters[c].scatter_start(0)
    gather_step(gathers, 0)
    loads[1].wait()

    def gn_part(at, cols):
        r = block_rows(at, block)
        total = dot_nt(dq[r, :], w[0, cols, :])
        total += dot_nt(dk[r, :], w[1, cols, :])
        return total + dot_nt(dv[r, :], w[2, cols, :])

    def gn_copy(j):
        r = pl.ds(j * block, block)
        return remote(gn_send.at[r], gn_got.at[r], narrow, j, peer)

    for j in range(each):
        at = (1 - n) * half + j * block
        for c in range(2):
            cols = slice(c * cw, (c + 1) * cw)
            gn_send[j * block : (j + 1) * block, cols] = gn_part(at, cols).astype(BF16)
        gn_copy(j).start()
    scatter_step(0)
    for j in range(each):
        at = n * half + j * block
        for c in range(2):
            cols = slice(c * cw, (c + 1) * cw)
            gn_own[j * block : (j + 1) * block, cols] = gn_part(at, cols)
    gather_step(gathers, 1)
    loads[2].wait()

    vec[...] = jnp.zeros_like(vec)

    def put(at, value):
        for i in range(value.shape[1] // 128):
            vec[at + i : at + i + 1, :] = value[:, i * 128 : (i + 1) * 128]

    dr, fr, lr = d // 128, s_ub.shape[1] // 128, lw // 128
    shared = -(-6 * dr // 8) * 8
    put(2 * dr, s_g2[...])
    put(3 * dr, s_s2[...])
    put(4 * dr, s_pb[...])
    put(5 * dr, s_db[...])
    put(shared, s_ub[...])
    put(shared + fr, jnp.sum(dq[...].astype(F32), axis=0, keepdims=True))
    put(shared + fr + lr, jnp.sum(dv[...].astype(F32), axis=0, keepdims=True))

    mine, other = lane_part(n, cw), lane_part(1 - n, cw)
    g1 = s1 = 0.0

    def ig_copy(j):
        r = block_rows(n * half + j * block, block)
        return remote(ig_send.at[pl.ds(j * block, block)], ig.at[r], narrow, each + j, peer)

    for j in range(each):
        gn_copy(j).wait()
        rh = pl.ds(j * block, block)
        r = block_rows(n * half + j * block, block)
        g = gn_own[rh, :] + gn_got[rh, :].astype(F32)
        xhat, scale = norm_rows(xf[r, :].astype(F32))
        gg = g * gain[...]
        m1 = jnp.mean(gg, axis=-1, keepdims=True)
        m2 = jnp.mean(gg * xhat, axis=-1, keepdims=True)
        ig_own[...] = gm[rh, :] + scale * (gg - m1 - xhat * m2)
        ig_send[rh, :] = ig_own[:, other].astype(BF16)
        ig_copy(j).start()
        ig[r, :] = ig_own[:, mine].astype(BF16)
        g1 += jnp.sum(g * xhat, axis=0, keepdims=True)
        s1 += jnp.sum(g, axis=0, keepdims=True)
    put(0, g1)
    put(dr, s1)

    def vec_copy(step):
        if step == 0:
            top = pl.ds(0, shared)
            return remote(vec.at[top], vec_box.at[0, top], narrow, 2 * each, peer)
        return remote(vec, vec_box.at[step], across, 10 * steps + step - 1, {"wide": flip(me, step - 1)})

    def vec_end(step):
        vec_copy(step).wait()
        if step == 0:
            vec[0:shared, :] += vec_box[0, 0:shared, :]
        else:
            vec[...] += vec_box[step]
        if step < steps:
            vec_copy(step + 1).start()

    vec_copy(0).start()
    for step in range(1, steps):
        scatter_step(step)
        vec_end(step - 1)
    for step in range(2, steps):
        gather_step(gathers, step)
    vec_end(steps - 1)
    for step in range(steps):
        gather_step(scatters, step)
    vec_end(steps)
    small[...] = vec[...]
    for j in range(each):
        ig_copy(j).wait()


def last_call(dq, dk, dv, low, w, xf, gm, gain, up_own, gp_sum, s_ub, s_db, s_g2, s_s2, s_pb, wide):
    rows, lw = dq.shape
    d, f = xf.shape[1], s_ub.shape[1]
    cw, half = d // 2, rows // 2
    block = min(256, half)
    each, steps = half // block, bits(wide)
    sd, vm = jax.ShapeDtypeStruct, pltpu.VMEM
    chain = Chain(0, order_of(wide, 0), d)
    vec_rows = -(-6 * d // 1024) * 8 + -(-(f + 2 * lw) // 1024) * 8
    return pl.pallas_call(
        functools.partial(last_body, wide=wide),
        out_shape=(sd((rows, cw), BF16), sd((d, f), BF16), sd((2 * lw, cw), BF16))
        + (sd((d, lw), BF16),) * 3 + (sd((vec_rows, 128), F32),),
        in_specs=[vmem()] * 3 + [anywhere()] * 3 + [vmem()] * 9,
        out_specs=(vmem(),) * 7,
        scratch_shapes=[
            vm((rows, d), BF16), vm(w.shape, BF16), vm((rows, d), BF16), vm((half, d), BF16), vm((half, d), BF16),
            vm((half, d), F32), vm((block, d), F32), vm((half, cw), BF16), vm((3, d, lw), BF16),
            vm((3, chain.box_rows, lw), BF16), vm((3, d // 2, lw), BF16), vm((3, chain.size, lw), BF16),
            vm((vec_rows, 128), F32), vm((steps + 1, vec_rows, 128), F32),
        ]
        + sems(3, 2 * each + 1, 2 * each + 1, 11 * steps, 11 * steps),
        compiler_params=params(collective_id=5, has_side_effects=True),
        cost_estimate=cost(2 * rows * d * 6 * lw, 2 * rows * d * 8),
        name="last",
    )(dq, dk, dv, low, w, xf, gm, gain, up_own, gp_sum, s_ub, s_db, s_g2, s_s2, s_pb)


def on_device(
    tokens, lengths, qkv_weight, qv_bias, proj_weight, proj_bias, up_weight, up_bias,
    down_weight, down_bias, first_gain, first_shift, second_gain, second_shift, cotangent,
):
    cw = tokens.shape[1]
    d, ff, lw = 2 * cw, up_weight.shape[1], proj_weight.shape[0]
    wide = lax.axis_size("wide")
    row = lambda a: a.astype(F32).reshape(1, -1)
    w3 = jnp.transpose(qkv_weight, (1, 0, 2))
    gain1, shift1, gain2, shift2 = map(row, (first_gain, first_shift, second_gain, second_shift))

    xf, low, q, k, v = qkv_call(tokens, w3, qv_bias.astype(F32), gain1, shift1)
    mixed, qa, mixed_got, proj_got = attend_forward(lengths, q, k, v, proj_weight)
    lo, lo_send, gmix, gm, gup, down_own, gp_own, gp_other, s_ub, s_db, s_g2, s_s2, s_pb = mlp_call(
        lengths, xf, mixed, mixed_got, proj_weight, proj_got, row(proj_bias), gain2, shift2,
        up_weight, row(up_bias), down_weight, row(down_bias), cotangent, wide,
    )
    dq, dk, dv, lo_got, gdown, up_own, gp_sum = attend_backward(
        lengths, qa, k, v, gmix, mixed, lo_send, gup, down_own, gp_own, gp_other, wide
    )
    ig, gup, gp, gq, gk, gv, small = last_call(
        dq, dk, dv, low, w3, xf, gm, gain1, up_own, gp_sum, s_ub, s_db, s_g2, s_s2, s_pb, wide
    )
    layer_out = (lo + lo_got.astype(F32)).astype(BF16)
    factor = 1.0 / (lengths.shape[0] * wide)
    fin = lambda a: a.astype(F32) * factor
    s_qkv = jnp.stack([fin(a) for a in (gq, gk, gv)])
    s_proj = jnp.concatenate([fin(gp[:lw]), fin(gp[lw:])], axis=1)
    flat = (small * factor).reshape(-1)
    shared = -(-6 * d // 1024) * 1024
    g1, s1, g2, s2, pb, dbs = (flat[i * d : (i + 1) * d] for i in range(6))
    ubs = flat[shared : shared + ff]
    qvb = flat[shared + ff : shared + ff + 2 * lw].reshape(2, lw)
    return (
        layer_out, ig, jnp.transpose(s_qkv, (1, 0, 2)), qvb,
        s_proj, pb, fin(gup), ubs, fin(gdown), dbs, g1, s1, g2, s2,
    )


def solution(mesh):
    split = P("wide", "narrow")
    none3, cols, rows1 = P(None, None, "narrow"), P(None, "narrow"), P("narrow", None)
    return jax.shard_map(
        on_device,
        mesh=mesh,
        in_specs=(
            split, P("wide"), none3, cols, rows1, P(), cols, P("narrow"), rows1, P(), P(), P(), P(), P(), split,
        ),
        out_specs=(
            split, split, none3, cols, rows1, P(), cols, P("narrow"), rows1, P(), P(), P(), P(), P(),
        ),
        check_vma=False,
    )
```

time: 387 us -> 250 us (0.65)
  waiting for transfers between devices: 223 us -> 0 us
  Pallas kernels: 86.3 us -> 221 us
  matrix products: 15.6 us -> 0 us
  between operations: 14.9 us -> 1.4 us
  starting transfers between devices: 10 us -> 0 us
  other arithmetic: 21.1 us -> 14.5 us
    psum x1 -> x0, waiting for transfers between devices: 136 us -> none  [on_device(): lax.psum((grad_down.astype(BF16), grad_up.astype(BF16), proj_small, grad_...]
    pallas_call x6 -> x4, Pallas kernels: 79.5 us -> 197 us  [the longest x1 63.3 us: last_call(): pl.pallas_call(functools.partial(last_body, wide=wide), out_shape=(sd((ro...]
    ppermute x9 -> x0, waiting for transfers between devices: 86.9 us -> none  [on_device(): swap = lambda a: lax.ppermute(a, 'narrow', [(0, 1), (1, 0)])]
    pallas_call x1, Pallas kernels: 6.84 us -> 24.2 us  [qkv_call(): pl.pallas_call(qkv_body, out_shape=(sd((rows, d), BF16), sd((rows, d), BF...]
    dot_general x6 -> x0, matrix products: 15.6 us -> none  [dot_tn(): return lax.dot_general(a, b, TN, preferred_element_type=F32)]
    ppermute x9 -> x0, starting transfers between devices: 10 us -> none  [on_device(): swap = lambda a: lax.ppermute(a, 'narrow', [(0, 1), (1, 0)])]
    unnamed x63 -> x13, local copies, waits for them, and re-layouts: 7.74 us -> 2.22 us
    mul x4 -> x3, other arithmetic: 10 us -> 5.4 us  [on_device(): fin = lambda a: a.astype(F32) * factor]
  transfers between devices with their start and end apart: 10 -> 0, of which waited for: 7 -> 0; matrix products, arithmetic and copies ran while one was open for 6% -> 0% of each run, Pallas kernels for 5% -> 0%
where the time goes in v3:
time: 250 us
  Pallas kernels  221 us (88%)
  other arithmetic  14.5 us (6%)
  local copies, waits for them, and re-layouts  12.9 us (5%)
    pallas_call x1, Pallas kernels, last_call(): pl.pallas_call(functools.partial(last_body, wide=wide), out_shape=(sd((ro...  63.3 us
    pallas_call x1, Pallas kernels, mlp_call(): pl.pallas_call(functools.partial(mlp_body, wide=wide), out_shape=(sd((row...  56.6 us
    pallas_call x1, Pallas kernels, attend_backward(): pl.pallas_call(functools.partial(bwd_body, bq=bq, wide=wide), out_shape=(...  47.9 us
    pallas_call x1, Pallas kernels, attend_forward(): pl.pallas_call(functools.partial(fwd_body, bq=bq), out_shape=(sd((rows, w...  28.8 us
    pallas_call x1, Pallas kernels, qkv_call(): pl.pallas_call(qkv_body, out_shape=(sd((rows, d), BF16), sd((rows, d), BF...  24.2 us
    reshape x7, local copies, waits for them, and re-layouts, on_device(): row = lambda a: a.astype(F32).reshape(1, -1)  8.85 us
    mul x3, other arithmetic, on_device(): fin = lambda a: a.astype(F32) * factor  5.4 us

profile of v3, /device:TPU:0, one launch (start us, length us, event | category | flops | bytes accessed | tf_op | source)
XLA Modules:
  0.0 249.7 jit_solution(11556327722397246820)
XLA Ops:
  1.3 1.3 reshape.92.gain
  2.6 1.3 convert_element_type.37.bias
  3.8 1.3 reshape.96.pb
  5.1 1.3 reshape.104.db
  6.3 1.3 reshape.94.shift
  7.6 1.3 reshape.98.gain
  8.9 1.3 reshape.100.shift
  10.1 1.3 reshape.102.ub
  11.4 24.2 %norm_qkv.1 = (bf16[1024,768]{1,0:T(8,128)(2,1)}, bf16[1024,768]{1,0:T(8,128)(2,1)}, bf16[1024,384]{1,0:T(8,128)(2,1)}, bf16[1024,384]{1,0:T(8,128)(2,1)}, bf16[1024,384]{1,0:T(8,128)(2,1)}) custom-call(bf16[1024,384]{1,0:T(8,128)(2,1)} %own.1, bf16[1024,384]{1,0:T(8,128)(2,1)} %own.1, bf16[3,768,384]{2,1,0:T(8,128)(2,1)} %bitcast.23, ...), custom_call_target="tpu_custom_call" | custom-call | flops 1811939328 | bytes 9633792 | tf_op jit(solution)/shard_map/norm_qkv/pallas_call | solution.py:231
  35.6 28.8 %attend_fwd.1 = (bf16[1024,384]{1,0:T(8,128)(2,1)}, bf16[6,1024,128]{2,1,0:T(8,128)(2,1)}, bf16[1024,384]{1,0:T(8,128)(2,1)}, bf16[384,768]{1,0:T(8,128)(2,1)}) custom-call(s32[1]{0:T(128)S(6)} %copy.30.len_ref, bf16[1024,384]{1,0:T(8,128)(2,1)} %get-tuple-element.51.q, bf16[1024,384]{1,0:T(8,128)(2,1)} %get-tuple-element.52.k, ...), custom_call_target="tpu_custom_call" | custom-call | flops 3221225472 | bytes 4718592 | tf_op jit(solution)/shard_map/attend_fwd/pallas_call | solution.py:341
  64.4 56.6 %mlp.1 = (f32[1024,384]{1,0:T(8,128)}, bf16[1024,384]{1,0:T(8,128)(2,1)}, bf16[1024,384]{1,0:T(8,128)(2,1)}, f32[512,768]{1,0:T(8,128)}, bf16[768,1536]{1,0:T(8,...) custom-call(s32[1]{0:T(128)S(6)} %copy.30.len_ref, ...), custom_call_target="tpu_custom_call" | custom-call | flops 15703474176 | bytes 17301504 | tf_op jit(solution)/shard_map/mlp/pallas_call | solution.py:532
  121.1 47.9 %attend_bwd.1 = (bf16[1024,384]{1,0:T(8,128)(2,1)}, bf16[1024,384]{1,0:T(8,128)(2,1)}, bf16[1024,384]{1,0:T(8,128)(2,1)}, bf16[1024,384]{1,0:T(8,128)(2,1)}, bf1...) custom-call(s32[1]{0:T(128)S(6)} %copy.30.len_ref, ...), custom_call_target="tpu_custom_call" | custom-call | flops 8053063680 | bytes 7077888 | tf_op jit(solution)/shard_map/attend_bwd/pallas_call | solution.py:669
  169.0 2.6 %add_convert_fusion = bf16[1024,384]{1,0:T(8,128)(2,1)} fusion(f32[1024,384]{1,0:T(8,128)} %get-tuple-element.57, bf16[1024,384]{1,0:T(8,128)(2,1)} %get-tuple-element.65), kind=kLoop, calls=%fused_computation.3 | loop fusion | flops 1179648 | bytes 3145728 | tf_op jit(solution)/shard_map/convert_element_type | solution.py:899
  171.6 63.3 %last.1 = (bf16[1024,384]{1,0:T(8,128)(2,1)}, bf16[768,1536]{1,0:T(8,128)(2,1)}, bf16[768,384]{1,0:T(8,128)(2,1)}, bf16[768,384]{1,0:T(8,128)(2,1)}, bf16[768,38...) custom-call(bf16[1024,384]{1,0:T(8,128)(2,1)} %get-tuple-element.66.dq, ...), custom_call_target="tpu_custom_call" | custom-call | flops 3623878656 | bytes 12582912 | tf_op jit(solution)/shard_map/last/pallas_call | solution.py:857
  235.0 0.0 copy-start.5
  235.0 0.8 broadcast_multiply_fusion
  235.8 0.6 slice_bitcast_fusion
  236.4 0.6 slice_bitcast_fusion.1
  237.0 0.6 reshape.90
  237.6 1.1 multiply_bitcast_fusion.2
  238.7 0.0 copy-done.5
  238.7 0.1 convert_multiply_fusion.3
  238.8 0.0 copy-start.3
  238.8 0.0 copy-start.4
  238.9 1.1 pad_maximum_fusion
  240.0 0.1 copy-done.3
  240.0 0.5 copy-done.4
  240.5 0.2 multiply_bitcast_fusion
  240.7 0.0 copy-start.1
  240.7 2.0 maximum_bitcast_fusion
  242.7 0.8 copy-done.1
  243.5 0.0 copy-start
  243.5 2.8 %convert_multiply_fusion.1 = f32[768,1536]{1,0:T(8,128)} fusion(bf16[768,1536]{1,0:T(8,128)(2,1)S(1)} %copy-done.1), kind=kLoop, calls=%fused_computation.1 | loop fusion | flops 2359296 | bytes 7077888 | tf_op jit(solution)/shard_map/mul | solution.py:901
  246.3 0.0 copy-done
  246.3 0.0 copy-start.2
  246.3 2.5 convert_multiply_fusion
  248.8 0.0 copy-done.2
  248.8 0.9 copy.31
Async XLA Ops:
  235.0 3.8 %copy-start.5 = (bf16[768,384]{1,0:T(8,128)(2,1)S(1)}, bf16[768,384]{1,0:T(8,128)(2,1)}, u32[]{:S(2)}) copy-start(bf16[768,384]{1,0:T(8,128)(2,1)} %get-tuple-element.83) | copy-start | bytes 1769476
  238.8 1.2 copy-start.3
  238.8 1.7 copy-start.4
  240.7 2.8 %copy-start.1 = (bf16[768,1536]{1,0:T(8,128)(2,1)S(1)}, bf16[768,1536]{1,0:T(8,128)(2,1)}, u32[]{:S(2)}) copy-start(bf16[768,1536]{1,0:T(8,128)(2,1)} %get-tuple-element.84) | copy-start | bytes 7077892
  243.5 2.8 %copy-start = (bf16[1536,768]{1,0:T(8,128)(2,1)S(1)}, bf16[1536,768]{1,0:T(8,128)(2,1)}, u32[]{:S(2)}) copy-start(bf16[1536,768]{1,0:T(8,128)(2,1)} %get-tuple-element.85) | copy-start | bytes 7077892
  246.3 2.5 copy-start.2

commit v4 on v3

--- a/solution.py
+++ b/solution.py
@@ -58,6 +58,11 @@
 
 
 MESH = pl.DeviceIdType.MESH
+scope = jax.named_scope
+
+
+def vec(ref):
+    return ref[...].astype(F32).reshape(1, -1)
 
 
 def bit_of(index, bit):
@@ -214,14 +219,15 @@
             copy(at).start()
 
     xf[:, lane_part(n, cw)] = own[...]
-    copy(i).wait()
+    with scope("wait"):
+        copy(i).wait()
     xf[:, lane_part(1 - n, cw)] = got[block_rows(i * rows, rows), :]
     xhat, _ = norm_rows(xf[...].astype(F32))
-    y = (xhat * gain[...] + shift[...]).astype(BF16)
+    y = (xhat * vec(gain) + vec(shift)).astype(BF16)
     low[...] = y
-    q[...] = (dot(y, w[0]) + bias[0:1, :]).astype(BF16) * jnp.asarray(HEAD**-0.5, BF16)
+    q[...] = (dot(y, w[0]) + bias[0:1, :].astype(F32)).astype(BF16) * jnp.asarray(HEAD**-0.5, BF16)
     k[...] = dot(y, w[1]).astype(BF16)
-    v[...] = (dot(y, w[2]) + bias[1:2, :]).astype(BF16)
+    v[...] = (dot(y, w[2]) + bias[1:2, :].astype(F32)).astype(BF16)
 
 
 def qkv_call(own, w, bias, gain, shift, block=256):
@@ -357,7 +363,7 @@
 
 
 def mlp_body(
-    len_ref, xf, mo, mr, pwo, pwr, pb, gain, shift, ub, db, up_hbm, down_hbm, cot,
+    len_ref, xf, mo, mr, pwo, pwr, pb, gain, shift, ub, up_hbm, down_hbm, cot,
     lo, lo_send, gmix, gm, gup, down_own, gp_own, gp_other, sum_ub, sum_db, sum_g, sum_s, sum_pb,
     up, down, cot_got, cf, mid, second, active, slope, gh, gs_send, gs_got, gs_own, gdown, box, part,
     glow, gmix_send, load_sem, nsend, nrecv, wsend, wrecv,
@@ -390,25 +396,27 @@
 
     def forward(i, carry):
         r = block_rows(i * block, block)
-        m = xf[r, :].astype(F32) + (dot(mo[r, :], pwo[...]) + dot(mr[r, :], pwr[...])) + pb[...]
+        m = xf[r, :].astype(F32) + (dot(mo[r, :], pwo[...]) + dot(mr[r, :], pwr[...])) + vec(pb)
         mid[r, :] = m
         xhat, _ = norm_rows(m)
-        sec = (xhat * gain[...] + shift[...]).astype(BF16)
+        sec = (xhat * vec(gain) + vec(shift)).astype(BF16)
         second[r, :] = sec
-        hid = dot(sec, up[...]) + ub[...]
+        hid = dot(sec, up[...]) + vec(ub)
         sq = hid * hid
         t = jnp.tanh(GELU_A * (hid + GELU_B * (sq * hid)))
         hf = 0.5 * (1.0 + t)
         act = (hid * hf).astype(BF16)
         active[r, :] = act
         slope[r, :] = hf + (0.5 * hid) * (1.0 - t * t) * (GELU_A + (3.0 * GELU_A * GELU_B) * sq)
-        lo[r, :] = mid[r, mine] + dot(act, down[:, mine]) + db[:, mine]
+        lo[r, :] = mid[r, mine] + dot(act, down[:, mine])
         lo_send[r, :] = dot(act, down[:, other]).astype(BF16)
         return carry
 
-    for load in loads:
-        load.wait()
-    lax.fori_loop(0, rows // block, forward, 0)
+    with scope("load"):
+        for load in loads:
+            load.wait()
+    with scope("forward"):
+        lax.fori_loop(0, rows // block, forward, 0)
 
     def backward(side, j, a):
         src, dst = cot_copy(side, j)
@@ -443,8 +451,10 @@
         sum_ub[...] += jnp.sum(ghid.astype(F32), axis=0, keepdims=True)
         return carry
 
-    lax.fori_loop(0, each, for_peer, 0)
-    lax.fori_loop(0, each, for_own, 0)
+    with scope("for_peer"):
+        lax.fori_loop(0, each, for_peer, 0)
+    with scope("for_own"):
+        lax.fori_loop(0, each, for_own, 0)
 
     chains = []
     for a, (kind, cols) in enumerate(thirds(d)):
@@ -461,20 +471,24 @@
         gup[c, :] = dot_tn(second[:, c], gh[...]).astype(BF16)
         return carry
 
-    lax.fori_loop(0, f // 256, weight_down, 0)
+    with scope("w_down"):
+        lax.fori_loop(0, f // 256, weight_down, 0)
     for chain in chains:
         chain.scatter_start(0)
-    lax.fori_loop(0, d // 256, weight_up, 0)
+    with scope("w_up"):
+        lax.fori_loop(0, d // 256, weight_up, 0)
 
     def advance(step):
-        for chain in chains:
-            chain.scatter_end(step)
-            if step + 1 < bits(wide):
-                chain.scatter_start(step + 1)
+        with scope(f"step{step}"):
+            for chain in chains:
+                chain.scatter_end(step)
+                if step + 1 < bits(wide):
+                    chain.scatter_start(step + 1)
 
     advance(0)
-    for j in range(each):
-        gs_copy(j).wait()
+    with scope("gs_wait"):
+        for j in range(each):
+            gs_copy(j).wait()
     for ref in (sum_g, sum_s, sum_pb, sum_db):
         ref[...] = jnp.zeros_like(ref)
 
@@ -486,7 +500,7 @@
         r, rh = block_rows(n * half + j * block, block), block_rows(j * block, block)
         g = gs_own[rh, :] + gs_got[rh, :].astype(F32)
         xhat, scale = norm_rows(mid[r, :])
-        gg = g * gain[...]
+        gg = g * vec(gain)
         m1 = jnp.mean(gg, axis=-1, keepdims=True)
         m2 = jnp.mean(gg * xhat, axis=-1, keepdims=True)
         c = cf[r, :].astype(F32)
@@ -503,7 +517,8 @@
         sum_db[...] += jnp.sum(c, axis=0, keepdims=True)
         return carry
 
-    lax.fori_loop(0, each, back_norm, 0)
+    with scope("back_norm"):
+        lax.fori_loop(0, each, back_norm, 0)
     for step in range(1, bits(wide)):
         advance(step)
         if step == 1:
@@ -514,15 +529,12 @@
                 dst[0:lw, :] = total[:, :cw]
                 dst[lw : 2 * lw, :] = total[:, cw:]
 
-    def received(j):
-        r = block_rows((1 - n) * half + j * block, block)
-        return remote(gmix_send.at[block_rows(j * block, block)], gmix.at[r], narrow, 3 * each + j, peer)
-
-    for j in range(each):
-        gmix_copy(j).wait()
-
-
-def mlp_call(length, xf, mo, mr, pwo, pwr, pb, gain, shift, up, ub, down, db, cot, wide):
+    with scope("gmix_wait"):
+        for j in range(each):
+            gmix_copy(j).wait()
+
+
+def mlp_call(length, xf, mo, mr, pwo, pwr, pb, gain, shift, up, ub, down, cot, wide):
     rows, d = xf.shape
     f, lw, cw = up.shape[1], mo.shape[1], cot.shape[1]
     half = rows // 2
@@ -536,7 +548,7 @@
             sd((d, f), BF16), sd((chain.size, d), BF16), sd((2 * lw, cw), BF16), sd((2 * lw, cw), BF16),
             sd((1, f), F32), sd((1, d), F32), sd((1, d), F32), sd((1, d), F32), sd((1, d), F32),
         ),
-        in_specs=[pl.BlockSpec(memory_space=pltpu.SMEM)] + [vmem()] * 10 + [anywhere(), anywhere(), vmem()],
+        in_specs=[pl.BlockSpec(memory_space=pltpu.SMEM)] + [vmem()] * 9 + [anywhere(), anywhere(), vmem()],
         out_specs=(vmem(),) * 13,
         scratch_shapes=[
             vm((d, f), BF16), vm((f, d), BF16), vm((rows, cw), BF16), vm((rows, d), BF16), vm((rows, d), F32),
@@ -548,7 +560,7 @@
         compiler_params=params(collective_id=3, has_side_effects=True),
         cost_estimate=cost(2 * rows * d * (d + 6 * f), 2 * (rows * d * 8 + 2 * d * f), rows * f),
         name="mlp",
-    )(length, xf, mo, mr, pwo, pwr, pb, gain, shift, ub, db, up, down, cot)
+    )(length, xf, mo, mr, pwo, pwr, pb, gain, shift, ub, up, down, cot)
 
 
 def bwd_body(
@@ -631,13 +643,15 @@
     put(dv, pl.ds(0, keys), dv_acc[...])
 
     def advance(step):
-        for chain in scatters:
-            chain.scatter_end(step)
-            if step + 1 < steps:
-                chain.scatter_start(step + 1)
-        for chain in gathers:
-            chain.gather_end(step)
-            chain.gather_start(step + 1)
+        with scope(f"scatter{step}"):
+            for chain in scatters:
+                chain.scatter_end(step)
+                if step + 1 < steps:
+                    chain.scatter_start(step + 1)
+        with scope(f"gather{step}"):
+            for chain in gathers:
+                chain.gather_end(step)
+                chain.gather_start(step + 1)
         if step == steps - 1:
             shard.start()
 
@@ -692,7 +706,7 @@
 def last_body(
     dq, dk, dv, low_hbm, w_hbm, xf_hbm, gm, gain, up_own, gp_sum, s_ub, s_db, s_g2, s_s2, s_pb,
     ig, gup, gp, gq, gk, gv, small,
-    low, w, xf, gn_send, gn_got, gn_own, ig_own, ig_send, src, box, part, own, vec, vec_box,
+    low, w, xf, gn_send, gn_got, gn_own, ig_own, ig_send, src, box, part, own, sums, sums_box,
     load_sem, nsend, nrecv, wsend, wrecv, *, wide,
 ):
     n, me = lax.axis_index("narrow"), lax.axis_index("wide")
@@ -700,7 +714,7 @@
     narrow, across = (nsend, nrecv), (wsend, wrecv)
     steps = bits(wide)
     rows, lw = dq.shape
-    d = gain.shape[1]
+    d = gain.shape[0]
     cw = d // 2
     half, block = rows // 2, min(256, rows // 2)
     each = half // block
@@ -729,22 +743,25 @@
         scatters.append(chain.gather(own.at[c], outs[c], across, (7 + c) * steps, pl.ds(0, lw)))
 
     def scatter_step(step):
-        for chain in scatters:
-            chain.scatter_end(step)
-            if step + 1 < steps:
-                chain.scatter_start(step + 1)
-            else:
-                chain.gather_open()
-                chain.gather_start(0)
+        with scope(f"scatter{step}"):
+            for chain in scatters:
+                chain.scatter_end(step)
+                if step + 1 < steps:
+                    chain.scatter_start(step + 1)
+                else:
+                    chain.gather_open()
+                    chain.gather_start(0)
 
     def gather_step(chains, step):
-        for chain in chains:
-            chain.gather_end(step)
-            chain.gather_start(step + 1)
+        with scope(f"gather{len(chains)}_{step}"):
+            for chain in chains:
+                chain.gather_end(step)
+                chain.gather_start(step + 1)
 
     loads[0].wait()
     for c in range(3):
-        src[c] = dot_tn(low[...], grads[c][...]).astype(BF16)
+        with scope("weights"):
+            src[c] = dot_tn(low[...], grads[c][...]).astype(BF16)
         scatters[c].scatter_start(0)
     gather_step(gathers, 0)
     loads[1].wait()
@@ -774,11 +791,11 @@
     gather_step(gathers, 1)
     loads[2].wait()
 
-    vec[...] = jnp.zeros_like(vec)
+    sums[...] = jnp.zeros_like(sums)
 
     def put(at, value):
         for i in range(value.shape[1] // 128):
-            vec[at + i : at + i + 1, :] = value[:, i * 128 : (i + 1) * 128]
+            sums[at + i : at + i + 1, :] = value[:, i * 128 : (i + 1) * 128]
 
     dr, fr, lr = d // 128, s_ub.shape[1] // 128, lw // 128
     shared = -(-6 * dr // 8) * 8
@@ -798,12 +815,13 @@
         return remote(ig_send.at[pl.ds(j * block, block)], ig.at[r], narrow, each + j, peer)
 
     for j in range(each):
-        gn_copy(j).wait()
+        with scope("gn_wait"):
+            gn_copy(j).wait()
         rh = pl.ds(j * block, block)
         r = block_rows(n * half + j * block, block)
         g = gn_own[rh, :] + gn_got[rh, :].astype(F32)
         xhat, scale = norm_rows(xf[r, :].astype(F32))
-        gg = g * gain[...]
+        gg = g * vec(gain)
         m1 = jnp.mean(gg, axis=-1, keepdims=True)
         m2 = jnp.mean(gg * xhat, axis=-1, keepdims=True)
         ig_own[...] = gm[rh, :] + scale * (gg - m1 - xhat * m2)
@@ -818,15 +836,15 @@
     def vec_copy(step):
         if step == 0:
             top = pl.ds(0, shared)
-            return remote(vec.at[top], vec_box.at[0, top], narrow, 2 * each, peer)
-        return remote(vec, vec_box.at[step], across, 10 * steps + step - 1, {"wide": flip(me, step - 1)})
+            return remote(sums.at[top], sums_box.at[0, top], narrow, 2 * each, peer)
+        return remote(sums, sums_box.at[step], across, 10 * steps + step - 1, {"wide": flip(me, step - 1)})
 
     def vec_end(step):
         vec_copy(step).wait()
         if step == 0:
-            vec[0:shared, :] += vec_box[0, 0:shared, :]
+            sums[0:shared, :] += sums_box[0, 0:shared, :]
         else:
-            vec[...] += vec_box[step]
+            sums[...] += sums_box[step]
         if step < steps:
             vec_copy(step + 1).start()
 
@@ -840,7 +858,7 @@
     for step in range(steps):
         gather_step(scatters, step)
     vec_end(steps)
-    small[...] = vec[...]
+    small[...] = sums[...]
     for j in range(each):
         ig_copy(j).wait()
 
@@ -873,6 +891,69 @@
     )(dq, dk, dv, low, w, xf, gm, gain, up_own, gp_sum, s_ub, s_db, s_g2, s_s2, s_pb)
 
 
+def finish_body(
+    lo, lo_got, bias, ig, up, down, q, k, v, p0, p1, small,
+    out, ig_out, o_qkv, o_qvb, o_proj, o_pb, o_up, o_ub, o_down, o_db, o_g1, o_s1, o_g2, o_s2,
+    *, factor, dr, shared,
+):
+    n = lax.axis_index("narrow")
+    cw = lo.shape[1]
+    out[...] = (lo[...] + lo_got[...].astype(F32) + bias[:, lane_part(n, cw)]).astype(BF16)
+    ig_out[...] = ig[...]
+    for c, ref in enumerate((q, k, v)):
+        o_qkv[c] = ref[...].astype(F32) * factor
+    o_proj[:, :cw] = p0[...].astype(F32) * factor
+    o_proj[:, cw:] = p1[...].astype(F32) * factor
+    o_up[...] = up[...].astype(F32) * factor
+    o_down[...] = down[...].astype(F32) * factor
+
+    @pl.when(pl.program_id(0) == 0)
+    def _():
+        for i, ref in enumerate((o_g1, o_s1, o_g2, o_s2, o_pb, o_db)):
+            ref[...] = small[i * dr : (i + 1) * dr, :] * factor
+        fr = o_ub.shape[0]
+        o_ub[...] = small[shared : shared + fr, :] * factor
+        lr = o_qvb.shape[1] // 128
+        for c in range(2):
+            for i in range(lr):
+                at = shared + fr + c * lr + i
+                o_qvb[c : c + 1, i * 128 : (i + 1) * 128] = small[at : at + 1, :] * factor
+
+
+def finish_call(lo, lo_got, bias, ig, up, down, q, k, v, p, small, factor, grid=8):
+    rows, cw = lo.shape
+    (d, f), lw = up.shape, q.shape[1]
+    dr, shared = d // 128, -(-6 * d // 1024) * 8
+    sd = jax.ShapeDtypeStruct
+    tiny = [sd((dr, 128), F32)] * 2
+    shapes = (
+        [sd((rows, cw), BF16), sd((rows, cw), BF16), sd((3, d, lw), F32), sd((2, lw), F32), sd((lw, d), F32)]
+        + [sd((dr, 128), F32), sd((d, f), F32), sd((f // 128, 128), F32), sd((f, d), F32)]
+        + [sd((dr, 128), F32)] * 5
+    )
+    big = lambda a: rows_spec(a.shape[0] // grid, a.shape[1])
+    pb = lw // grid
+    specs = []
+    for i, s in enumerate(shapes):
+        if len(s.shape) == 3:
+            specs.append(pl.BlockSpec((3, d // grid, lw), lambda i, *_: (0, i, 0)))
+        elif i in (0, 1, 4, 6, 8):
+            specs.append(big(s))
+        else:
+            specs.append(whole_spec(s.shape))
+    return pl.pallas_call(
+        functools.partial(finish_body, factor=factor, dr=dr, shared=shared),
+        out_shape=tuple(shapes),
+        grid=(grid,),
+        in_specs=[big(lo), big(lo_got), whole_spec(bias.shape), big(ig), big(up), big(down), big(q), big(k), big(v)]
+        + [rows_spec(pb, cw), rows_spec(pb, cw, grid), whole_spec(small.shape)],
+        out_specs=tuple(specs),
+        compiler_params=params(),
+        cost_estimate=cost(up.size * 8, up.size * 24),
+        name="finish",
+    )(lo, lo_got, bias, ig, up, down, q, k, v, p, p, small)
+
+
 def on_device(
     tokens, lengths, qkv_weight, qv_bias, proj_weight, proj_bias, up_weight, up_bias,
     down_weight, down_bias, first_gain, first_shift, second_gain, second_shift, cotangent,
@@ -880,35 +961,29 @@
     cw = tokens.shape[1]
     d, ff, lw = 2 * cw, up_weight.shape[1], proj_weight.shape[0]
     wide = lax.axis_size("wide")
-    row = lambda a: a.astype(F32).reshape(1, -1)
     w3 = jnp.transpose(qkv_weight, (1, 0, 2))
-    gain1, shift1, gain2, shift2 = map(row, (first_gain, first_shift, second_gain, second_shift))
-
-    xf, low, q, k, v = qkv_call(tokens, w3, qv_bias.astype(F32), gain1, shift1)
+
+    xf, low, q, k, v = qkv_call(tokens, w3, qv_bias, first_gain, first_shift)
     mixed, qa, mixed_got, proj_got = attend_forward(lengths, q, k, v, proj_weight)
     lo, lo_send, gmix, gm, gup, down_own, gp_own, gp_other, s_ub, s_db, s_g2, s_s2, s_pb = mlp_call(
-        lengths, xf, mixed, mixed_got, proj_weight, proj_got, row(proj_bias), gain2, shift2,
-        up_weight, row(up_bias), down_weight, row(down_bias), cotangent, wide,
+        lengths, xf, mixed, mixed_got, proj_weight, proj_got, proj_bias, second_gain, second_shift,
+        up_weight, up_bias, down_weight, cotangent, wide,
     )
     dq, dk, dv, lo_got, gdown, up_own, gp_sum = attend_backward(
         lengths, qa, k, v, gmix, mixed, lo_send, gup, down_own, gp_own, gp_other, wide
     )
     ig, gup, gp, gq, gk, gv, small = last_call(
-        dq, dk, dv, low, w3, xf, gm, gain1, up_own, gp_sum, s_ub, s_db, s_g2, s_s2, s_pb, wide
+        dq, dk, dv, low, w3, xf, gm, first_gain, up_own, gp_sum, s_ub, s_db, s_g2, s_s2, s_pb, wide
     )
-    layer_out = (lo + lo_got.astype(F32)).astype(BF16)
-    factor = 1.0 / (lengths.shape[0] * wide)
-    fin = lambda a: a.astype(F32) * factor
-    s_qkv = jnp.stack([fin(a) for a in (gq, gk, gv)])
-    s_proj = jnp.concatenate([fin(gp[:lw]), fin(gp[lw:])], axis=1)
-    flat = (small * factor).reshape(-1)
-    shared = -(-6 * d // 1024) * 1024
-    g1, s1, g2, s2, pb, dbs = (flat[i * d : (i + 1) * d] for i in range(6))
-    ubs = flat[shared : shared + ff]
-    qvb = flat[shared + ff : shared + ff + 2 * lw].reshape(2, lw)
+    out, ig, o_qkv, o_qvb, o_proj, *rest = finish_call(
+        lo, lo_got, down_bias.astype(F32).reshape(1, -1), ig, gup, gdown, gq, gk, gv, gp, small,
+        1.0 / (lengths.shape[0] * wide),
+    )
+    pb, up, ubs, down, dbs, g1, s1, g2, s2 = rest
+    flat = lambda a: a.reshape(-1)
     return (
-        layer_out, ig, jnp.transpose(s_qkv, (1, 0, 2)), qvb,
-        s_proj, pb, fin(gup), ubs, fin(gdown), dbs, g1, s1, g2, s2,
+        out, ig, jnp.transpose(o_qkv, (1, 0, 2)), o_qvb, o_proj, flat(pb), up, flat(ubs), down, flat(dbs),
+        flat(g1), flat(s1), flat(g2), flat(s2),
     )
 
 

time: 250 us -> 235 us (0.940)
  other arithmetic: 14.5 us -> 0 us
  local copies, waits for them, and re-layouts: 12.9 us -> 1.27 us
  Pallas kernels: 221 us -> 232 us
    pallas_call x0 -> x1, Pallas kernels: none -> 10.9 us  [finish_call(): pl.pallas_call(functools.partial(finish_body, factor=factor, dr=dr, share...]
    reshape x8 -> x1, local copies, waits for them, and re-layouts: 9.44 us -> 1.27 us  [on_device(): down_bias.astype(F32).reshape(1, -1)]
    mul x4 -> x0, other arithmetic: 6.23 us -> none  [the longest x3 5.4 us: on_device(): fin = lambda a: a.astype(F32) * factor]
    convert_element_type x2 -> x0, other arithmetic: 3.9 us -> none  [the longest x1 2.64 us: on_device(): layer_out = (lo + lo_got.astype(F32)).astype(BF16)]
where the time goes in v4:
time: 235 us
  Pallas kernels  232 us (99%)
    pallas_call x1, Pallas kernels, last_call(): pl.pallas_call(functools.partial(last_body, wide=wide), out_shape=(sd((ro...  63.3 us
    pallas_call x1, Pallas kernels, mlp_call(): pl.pallas_call(functools.partial(mlp_body, wide=wide), out_shape=(sd((row...  56.7 us
    pallas_call x1, Pallas kernels, attend_backward(): pl.pallas_call(functools.partial(bwd_body, bq=bq, wide=wide), out_shape=(...  47.9 us
    pallas_call x1, Pallas kernels, attend_forward(): pl.pallas_call(functools.partial(fwd_body, bq=bq), out_shape=(sd((rows, w...  28.8 us
    pallas_call x1, Pallas kernels, qkv_call(): pl.pallas_call(qkv_body, out_shape=(sd((rows, d), BF16), sd((rows, d), BF...  24.2 us
    pallas_call x1, Pallas kernels, finish_call(): pl.pallas_call(functools.partial(finish_body, factor=factor, dr=dr, share...  10.9 us

profile of v4, /device:TPU:0, one launch (start us, length us, event | category | flops | bytes accessed | tf_op | source)
XLA Modules:
  0.0 234.7 jit_solution(1378312130263886429)
XLA Ops:
  1.3 1.3 reshape.64.bias
  2.6 24.2 %norm_qkv.1 = (bf16[1024,768]{1,0:T(8,128)(2,1)}, bf16[1024,768]{1,0:T(8,128)(2,1)}, bf16[1024,384]{1,0:T(8,128)(2,1)}, bf16[1024,384]{1,0:T(8,128)(2,1)}, bf16[1024,384]{1,0:T(8,128)(2,1)}) custom-call(bf16[1024,384]{1,0:T(8,128)(2,1)} %own.1, bf16[1024,384]{1,0:T(8,128)(2,1)} %own.1, bf16[3,768,384]{2,1,0:T(8,128)(2,1)} %bitcast.10, bf16[2,384]{1,0:T(2,128)(2,1)} %bias.1, ...), custom_call_target="tpu_custom_call" | custom-call | flops 1811939328 | bytes 9633792 | tf_op jit(solution)/shard_map/norm_qkv/pallas_call | solution.py:237
  26.7 28.8 %attend_fwd.1 = (bf16[1024,384]{1,0:T(8,128)(2,1)}, bf16[6,1024,128]{2,1,0:T(8,128)(2,1)}, bf16[1024,384]{1,0:T(8,128)(2,1)}, bf16[384,768]{1,0:T(8,128)(2,1)}) custom-call(s32[1]{0:T(128)S(6)} %copy.29.len_ref, bf16[1024,384]{1,0:T(8,128)(2,1)} %get-tuple-element.65.q, bf16[1024,384]{1,0:T(8,128)(2,1)} %get-tuple-element.66.k, ...), custom_call_target="tpu_custom_call" | custom-call | flops 3221225472 | bytes 4718592 | tf_op jit(solution)/shard_map/attend_fwd/pallas_call | solution.py:347
  55.6 56.7 %mlp.1 = (f32[1024,384]{1,0:T(8,128)}, bf16[1024,384]{1,0:T(8,128)(2,1)}, bf16[1024,384]{1,0:T(8,128)(2,1)}, f32[512,768]{1,0:T(8,128)}, bf16[768,1536]{1,0:T(8,...) custom-call(s32[1]{0:T(128)S(6)} %copy.29.len_ref, ...), custom_call_target="tpu_custom_call" | custom-call | flops 15703474176 | bytes 17301504 | tf_op jit(solution)/shard_map/mlp/pallas_call | solution.py:544
  112.3 47.9 %attend_bwd.1 = (bf16[1024,384]{1,0:T(8,128)(2,1)}, bf16[1024,384]{1,0:T(8,128)(2,1)}, bf16[1024,384]{1,0:T(8,128)(2,1)}, bf16[1024,384]{1,0:T(8,128)(2,1)}, bf1...) custom-call(s32[1]{0:T(128)S(6)} %copy.29.len_ref, ...), custom_call_target="tpu_custom_call" | custom-call | flops 8053063680 | bytes 7077888 | tf_op jit(solution)/shard_map/attend_bwd/pallas_call | solution.py:683
  160.2 63.3 %last.1 = (bf16[1024,384]{1,0:T(8,128)(2,1)}, bf16[768,1536]{1,0:T(8,128)(2,1)}, bf16[768,384]{1,0:T(8,128)(2,1)}, bf16[768,384]{1,0:T(8,128)(2,1)}, bf16[768,38...) custom-call(bf16[1024,384]{1,0:T(8,128)(2,1)} %get-tuple-element.80.dq, ...), custom_call_target="tpu_custom_call" | custom-call | flops 3623878656 | bytes 12582912 | tf_op jit(solution)/shard_map/last/pallas_call | solution.py:875
  223.6 10.9 %finish.1 = (bf16[1024,384]{1,0:T(8,128)(2,1)}, bf16[1024,384]{1,0:T(8,128)(2,1)}, f32[3,768,384]{2,1,0:T(8,128)}, f32[2,384]{1,0:T(2,128)}, f32[384,768]{1,0:T(...) custom-call(f32[1024,384]{1,0:T(8,128)} %get-tuple-element.71.lo, ...), custom_call_target="tpu_custom_call" | custom-call | flops 9437184 | bytes 28311552 | tf_op jit(solution)/shard_map/finish/pallas_call | solution.py:944

commit v5 on v4

v5 whole, which is shorter than its diff:
```python
import functools

import jax
import jax.numpy as jnp
from jax import lax
from jax.experimental import pallas as pl
from jax.experimental.pallas import tpu as pltpu
from jax.sharding import PartitionSpec as P

EPS = 1e-05
HEAD = 64
F32, BF16 = jnp.float32, jnp.bfloat16
NT = (((1,), (1,)), ((), ()))
TN = (((0,), (0,)), ((), ()))
GELU_A, GELU_B = 0.7978845608028654, 0.044715
VMEM_LIMIT = 63 * 1024 * 1024


def dot(a, b):
    return jnp.dot(a, b, preferred_element_type=F32)


def dot_nt(a, b):
    return lax.dot_general(a, b, NT, preferred_element_type=F32)


def dot_tn(a, b):
    return lax.dot_general(a, b, TN, preferred_element_type=F32)


def params(**more):
    return pltpu.CompilerParams(vmem_limit_bytes=VMEM_LIMIT, **more)


def cost(flops, size, trans=0):
    return pl.CostEstimate(flops=int(flops), bytes_accessed=int(size), transcendentals=int(trans))


def lane_part(which, width):
    return pl.ds(pl.multiple_of(which * width, 128), width)


def norm_rows(x):
    mean = jnp.mean(x, axis=-1, keepdims=True)
    cen = x - mean
    var = jnp.mean(cen * cen, axis=-1, keepdims=True)
    r = lax.rsqrt(var + EPS)
    return cen * r, r


def rows_spec(rows, cols, base=0):
    return pl.BlockSpec((rows, cols), lambda i, *_: (i + base, 0))


def whole_spec(shape):
    zeros = (0,) * len(shape)
    return pl.BlockSpec(shape, lambda i, *_: zeros)


MESH = pl.DeviceIdType.MESH
scope = jax.named_scope


def vec(ref):
    return ref[...].astype(F32).reshape(1, -1)


def bit_of(index, bit):
    return (index // (1 << bit)) % 2


def flip(index, bit):
    return index + (1 - 2 * bit_of(index, bit)) * (1 << bit)


def greet(peers):
    barrier = pltpu.get_barrier_semaphore()
    for peer in peers:
        pl.semaphore_signal(barrier, inc=1, device_id=peer, device_id_type=MESH)
    pl.semaphore_wait(barrier, len(peers))


def remote(src, dst, sems, at, peer):
    return pltpu.make_async_remote_copy(
        src_ref=src, dst_ref=dst, send_sem=sems[0].at[at], recv_sem=sems[1].at[at],
        device_id=peer, device_id_type=MESH,
    )


def block_rows(start, size, unit=16):
    return pl.ds(start if isinstance(start, int) else pl.multiple_of(start, unit), size)


class Chain:
    def __init__(self, me, order, rows, cols, sems, at):
        self.me, self.cols, self.sems, self.at = me, cols, sems, at
        self.steps, self.splits = [], []
        base, size, box = 0, rows, 0
        for bit in order:
            if size % 32 == 0:
                half = size // 2
                mine = bit_of(me, bit)
                keep, give = base + mine * half, base + (1 - mine) * half
                self.splits.append((bit, keep, half))
            else:
                half, keep, give = size, base, base
            self.steps.append((bit, keep, give, half, box))
            base, size, box = keep, half, box + half
        self.base, self.size, self.box_rows = base, size, box

    def bind(self, src, box, part, own, dst=None, entry=0):
        self.src, self.box, self.part, self.own, self.dst, self.entry = src, box, part, own, dst, entry
        return self

    def _source(self, step):
        off = 0 if step == 0 else self.steps[0][1]
        return (self.src if step == self.entry else self.part), off

    def _scatter_copy(self, step):
        bit, _, give, half, box = self.steps[step]
        source, off = self._source(step)
        return remote(
            source.at[block_rows(give - off, half), self.cols],
            self.box.at[pl.ds(box, half), self.cols],
            self.sems, self.at + step, {"wide": flip(self.me, bit)},
        )

    def scatter_start(self, step):
        self._scatter_copy(step).start()

    def scatter_end(self, step):
        self._scatter_copy(step).wait()
        _, keep, _, half, box = self.steps[step]
        source, off = self._source(step)
        last = step == len(self.steps) - 1
        target, out = (self.own, keep) if last else (self.part, self.steps[0][1])
        unit = next(u for u in (96, 64, 48, 32, 16) if half % u == 0)

        def add(i, carry):
            at = i * unit
            got = self.box[block_rows(box + at, unit), self.cols]
            mine = source[block_rows(keep - off + at, unit), self.cols]
            target[block_rows(keep - out + at, unit), self.cols] = got + mine
            return carry

        lax.fori_loop(0, half // unit, add, 0)

    def gather_open(self, sem):
        region = self.dst.at[block_rows(self.base, self.size), self.cols]
        return pltpu.make_async_copy(self.own.at[:, self.cols], region, sem)

    def _gather_copy(self, step):
        bit, keep, half = self.splits[len(self.splits) - 1 - step]
        region = self.dst.at[block_rows(keep, half), self.cols]
        at = self.at + len(self.steps) + step
        return remote(region, region, self.sems, at, {"wide": flip(self.me, bit)})

    def gather_start(self, step):
        self._gather_copy(step).start()

    def gather_end(self, step):
        self._gather_copy(step).wait()


class Group:
    def __init__(self, chains, open_sem=None, at=0, entry=0, leave=None):
        self.chains, self.open_sem, self.at = chains, open_sem, at
        steps, splits = len(chains[0].steps), len(chains[0].splits)
        self.last = steps
        self.ops = [("scatter", i) for i in range(entry, steps if leave is None else leave)]
        if leave is None:
            self.ops += [("gather", i) for i in range(splits)]
        self.pos = -1

    @property
    def done(self):
        return self.pos >= len(self.ops)

    def next(self):
        pos = self.pos
        self.pos = min(pos + 1, len(self.ops))

        def tick():
            if pos >= len(self.ops):
                return
            if pos >= 0:
                kind, i = self.ops[pos]
                for chain in self.chains:
                    (chain.scatter_end if kind == "scatter" else chain.gather_end)(i)
            if pos + 1 >= len(self.ops):
                return
            kind, i = self.ops[pos + 1]
            if kind == "gather" and i == 0:
                opens = [c.gather_open(self.open_sem.at[self.at + j]) for j, c in enumerate(self.chains)]
                for opened in opens:
                    opened.start()
                for opened in opens:
                    opened.wait()
            for chain in self.chains:
                (chain.scatter_start if kind == "scatter" else chain.gather_start)(i)

        return tick

    def tick(self):
        self.next()()


def bits(wide):
    return wide.bit_length() - 1


def order_of(wide, kind):
    steps = list(range(bits(wide)))
    return steps if kind == 0 else [0] + steps[2:] + steps[1:2]


def lanes_split(cols):
    w = max(128, cols // 6 // 128 * 128)
    return [(0, pl.ds(0, cols - w)), (1, pl.ds(cols - w, w))]


def wide_peers(me, wide):
    return [{"wide": flip(me, b)} for b in range(bits(wide))]


def vmem():
    return pl.BlockSpec(memory_space=pltpu.VMEM)


def anywhere():
    return pl.BlockSpec(memory_space=pl.ANY)


def sems(*counts):
    return [pltpu.SemaphoreType.DMA((c,)) for c in counts]


def qkv_body(own_hbm, own, w, bias, gain, shift, xf, low, q, k, v, got, send_sem, recv_sem):
    n = lax.axis_index("narrow")
    i = pl.program_id(0)
    rows, cw = own.shape
    peer = {"narrow": 1 - n}

    def copy(at):
        block = block_rows(at * rows, rows)
        return remote(own_hbm.at[block], got.at[block], (send_sem, recv_sem), at, peer)

    @pl.when(i == 0)
    def _():
        greet([peer])
        for at in range(got.shape[0] // rows):
            copy(at).start()

    xf[:, lane_part(n, cw)] = own[...]
    with scope("wait"):
        copy(i).wait()
    xf[:, lane_part(1 - n, cw)] = got[block_rows(i * rows, rows), :]
    xhat, _ = norm_rows(xf[...].astype(F32))
    y = (xhat * vec(gain) + vec(shift)).astype(BF16)
    low[...] = y
    q[...] = (dot(y, w[0]) + bias[0:1, :].astype(F32)).astype(BF16) * jnp.asarray(HEAD**-0.5, BF16)
    k[...] = dot(y, w[1]).astype(BF16)
    v[...] = (dot(y, w[2]) + bias[1:2, :].astype(F32)).astype(BF16)


def qkv_call(own, w, bias, gain, shift, block=256):
    rows, cw = own.shape
    d, lw = w.shape[1], w.shape[2]
    sd = jax.ShapeDtypeStruct
    return pl.pallas_call(
        qkv_body,
        out_shape=(sd((rows, d), BF16), sd((rows, d), BF16)) + (sd((rows, lw), BF16),) * 3,
        grid_spec=pltpu.PrefetchScalarGridSpec(
            num_scalar_prefetch=0,
            grid=(rows // block,),
            in_specs=[anywhere(), rows_spec(block, cw)] + [whole_spec(a.shape) for a in (w, bias, gain, shift)],
            out_specs=[rows_spec(block, d)] * 2 + [rows_spec(block, lw)] * 3,
            scratch_shapes=[pltpu.VMEM((rows, cw), BF16)] + sems(rows // block, rows // block),
        ),
        compiler_params=params(collective_id=1, has_side_effects=True),
        cost_estimate=cost(2 * rows * d * 3 * lw, 2 * (rows * d * 5 + w.size)),
        name="norm_qkv",
    )(own, own, w, bias, gain, shift)


def three(x):
    hi = x.astype(BF16).astype(F32)
    mid = (x - hi).astype(BF16).astype(F32)
    return hi, mid, x - hi - mid


def lanes_of(par):
    lane = lax.broadcasted_iota(jnp.int32, (1, 2 * HEAD), 1)
    mine = (lane // HEAD) == par
    return lane, mine, (1 - par) * HEAD


def place(lane, mine, at, base, terms):
    out = jnp.where(mine, base, 0.0)
    for i, term in enumerate(terms):
        out = jnp.where(lane == at + i, term, out)
    return out


def fwd_body(
    len_ref, q, k, v, pw, o, qa_out, o_got, pw_got, ka, va, send_sem, recv_sem, *, bq
):
    head = pl.program_id(0)
    par, pair = head % 2, head // 2
    lane, mine, at = lanes_of(par)
    n, me = lax.axis_index("narrow"), lax.axis_index("wide")
    peer, core = {"narrow": 1 - n}, {"wide": flip(me, 0)}
    pairs = pl.num_programs(0) // 2
    both = (send_sem, recv_sem)
    cols = lane_part(pair, 2 * HEAD)
    part = block_rows((me % 2) * (pw.shape[0] // 2), pw.shape[0] // 2)
    npairs = o.shape[1] // (2 * HEAD)
    weights = remote(pw.at[part], pw_got.at[part], both, npairs, peer)
    shared = remote(pw_got.at[part], pw_got.at[part], both, npairs + 1, core)

    @pl.when(head == 0)
    def _():
        greet([peer, core])
        weights.start()

    keys = k.shape[0]
    kpos = lax.broadcasted_iota(jnp.int32, (keys, 1), 0)
    kbias = jnp.where(kpos < len_ref[0], 0.0, -1e30)
    ka[...] = place(lane, mine, at, k[...].astype(F32), [kbias]).astype(BF16)
    va[...] = place(lane, mine, at, v[...].astype(F32), [1.0]).astype(BF16)
    tri = lax.broadcasted_iota(jnp.int32, (bq, bq), 1) <= lax.broadcasted_iota(jnp.int32, (bq, bq), 0)
    for i in range(q.shape[0] // bq):
        nk = (i + 1) * bq
        rows = pl.ds(i * bq, bq)
        qf = q[rows, :].astype(F32)
        qa = place(lane, mine, at, qf, [1.0])
        s = dot_nt(qa.astype(BF16), ka[0:nk, :])
        edge = jnp.where(tri, s[:, nk - bq :], -1e30)
        m = jnp.max(edge, axis=1, keepdims=True)
        if nk > bq:
            m = jnp.maximum(m, jnp.max(s[:, : nk - bq], axis=1, keepdims=True))
        pv = dot(jnp.exp(edge - m).astype(BF16), va[nk - bq : nk, :])
        if nk > bq:
            pv += dot(jnp.exp(s[:, : nk - bq] - m).astype(BF16), va[0 : nk - bq, :])
        total = jnp.sum(jnp.where(lane == at, pv, 0.0), axis=1, keepdims=True)
        out = (pv / total).astype(BF16).astype(F32)
        old = o[rows, cols].astype(F32)
        o[rows, cols] = jnp.where(mine, out, jnp.where(par == 0, 0.0, old)).astype(BF16)
        lse = m + jnp.log(total)
        qa_out[0, rows, :] = place(lane, mine, at, qf, [1.0, *three(lse)]).astype(BF16)

    def mixed(j):
        c = pl.ds(j * 2 * HEAD, 2 * HEAD)
        return remote(o.at[:, c], o_got.at[:, c], both, j, peer)

    for j in range(npairs):

        @pl.when(head == 2 * j + 1)
        def _():
            mixed(j).start()

    @pl.when(head == 3)
    def _():
        weights.wait()
        shared.start()

    @pl.when(head == 2 * npairs - 1)
    def _():
        shared.wait()
        for j in range(npairs):
            mixed(j).wait()


def attend_forward(length, q, k, v, pw, bq=256):
    rows, width = q.shape
    heads, pair = width // HEAD, 2 * HEAD
    half = lambda h, *_: (0, h // 2)
    sd = jax.ShapeDtypeStruct
    work = 2 * heads * rows * rows * HEAD
    return pl.pallas_call(
        functools.partial(fwd_body, bq=bq),
        out_shape=(
            sd((rows, width), BF16), sd((heads, rows, pair), BF16), sd((rows, width), BF16), sd(pw.shape, BF16),
        ),
        grid_spec=pltpu.PrefetchScalarGridSpec(
            num_scalar_prefetch=1,
            grid=(heads,),
            in_specs=[pl.BlockSpec((rows, pair), half)] * 3 + [anywhere()],
            out_specs=[vmem(), pl.BlockSpec((1, rows, pair), lambda h, *_: (h, 0, 0)), anywhere(), anywhere()],
            scratch_shapes=[pltpu.VMEM((rows, pair), BF16)] * 2 + sems(heads // 2 + 2, heads // 2 + 2),
        ),
        compiler_params=params(collective_id=2, has_side_effects=True),
        cost_estimate=cost(4 * work, 2 * rows * width * 6, work // 256),
        name="attend_fwd",
    )(length, q, k, v, pw)


def mlp_body(
    len_ref, xf_hbm, mo_hbm, mr_hbm, pwo_hbm, pwr_hbm, pb, gain, shift, ub, up_hbm, down_hbm, cot_hbm,
    lo_out, lo_send_out, gmix, gm_out, gup_out, down_part, gp_own, gp_other, sum_ub, sum_db, sum_g, sum_s, sum_pb,
    xf, mo, mr, pwo, pwr, up, down, cot, cot_got, cf, lo, lo_send, mid, second, active, slope, gh,
    gs_send, gs_got, gs_own, gdown, gup, box, gm, glow, gmix_send, load_sem, store_sem, nsend, nrecv, wsend, wrecv,
    *, wide,
):
    n, me = lax.axis_index("narrow"), lax.axis_index("wide")
    peer = {"narrow": 1 - n}
    rows, cw = cot.shape
    d, f = up.shape
    half, block = rows // 2, min(256, rows // 2)
    each = half // block
    mine, other = lane_part(n, cw), lane_part(1 - n, cw)
    narrow, across = (nsend, nrecv), (wsend, wrecv)
    count = iter(range(16))

    def load(src, dst):
        copy = pltpu.make_async_copy(src, dst, load_sem.at[next(count)])
        copy.start()
        return copy

    his, own = block_rows((1 - n) * half, half), block_rows(n * half, half)
    first = [load(a, b) for a, b in ((pwo_hbm, pwo), (pwr_hbm, pwr))]
    first += [load(a.at[his], b.at[his]) for a, b in ((xf_hbm, xf), (mo_hbm, mo), (mr_hbm, mr))]
    up_load = load(up_hbm, up)
    greet([peer] + wide_peers(me, wide))

    def cot_copy(side, j, a):
        r = block_rows(side * half + j * block, block)
        return remote(cot_hbm.at[r], cot_got.at[r], narrow, a * each + j, peer)

    for a, side in enumerate((n, 1 - n)):
        for j in range(each):
            cot_copy(side, j, a).start()
    down_load = load(down_hbm, down)
    cot_load = load(cot_hbm, cot)
    rest = [load(a.at[own], b.at[own]) for a, b in ((xf_hbm, xf), (mo_hbm, mo), (mr_hbm, mr))]

    def project(at):
        r = block_rows(at, block)
        m = xf[r, :].astype(F32) + (dot(mo[r, :], pwo[...]) + dot(mr[r, :], pwr[...])) + vec(pb)
        mid[r, :] = m
        xhat, _ = norm_rows(m)
        second[r, :] = (xhat * vec(gain) + vec(shift)).astype(BF16)

    def forward(at):
        r = block_rows(at, block)
        hid = dot(second[r, :], up[...]) + vec(ub)
        sq = hid * hid
        t = jnp.tanh(GELU_A * (hid + GELU_B * (sq * hid)))
        hf = 0.5 * (1.0 + t)
        act = (hid * hf).astype(BF16)
        active[r, :] = act
        slope[r, :] = hf + (0.5 * hid) * (1.0 - t * t) * (GELU_A + (3.0 * GELU_A * GELU_B) * sq)
        lo[r, :] = mid[r, mine] + dot(act, down[:, mine])
        lo_send[r, :] = dot(act, down[:, other]).astype(BF16)

    def backward(at):
        r = block_rows(at, block)
        pos = at + lax.broadcasted_iota(jnp.int32, (block, 1), 0)
        live = (pos < len_ref[0]).astype(F32)
        cf[r, mine] = (cot[r, :].astype(F32) * live).astype(BF16)
        cf[r, other] = (cot_got[r, :].astype(F32) * live).astype(BF16)
        ghid = (dot_nt(cf[r, :], down[...]) * slope[r, :]).astype(BF16)
        gh[r, :] = ghid
        sum_ub[...] += jnp.sum(ghid.astype(F32), axis=0, keepdims=True)
        return dot_nt(ghid, up[...])

    def every(side, body):
        def step(j, carry):
            body(side * half + j * block)
            return carry

        lax.fori_loop(0, each, step, 0)

    def both(at):
        project(at)
        forward(at)

    for ref in (sum_ub, sum_g, sum_s, sum_pb, sum_db):
        ref[...] = jnp.zeros_like(ref)
    with scope("load"):
        for copy in first:
            copy.wait()
    with scope("project"):
        every(1 - n, project)
    with scope("load2"):
        up_load.wait()
        down_load.wait()
    with scope("fwd_peer"):
        every(1 - n, forward)
    with scope("cot_wait"):
        cot_load.wait()
        for j in range(each):
            cot_copy(n, j, 0).wait()

    def gs_copy(j):
        r = block_rows(j * block, block)
        return remote(gs_send.at[r], gs_got.at[r], narrow, 2 * each + j, peer)

    def for_peer(j, carry):
        gs_send[block_rows(j * block, block), :] = backward((1 - n) * half + j * block).astype(BF16)
        gs_copy(j).start()
        return carry

    def for_own(j, carry):
        gs_own[block_rows(j * block, block), :] = backward(n * half + j * block)
        return carry

    with scope("for_peer"):
        lax.fori_loop(0, each, for_peer, 0)
    for copy in rest:
        copy.wait()
    with scope("fwd_own"):
        every(n, both)
    stores = []

    def store(src, dst):
        copy = pltpu.make_async_copy(src, dst, store_sem.at[len(stores)])
        copy.start()
        stores.append(copy)

    store(lo, lo_out)
    store(lo_send, lo_send_out)
    with scope("cot_wait2"):
        for j in range(each):
            cot_copy(1 - n, j, 1).wait()
    with scope("for_own"):
        lax.fori_loop(0, each, for_own, 0)

    def weight(dst, left, right):
        def step(i, carry):
            c = block_rows(i * 256, 256, 256)
            dst[c, :] = dot_tn(left[:, c], right[...]).astype(BF16)
            return carry

        lax.fori_loop(0, dst.shape[0] // 256, step, 0)

    chains = []
    for kind, cols in lanes_split(d):
        chain = Chain(me, order_of(wide, kind), f, cols, across, len(chains) * bits(wide))
        chains.append(chain.bind(gdown, box, down_part, None))
    reduce_down = Group(chains, leave=2)
    with scope("w_down"):
        weight(gdown, active, cf)
    reduce_down.tick()
    with scope("w_up"):
        weight(gup, second, gh)
    store(gup, gup_out)
    with scope("core"):
        reduce_down.tick()
    with scope("gs_wait"):
        for j in range(each):
            gs_copy(j).wait()

    def gmix_copy(j):
        r = block_rows(n * half + j * block, block)
        return remote(gmix_send.at[block_rows(j * block, block)], gmix.at[r], narrow, 3 * each + j, peer)

    def back_norm(j, carry):
        r, rh = block_rows(n * half + j * block, block), block_rows(j * block, block)
        g = gs_own[rh, :] + gs_got[rh, :].astype(F32)
        xhat, scale = norm_rows(mid[r, :])
        gg = g * vec(gain)
        m1 = jnp.mean(gg, axis=-1, keepdims=True)
        m2 = jnp.mean(gg * xhat, axis=-1, keepdims=True)
        c = cf[r, :].astype(F32)
        grad = c + scale * (gg - m1 - xhat * m2)
        gm[rh, :] = grad
        gl = grad.astype(BF16)
        glow[rh, :] = gl
        gmix_send[rh, :] = dot_nt(gl, pwr[...]).astype(BF16)
        gmix_copy(j).start()
        gmix[r, :] = dot_nt(gl, pwo[...]).astype(BF16)
        sum_g[...] += jnp.sum(g * xhat, axis=0, keepdims=True)
        sum_s[...] += jnp.sum(g, axis=0, keepdims=True)
        sum_pb[...] += jnp.sum(grad, axis=0, keepdims=True)
        sum_db[...] += jnp.sum(c, axis=0, keepdims=True)
        return carry

    with scope("back_norm"):
        lax.fori_loop(0, each, back_norm, 0)
    store(gm, gm_out)
    with scope("proj"):
        lw = mo.shape[1]
        for src, dst in ((mr, gp_other), (mo, gp_own)):
            total = dot_tn(src[own, :], glow[...]).astype(BF16)
            dst[0:lw, :] = total[:, :cw]
            dst[lw : 2 * lw, :] = total[:, cw:]
    with scope("gmix_wait"):
        for j in range(each):
            gmix_copy(j).wait()
    with scope("across"):
        reduce_down.tick()
    with scope("store"):
        for copy in stores:
            copy.wait()


def mlp_call(length, xf, mo, mr, pwo, pwr, pb, gain, shift, up, ub, down, cot, wide):
    rows, d = xf.shape
    f, lw, cw = up.shape[1], mo.shape[1], cot.shape[1]
    half = rows // 2
    sd, vm = jax.ShapeDtypeStruct, pltpu.VMEM
    each = half // min(256, half)
    return pl.pallas_call(
        functools.partial(mlp_body, wide=wide),
        out_shape=(
            sd((rows, cw), F32), sd((rows, cw), BF16), sd((rows, lw), BF16), sd((half, d), F32),
            sd((d, f), BF16), sd((f // 2, d), BF16), sd((2 * lw, cw), BF16), sd((2 * lw, cw), BF16),
            sd((1, f), F32), sd((1, d), F32), sd((1, d), F32), sd((1, d), F32), sd((1, d), F32),
        ),
        in_specs=[pl.BlockSpec(memory_space=pltpu.SMEM)] + [anywhere()] * 5 + [vmem()] * 4 + [anywhere()] * 3,
        out_specs=(anywhere(), anywhere(), vmem(), anywhere(), anywhere()) + (vmem(),) * 8,
        scratch_shapes=[
            vm((rows, d), BF16), vm((rows, lw), BF16), vm((rows, lw), BF16), vm((lw, d), BF16), vm((lw, d), BF16),
            vm((d, f), BF16), vm((f, d), BF16), vm((rows, cw), BF16), vm((rows, cw), BF16), vm((rows, d), BF16),
            vm((rows, cw), F32), vm((rows, cw), BF16), vm((rows, d), F32),
            vm((rows, d), BF16), vm((rows, f), BF16), vm((rows, f), F32), vm((rows, f), BF16),
            vm((half, d), BF16), vm((half, d), BF16), vm((half, d), F32), vm((f, d), BF16), vm((d, f), BF16),
            vm((f - f // 4, d), BF16), vm((half, d), F32), vm((half, d), BF16), vm((half, lw), BF16),
        ]
        + sems(16, 4, 4 * each, 4 * each, 2 * bits(wide), 2 * bits(wide)),
        compiler_params=params(collective_id=3, has_side_effects=True),
        cost_estimate=cost(2 * rows * d * (d + 6 * f), 2 * (rows * d * 8 + 2 * d * f), rows * f),
        name="mlp",
    )(length, xf, mo, mr, pwo, pwr, pb, gain, shift, ub, up, down, cot)


def back_body(
    len_ref, qa_hbm, k_hbm, v_hbm, do_hbm, o_hbm, low_hbm, w_hbm, xf_hbm, gm_hbm, gain, lo_send, gup_hbm,
    down_part_hbm, gp_own_hbm, gp_other_hbm, s_ub, s_db, s_g2, s_s2, s_pb,
    lo_got, down_out, up_out, gp_out, g0_out, g1_out, g2_out, ig, small,
    qa, k, v, do, o, low, wp, xf, gm, gup, down_part, gp_src, gp_got,
    ka, va, dk_acc, dv_acc, dqkv, gpair,
    down_box, down_part2, down_own, up_box, up_part, up_own, gp_box, gp_part, gp_own, pair_box, pair_part, pair_own,
    gn_send, gn_got, gn_own, ig_own, ig_send, sums, sums_box,
    load_sem, open_sem, nsend, nrecv, wsend, wrecv, *, bq, wide,
):
    n, me = lax.axis_index("narrow"), lax.axis_index("wide")
    peer = {"narrow": 1 - n}
    narrow, across = (nsend, nrecv), (wsend, wrecv)
    steps = bits(wide)
    heads, rows = qa.shape[0], qa.shape[1]
    pair_w = 2 * HEAD
    pairs = heads // 2
    d, lw = gain.shape[0], k.shape[1]
    cw = d // 2
    half, block = rows // 2, min(256, rows // 2)
    each = half // block
    count = iter(range(64))

    def load(src, dst):
        copy = pltpu.make_async_copy(src, dst, load_sem.at[next(count)])
        copy.start()
        return copy

    pair_loads = []
    for p in range(pairs):
        c = pl.ds(p * pair_w, pair_w)
        pair_loads.append(
            [load(a.at[:, c], b.at[:, c]) for a, b in ((k_hbm, k), (v_hbm, v), (do_hbm, do), (o_hbm, o))]
            + [load(qa_hbm.at[pl.ds(2 * p, 2)], qa.at[pl.ds(2 * p, 2)])]
        )
    part_load = load(down_part_hbm, down_part)
    up_load = load(gup_hbm, gup)
    gp_load = load(gp_own_hbm, gp_src)
    low_load = load(low_hbm, low)
    greet([peer] + wide_peers(me, wide))
    gp_swap = remote(gp_other_hbm, gp_got, narrow, 0, peer)
    layer = remote(lo_send, lo_got, narrow, 1, peer)
    gp_swap.start()
    late = [
        load(w_hbm.at[c, :, pl.ds(p * pair_w, pair_w)], wp.at[p, :, pl.ds(c * pair_w, pair_w)])
        for p in range(pairs)
        for c in range(3)
    ]
    own_half = block_rows(n * half, half)
    late += [load(xf_hbm.at[own_half], xf), load(gm_hbm, gm)]

    at = iter(range(0, 64 * steps, 2 * steps))
    opening = iter(range(32))

    def group(src, box, part, own, dst, entry=0, cut=True):
        rows_, cols_ = dst.shape
        parts = lanes_split(cols_) if cut else [(0, pl.ds(0, cols_))]
        chains = []
        for kind, cols in parts:
            chain = Chain(me, order_of(wide, kind), rows_, cols, across, next(at))
            chains.append(chain.bind(src, box, part, own, dst, entry))
        first = [next(opening) for _ in chains][0]
        return Group(chains, open_sem, first, entry)

    down = group(down_part, down_box, down_part2, down_own, down_out, entry=2)
    up = group(gup, up_box, up_part, up_own, up_out)
    proj = group(gp_src, gp_box, gp_part, gp_own, gp_out, cut=False)
    qkv = [
        group(gpair.at[p], pair_box.at[p], pair_part.at[p], pair_own.at[p], out, cut=False)
        for p, out in zip(range(pairs), (g0_out, g1_out, g2_out))
    ]

    def tick(name, *groups):
        with scope(name):
            for g in groups:
                g.tick()

    part_load.wait()
    down.tick()
    up_load.wait()
    up.tick()

    kpos = lax.broadcasted_iota(jnp.int32, (rows, 1), 0)
    kbias = jnp.where(kpos < len_ref[0], 0.0, -1e30)
    tri = lax.broadcasted_iota(jnp.int32, (bq, bq), 0) <= lax.broadcasted_iota(jnp.int32, (bq, bq), 1)

    def plan(name, *groups):
        ticks = [g.next() for g in groups]

        def run():
            with scope(name):
                for one in ticks:
                    one()

        return run

    def start_proj(first):
        gp_swap.wait()
        gp_load.wait()
        gp_src[...] = gp_src[...] + gp_got[...]
        first()

    hooks = {
        (0, 1): [plan("t0", up)],
        (1, 1): [plan("t1", down, qkv[0])],
        (2, 1): [plan("t2", down, qkv[0]), layer.start],
        (3, 0): [plan("t3a", up)],
        (3, 1): [plan("t3", down, *qkv[:2]), functools.partial(start_proj, proj.next())],
        (4, 1): [plan("t4", up, down, *qkv[:2], proj)],
        (5, 1): [plan("t5", up, *qkv[:3], proj)],
    }

    def run_hooks(head, place_):
        for (h, where), actions in hooks.items():
            if where == place_:

                @pl.when(head == h)
                def _():
                    for action in actions:
                        action()

    def one_head(head, carry):
        par, pair = head % 2, head // 2
        lane, mine, extra = lanes_of(par)
        cols = lane_part(pair, pair_w)
        for p in range(pairs):

            @pl.when(head == 2 * p)
            def _():
                for copy in pair_loads[p]:
                    copy.wait()

        ka[...] = place(lane, mine, extra, k[:, cols].astype(F32), [kbias, -1.0, -1.0, -1.0]).astype(BF16)
        va[...] = place(lane, mine, extra, v[:, cols].astype(F32), [-1.0, -1.0, -1.0]).astype(BF16)
        dk_acc[...] = jnp.zeros_like(dk_acc)
        dv_acc[...] = jnp.zeros_like(dv_acc)

        def put(c, r, new):
            lanes = pl.ds(c * pair_w, pair_w)
            old = dqkv[pair, r, lanes].astype(F32)
            dqkv[pair, r, lanes] = jnp.where(mine, new, jnp.where(par == 0, 0.0, old)).astype(BF16)

        for i in range(rows // bq):
            r = pl.ds(i * bq, bq)
            qb = qa[head, r, :]
            df = do[r, cols].astype(F32)
            delta = jnp.sum(jnp.where(mine, df * o[r, cols].astype(F32), 0.0), axis=1, keepdims=True)
            db = place(lane, mine, extra, df, three(delta)).astype(BF16)
            dqs = None
            for j in range(i + 1):
                c = pl.ds(j * bq, bq)
                kb, vb = ka[c, :], va[c, :]
                s = dot_nt(kb, qb)
                if j == i:
                    s = jnp.where(tri, s, -1e30)
                p = jnp.exp(s)
                ds = (p * dot_nt(vb, db)).astype(BF16)
                dv_acc[c, :] += dot(p.astype(BF16), db)
                dk_acc[c, :] += dot(ds, qb)
                part = dot_tn(ds, kb)
                dqs = part if dqs is None else dqs + part
            put(0, r, dqs * HEAD**-0.5)
            if i == rows // bq - 2:
                run_hooks(head, 0)
        put(1, pl.ds(0, rows), dk_acc[...])
        put(2, pl.ds(0, rows), dv_acc[...])

        @pl.when(head == 1)
        def _():
            low_load.wait()

        @pl.when(par == 1)
        def _():
            with scope("weights"):
                gpair[pair] = dot_tn(low[...], dqkv[pair]).astype(BF16)

        run_hooks(head, 1)
        return carry

    lax.fori_loop(0, heads, one_head, 0)

    for copy in late:
        copy.wait()

    def gn_part(start):
        r = block_rows(start, block)
        total = dot_nt(dqkv[0, r, :], wp[0])
        for p in range(1, pairs):
            total += dot_nt(dqkv[p, r, :], wp[p])
        return total

    def gn_copy(j):
        r = pl.ds(j * block, block)
        return remote(gn_send.at[r], gn_got.at[r], narrow, 2 + j, peer)

    for j in range(each):
        gn_send[j * block : (j + 1) * block, :] = gn_part((1 - n) * half + j * block).astype(BF16)
        gn_copy(j).start()
        tick(f"p{j}", *qkv[::-1], proj)
    for j in range(each):
        gn_own[j * block : (j + 1) * block, :] = gn_part(n * half + j * block)
    tick("q0", up, down)

    sums[...] = jnp.zeros_like(sums)

    def put_sum(start, value):
        for i in range(value.shape[1] // 128):
            sums[start + i : start + i + 1, :] = value[:, i * 128 : (i + 1) * 128]

    dr, fr, lr = d // 128, s_ub.shape[1] // 128, lw // 128
    shared = -(-6 * dr // 8) * 8
    put_sum(2 * dr, s_g2[...])
    put_sum(3 * dr, s_s2[...])
    put_sum(4 * dr, s_pb[...])
    put_sum(5 * dr, s_db[...])
    put_sum(shared, s_ub[...])
    for p in range(pairs):
        put_sum(shared + fr + p, jnp.sum(dqkv[p, :, 0:pair_w].astype(F32), axis=0, keepdims=True))
        put_sum(shared + fr + lr + p, jnp.sum(dqkv[p, :, 2 * pair_w :].astype(F32), axis=0, keepdims=True))
    tick("q1", *qkv[::-1], proj)

    mine, other = lane_part(n, cw), lane_part(1 - n, cw)
    g1 = s1 = 0.0

    def ig_copy(j):
        r = block_rows(n * half + j * block, block)
        return remote(ig_send.at[pl.ds(j * block, block)], ig.at[r], narrow, 2 + each + j, peer)

    for j in range(each):
        with scope("gn_wait"):
            gn_copy(j).wait()
        rh = pl.ds(j * block, block)
        r = block_rows(n * half + j * block, block)
        g = gn_own[rh, :] + gn_got[rh, :].astype(F32)
        xhat, scale = norm_rows(xf[rh, :].astype(F32))
        gg = g * vec(gain)
        m1 = jnp.mean(gg, axis=-1, keepdims=True)
        m2 = jnp.mean(gg * xhat, axis=-1, keepdims=True)
        ig_own[...] = gm[rh, :] + scale * (gg - m1 - xhat * m2)
        ig_send[rh, :] = ig_own[:, other].astype(BF16)
        ig_copy(j).start()
        ig[r, :] = ig_own[:, mine].astype(BF16)
        g1 += jnp.sum(g * xhat, axis=0, keepdims=True)
        s1 += jnp.sum(g, axis=0, keepdims=True)
        tick(f"r{j}", *qkv[::-1], proj, up, down)
    put_sum(0, g1)
    put_sum(dr, s1)

    def vec_copy(step):
        if step == 0:
            top = pl.ds(0, shared)
            return remote(sums.at[top], sums_box.at[0, top], narrow, 2 + 2 * each, peer)
        slot = 2 * steps * 32 + step - 1
        return remote(sums, sums_box.at[step], across, slot, {"wide": flip(me, step - 1)})

    def vec_end(step):
        vec_copy(step).wait()
        if step == 0:
            sums[0:shared, :] += sums_box[0, 0:shared, :]
        else:
            sums[...] += sums_box[step]
        if step < steps:
            vec_copy(step + 1).start()

    vec_copy(0).start()
    todo = [*qkv[::-1], proj, up, down]
    step = 0
    while step <= steps or not all(g.done for g in todo):
        tick(f"s{step}", *todo)
        if step <= steps:
            vec_end(step)
        step += 1
    small[...] = sums[...]
    with scope("end"):
        layer.wait()
        for j in range(each):
            ig_copy(j).wait()


def back_call(
    length, qa, k, v, do, o, low, w, xf, gm, gain, lo_send, gup, down_part, gp_own, gp_other,
    s_ub, s_db, s_g2, s_s2, s_pb, wide, bq=256,
):
    heads, rows, pair = qa.shape
    d, f, lw = gain.shape[0], gup.shape[1], k.shape[1]
    cw, half = d // 2, rows // 2
    block = min(256, half)
    each, steps, pairs = half // block, bits(wide), heads // 2
    sd, vm = jax.ShapeDtypeStruct, pltpu.VMEM
    shape = lambda r: Chain(0, order_of(wide, 0), r, None, None, 0)
    c_down, c_up, c_gp = shape(f), shape(d), shape(2 * lw)
    vec_rows = -(-6 * d // 1024) * 8 + -(-(f + 2 * lw) // 1024) * 8
    work = 2 * heads * rows * rows * HEAD
    return pl.pallas_call(
        functools.partial(back_body, bq=bq, wide=wide),
        out_shape=(sd((rows, cw), BF16), sd((f, d), BF16), sd((d, f), BF16), sd((2 * lw, cw), BF16))
        + (sd((d, 3 * pair), BF16),) * 3 + (sd((rows, cw), BF16), sd((vec_rows, 128), F32)),
        in_specs=[pl.BlockSpec(memory_space=pltpu.SMEM)] + [anywhere()] * 9 + [vmem()] + [anywhere()] * 5 + [vmem()] * 5,
        out_specs=(anywhere(),) * 7 + (vmem(), vmem()),
        scratch_shapes=[
            vm(qa.shape, BF16), vm((rows, lw), BF16), vm((rows, lw), BF16), vm((rows, lw), BF16), vm((rows, lw), BF16),
            vm((rows, d), BF16), vm((pairs, d, 3 * pair), BF16), vm((half, d), BF16), vm((half, d), F32),
            vm((d, f), BF16), vm((f // 2, d), BF16), vm((2 * lw, cw), BF16), vm((2 * lw, cw), BF16),
            vm((rows, pair), BF16), vm((rows, pair), BF16), vm((rows, pair), F32), vm((rows, pair), F32),
            vm((pairs, rows, 3 * pair), BF16), vm((pairs, d, 3 * pair), BF16),
            vm((c_down.box_rows, d), BF16), vm((f // 2, d), BF16), vm((c_down.size, d), BF16),
            vm((c_up.box_rows, f), BF16), vm((d // 2, f), BF16), vm((c_up.size, f), BF16),
            vm((c_gp.box_rows, cw), BF16), vm((lw, cw), BF16), vm((c_gp.size, cw), BF16),
            vm((pairs, c_up.box_rows, 3 * pair), BF16), vm((pairs, d // 2, 3 * pair), BF16),
            vm((pairs, c_up.size, 3 * pair), BF16),
            vm((half, d), BF16), vm((half, d), BF16), vm((half, d), F32), vm((block, d), F32), vm((half, cw), BF16),
            vm((vec_rows, 128), F32), vm((steps + 1, vec_rows, 128), F32),
        ]
        + sems(64, 32, 3 + 2 * each, 3 + 2 * each, 65 * steps, 65 * steps),
        compiler_params=params(collective_id=4, has_side_effects=True),
        cost_estimate=cost(10 * work + 4 * rows * d * 3 * lw, 2 * rows * d * 20, work // 256),
        name="back",
    )(
        length, qa, k, v, do, o, low, w, xf, gm, gain, lo_send, gup, down_part, gp_own, gp_other,
        s_ub, s_db, s_g2, s_s2, s_pb,
    )


def finish_body(
    lo, lo_got, bias, ig, up, down, q, k, v, p0, p1, small,
    out, ig_out, o_qkv, o_qvb, o_proj, o_pb, o_up, o_ub, o_down, o_db, o_g1, o_s1, o_g2, o_s2,
    *, factor, dr, shared,
):
    n = lax.axis_index("narrow")
    cw = lo.shape[1]
    out[...] = (lo[...] + lo_got[...].astype(F32) + bias[:, lane_part(n, cw)]).astype(BF16)
    ig_out[...] = ig[...]
    for p, ref in enumerate((q, k, v)):
        for c in range(3):
            lanes = slice(c * 128, (c + 1) * 128)
            o_qkv[c, :, p * 128 : (p + 1) * 128] = ref[:, lanes].astype(F32) * factor
    o_proj[:, :cw] = p0[...].astype(F32) * factor
    o_proj[:, cw:] = p1[...].astype(F32) * factor
    o_up[...] = up[...].astype(F32) * factor
    o_down[...] = down[...].astype(F32) * factor

    @pl.when(pl.program_id(0) == 0)
    def _():
        for i, ref in enumerate((o_g1, o_s1, o_g2, o_s2, o_pb, o_db)):
            ref[...] = small[i * dr : (i + 1) * dr, :] * factor
        fr = o_ub.shape[0]
        o_ub[...] = small[shared : shared + fr, :] * factor
        lr = o_qvb.shape[1] // 128
        for c in range(2):
            for i in range(lr):
                at = shared + fr + c * lr + i
                o_qvb[c : c + 1, i * 128 : (i + 1) * 128] = small[at : at + 1, :] * factor


def finish_call(lo, lo_got, bias, ig, up, down, q, k, v, p, small, factor, grid=8):
    rows, cw = lo.shape
    (d, f), lw = up.shape, q.shape[1]
    dr, shared = d // 128, -(-6 * d // 1024) * 8
    sd = jax.ShapeDtypeStruct
    tiny = [sd((dr, 128), F32)] * 2
    shapes = (
        [sd((rows, cw), BF16), sd((rows, cw), BF16), sd((3, d, lw), F32), sd((2, lw), F32), sd((lw, d), F32)]
        + [sd((dr, 128), F32), sd((d, f), F32), sd((f // 128, 128), F32), sd((f, d), F32)]
        + [sd((dr, 128), F32)] * 5
    )
    big = lambda a: rows_spec(a.shape[0] // grid, a.shape[1])
    pb = lw // grid
    specs = []
    for i, s in enumerate(shapes):
        if len(s.shape) == 3:
            specs.append(pl.BlockSpec((3, d // grid, lw), lambda i, *_: (0, i, 0)))
        elif i in (0, 1, 4, 6, 8):
            specs.append(big(s))
        else:
            specs.append(whole_spec(s.shape))
    return pl.pallas_call(
        functools.partial(finish_body, factor=factor, dr=dr, shared=shared),
        out_shape=tuple(shapes),
        grid=(grid,),
        in_specs=[big(lo), big(lo_got), whole_spec(bias.shape), big(ig), big(up), big(down), big(q), big(k), big(v)]
        + [rows_spec(pb, cw), rows_spec(pb, cw, grid), whole_spec(small.shape)],
        out_specs=tuple(specs),
        compiler_params=params(),
        cost_estimate=cost(up.size * 8, up.size * 24),
        name="finish",
    )(lo, lo_got, bias, ig, up, down, q, k, v, p, p, small)


def on_device(
    tokens, lengths, qkv_weight, qv_bias, proj_weight, proj_bias, up_weight, up_bias,
    down_weight, down_bias, first_gain, first_shift, second_gain, second_shift, cotangent,
):
    cw = tokens.shape[1]
    d, ff, lw = 2 * cw, up_weight.shape[1], proj_weight.shape[0]
    wide = lax.axis_size("wide")
    w3 = jnp.transpose(qkv_weight, (1, 0, 2))

    xf, low, q, k, v = qkv_call(tokens, w3, qv_bias, first_gain, first_shift)
    mixed, qa, mixed_got, proj_got = attend_forward(lengths, q, k, v, proj_weight)
    lo, lo_send, gmix, gm, gup, down_part, gp_own, gp_other, s_ub, s_db, s_g2, s_s2, s_pb = mlp_call(
        lengths, xf, mixed, mixed_got, proj_weight, proj_got, proj_bias, second_gain, second_shift,
        up_weight, up_bias, down_weight, cotangent, wide,
    )
    lo_got, gdown, gup, gp, g0, g1, g2, ig, small = back_call(
        lengths, qa, k, v, gmix, mixed, low, w3, xf, gm, first_gain, lo_send, gup, down_part, gp_own, gp_other,
        s_ub, s_db, s_g2, s_s2, s_pb, wide,
    )
    out, ig, o_qkv, o_qvb, o_proj, *rest = finish_call(
        lo, lo_got, down_bias.astype(F32).reshape(1, -1), ig, gup, gdown, g0, g1, g2, gp, small,
        1.0 / (lengths.shape[0] * wide),
    )
    pb, up, ubs, down, dbs, g1, s1, g2, s2 = rest
    flat = lambda a: a.reshape(-1)
    return (
        out, ig, jnp.transpose(o_qkv, (1, 0, 2)), o_qvb, o_proj, flat(pb), up, flat(ubs), down, flat(dbs),
        flat(g1), flat(s1), flat(g2), flat(s2),
    )


def solution(mesh):
    split = P("wide", "narrow")
    none3, cols, rows1 = P(None, None, "narrow"), P(None, "narrow"), P("narrow", None)
    return jax.shard_map(
        on_device,
        mesh=mesh,
        in_specs=(
            split, P("wide"), none3, cols, rows1, P(), cols, P("narrow"), rows1, P(), P(), P(), P(), P(), split,
        ),
        out_specs=(
            split, split, none3, cols, rows1, P(), cols, P("narrow"), rows1, P(), P(), P(), P(), P(),
        ),
        check_vma=False,
    )
```

time: 235 us -> 237 us (level)
    pallas_call x2 -> x1, Pallas kernels: 111 us -> 119 us  [back_call(): pl.pallas_call(functools.partial(back_body, bq=bq, wide=wide), out_shape=...]
    pallas_call x1, Pallas kernels: 56.7 us -> 50.4 us  [mlp_call(): pl.pallas_call(functools.partial(mlp_body, wide=wide), out_shape=(sd((row...]
where the time goes in v5:
time: 237 us; the launch traced here: 236 us
  Pallas kernels  234 us (99%)
    pallas_call x1, Pallas kernels, back_call(): pl.pallas_call(functools.partial(back_body, bq=bq, wide=wide), out_shape=...  119 us
    pallas_call x1, Pallas kernels, mlp_call(): pl.pallas_call(functools.partial(mlp_body, wide=wide), out_shape=(sd((row...  50.4 us
    pallas_call x1, Pallas kernels, attend_forward(): pl.pallas_call(functools.partial(fwd_body, bq=bq), out_shape=(sd((rows, w...  28.8 us
    pallas_call x1, Pallas kernels, qkv_call(): pl.pallas_call(qkv_body, out_shape=(sd((rows, d), BF16), sd((rows, d), BF...  24.2 us
    pallas_call x1, Pallas kernels, finish_call(): pl.pallas_call(functools.partial(finish_body, factor=factor, dr=dr, share...  10.9 us

profile of v5, /device:TPU:0, one launch (start us, length us, event | category | flops | bytes accessed | tf_op | source)
XLA Modules:
  0.0 236.4 jit_solution(12331721088452134068)
XLA Ops:
  1.3 1.3 reshape.64.bias
  2.6 24.2 %norm_qkv.1 = (bf16[1024,768]{1,0:T(8,128)(2,1)}, bf16[1024,768]{1,0:T(8,128)(2,1)}, bf16[1024,384]{1,0:T(8,128)(2,1)}, bf16[1024,384]{1,0:T(8,128)(2,1)}, bf16[1024,384]{1,0:T(8,128)(2,1)}) custom-call(bf16[1024,384]{1,0:T(8,128)(2,1)} %own.1, bf16[1024,384]{1,0:T(8,128)(2,1)} %own.1, bf16[3,768,384]{2,1,0:T(8,128)(2,1)} %bitcast.10, bf16[2,384]{1,0:T(2,128)(2,1)} %bias.1, ...), custom_call_target="tpu_custom_call" | custom-call | flops 1811939328 | bytes 9633792 | tf_op jit(solution)/shard_map/norm_qkv/pallas_call | solution.py:270
  26.7 28.8 %attend_fwd.1 = (bf16[1024,384]{1,0:T(8,128)(2,1)}, bf16[6,1024,128]{2,1,0:T(8,128)(2,1)}, bf16[1024,384]{1,0:T(8,128)(2,1)}, bf16[384,768]{1,0:T(8,128)(2,1)}) custom-call(s32[1]{0:T(128)S(6)} %copy.29.len_ref, bf16[1024,384]{1,0:T(8,128)(2,1)} %get-tuple-element.60.q, bf16[1024,384]{1,0:T(8,128)(2,1)} %get-tuple-element.61.k.k_hbm, ...), custom_call_target="tpu_custom_call" | custom-call | flops 3221225472 | bytes 4718592 | tf_op jit(solution)/shard_map/attend_fwd/pallas_call | solution.py:380
  55.6 50.4 %mlp.1 = (f32[1024,384]{1,0:T(8,128)}, bf16[1024,384]{1,0:T(8,128)(2,1)}, bf16[1024,384]{1,0:T(8,128)(2,1)}, f32[512,768]{1,0:T(8,128)}, bf16[768,1536]{1,0:T(8,...) custom-call(s32[1]{0:T(128)S(6)} %copy.29.len_ref, ...), custom_call_target="tpu_custom_call" | custom-call | flops 15703474176 | bytes 17301504 | tf_op jit(solution)/shard_map/mlp/pallas_call | solution.py:604
  106.0 119.3 %back.1 = (bf16[1024,384]{1,0:T(8,128)(2,1)}, bf16[1536,768]{1,0:T(8,128)(2,1)}, bf16[768,1536]{1,0:T(8,128)(2,1)}, bf16[768,384]{1,0:T(8,128)(2,1)}, bf16[768,3...) custom-call(s32[1]{0:T(128)S(6)} %copy.29.len_ref, ...), custom_call_target="tpu_custom_call" | custom-call | flops 11676942336 | bytes 31457280 | tf_op jit(solution)/shard_map/back/pallas_call | solution.py:921
  225.3 10.9 %finish.1 = (bf16[1024,384]{1,0:T(8,128)(2,1)}, bf16[1024,384]{1,0:T(8,128)(2,1)}, f32[3,768,384]{2,1,0:T(8,128)}, f32[2,384]{1,0:T(2,128)}, f32[384,768]{1,0:T(...) custom-call(f32[1024,384]{1,0:T(8,128)} %get-tuple-element.66.lo, ...), custom_call_target="tpu_custom_call" | custom-call | flops 9437184 | bytes 28311552 | tf_op jit(solution)/shard_map/finish/pallas_call | solution.py:1003

commit v6 on v5

--- a/solution.py
+++ b/solution.py
@@ -91,85 +91,205 @@
     return pl.ds(start if isinstance(start, int) else pl.multiple_of(start, unit), size)
 
 
+LINE = 4
+
+
+def when(cond, action):
+    @pl.when(cond)
+    def _():
+        action()
+
+
+def line_peer(me, by):
+    q = (me // 4) % LINE
+    return me + ((q + by) % LINE - q) * 4
+
+
 class Chain:
     def __init__(self, me, order, rows, cols, sems, at):
         self.me, self.cols, self.sems, self.at = me, cols, sems, at
-        self.steps, self.splits = [], []
+        self.phases, self.ops, back = [], [], []
         base, size, box = 0, rows, 0
-        for bit in order:
-            if size % 32 == 0:
-                half = size // 2
+        for kind, bit in order:
+            if kind == "line" and size % (16 * LINE):
+                raise ValueError(rows)
+            if kind == "line":
+                part = size // LINE
+                keep, give, boxes = base + (me // 4) % LINE * part, None, 2 * (LINE - 1) * part
+                self.ops += [("line", len(self.phases), i) for i in range(1, LINE)]
+                back = [("spread", len(self.phases), i) for i in range(1, LINE)] + back
+            elif size % 32 == 0:
+                part = size // 2
                 mine = bit_of(me, bit)
-                keep, give = base + mine * half, base + (1 - mine) * half
-                self.splits.append((bit, keep, half))
+                keep, give, boxes = base + mine * part, base + (1 - mine) * part, part
+                self.ops.append(("pair", len(self.phases), 0))
+                back = [("join", len(self.phases), 0)] + back
             else:
-                half, keep, give = size, base, base
-            self.steps.append((bit, keep, give, half, box))
-            base, size, box = keep, half, box + half
+                part, keep, give, boxes = size, base, base, size
+                self.ops.append(("pair", len(self.phases), 0))
+            self.phases.append((bit, base, keep, give, part, box))
+            base, size, box = keep, part, box + boxes
+        self.scatters = len(self.ops)
+        self.ops += back
         self.base, self.size, self.box_rows = base, size, box
 
     def bind(self, src, box, part, own, dst=None, entry=0):
-        self.src, self.box, self.part, self.own, self.dst, self.entry = src, box, part, own, dst, entry
+        self.src, self.box, self.part, self.own, self.dst = src, box, part, own, dst
+        self.entry = self.ops[entry][1]
         return self
 
-    def _source(self, step):
-        off = 0 if step == 0 else self.steps[0][1]
-        return (self.src if step == self.entry else self.part), off
-
-    def _scatter_copy(self, step):
-        bit, _, give, half, box = self.steps[step]
-        source, off = self._source(step)
-        return remote(
-            source.at[block_rows(give - off, half), self.cols],
-            self.box.at[pl.ds(box, half), self.cols],
-            self.sems, self.at + step, {"wide": flip(self.me, bit)},
-        )
-
-    def scatter_start(self, step):
-        self._scatter_copy(step).start()
-
-    def scatter_end(self, step):
-        self._scatter_copy(step).wait()
-        _, keep, _, half, box = self.steps[step]
-        source, off = self._source(step)
-        last = step == len(self.steps) - 1
-        target, out = (self.own, keep) if last else (self.part, self.steps[0][1])
-        unit = next(u for u in (96, 64, 48, 32, 16) if half % u == 0)
+    def _source(self, phase):
+        off = 0 if phase == 0 else self.phases[0][2]
+        return (self.src if phase == self.entry else self.part), off
+
+    def _target(self, phase):
+        if phase == len(self.phases) - 1:
+            return self.own, self.phases[phase][2]
+        return self.part, self.phases[0][2]
+
+    def _remote(self, op, lane, src, dst, to):
+        return remote(src, dst, self.sems, self.at + 2 * op + lane, {"wide": to})
+
+    def _add(self, rows, target, first, *terms):
+        unit = next(u for u in (96, 64, 48, 32, 16) if rows % u == 0)
 
         def add(i, carry):
-            at = i * unit
-            got = self.box[block_rows(box + at, unit), self.cols]
-            mine = source[block_rows(keep - off + at, unit), self.cols]
-            target[block_rows(keep - out + at, unit), self.cols] = got + mine
+            total = None
+            for ref, start in terms:
+                value = ref[block_rows(start + i * unit, unit), self.cols]
+                total = value if total is None else total + value
+            target[block_rows(first + i * unit, unit), self.cols] = total
             return carry
 
-        lax.fori_loop(0, half // unit, add, 0)
+        lax.fori_loop(0, rows // unit, add, 0)
+
+
+    def _pair(self, op, phase):
+        bit, _, _, give, rows, box = self.phases[phase]
+        source, off = self._source(phase)
+        src = source.at[block_rows(give - off, rows), self.cols]
+        return self._remote(op, 0, src, self.box.at[pl.ds(box, rows), self.cols], flip(self.me, bit))
+
+    def _join(self, op, phase):
+        bit, _, keep, _, rows, _ = self.phases[phase]
+        region = self.dst.at[block_rows(keep, rows), self.cols]
+        return self._remote(op, 0, region, region, flip(self.me, bit))
+
+
+    def _slot(self, phase, lane, i):
+        rows, box = self.phases[phase][4:]
+        return box + (lane * (LINE - 1) + i - 1) * rows
+
+    def _line_sends(self, op, phase, i):
+        q = (self.me // 4) % LINE
+        _, base, _, _, rows, _ = self.phases[phase]
+        source, off = self._source(phase)
+        sends = []
+        for lane, by in ((0, 1), (1, -1)):
+            place_ = q if lane == 0 else LINE - 1 - q
+            chunk = LINE - i if lane == 0 else i - 1
+            dst = self.box.at[pl.ds(self._slot(phase, lane, i), rows), self.cols]
+            to = line_peer(self.me, by)
+            src = source.at[block_rows(base - off + chunk * rows, rows), self.cols]
+            sends.append((place_ == 0, functools.partial(self._remote, op, lane, src, dst, to)))
+            if i > 1:
+                src = self.box.at[pl.ds(self._slot(phase, lane, i - 1), rows), self.cols]
+                moving = jnp.logical_and(place_ >= 1, place_ <= min(i - 1, LINE - 2))
+                sends.append((moving, functools.partial(self._remote, op, lane, src, dst, to)))
+        return sends
+
+    def _line_end(self, op, phase, i):
+        q = (self.me // 4) % LINE
+        _, base, keep, _, rows, _ = self.phases[phase]
+        source, off = self._source(phase)
+        for cond, copy in self._line_sends(op, phase, i):
+            when(cond, lambda: copy().wait_send())
+        for lane, by in ((0, -1), (1, 1)):
+            place_ = q if lane == 0 else LINE - 1 - q
+            slot = self._slot(phase, lane, i)
+            dst = self.box.at[pl.ds(slot, rows), self.cols]
+            arrived = jnp.logical_and(place_ >= 1, place_ <= i)
+            chunk = LINE - 1 - i + q if lane == 0 else i + q - (LINE - 1)
+
+            @pl.when(arrived)
+            def _():
+                self._remote(op, lane, dst, dst, line_peer(self.me, by)).wait_recv()
+                if i < LINE - 1:
+                    self._add(rows, self.box, slot, (self.box, slot), (source, base - off + chunk * rows))
+
+        if i == LINE - 1:
+            target, out = self._target(phase)
+            own = (source, keep - off)
+            left, right = (self.box, self._slot(phase, 0, i)), (self.box, self._slot(phase, 1, i))
+
+            @pl.when(q == 0)
+            def _():
+                self._add(rows, target, keep - out, own, right)
+
+            @pl.when(q == LINE - 1)
+            def _():
+                self._add(rows, target, keep - out, own, left)
+
+            @pl.when(jnp.logical_and(q > 0, q < LINE - 1))
+            def _():
+                self._add(rows, target, keep - out, left, own, right)
+
+    def _spread(self, op, phase, i):
+        q = (self.me // 4) % LINE
+        _, base, _, _, rows, _ = self.phases[phase]
+        ways = []
+        for lane, by in ((0, 1), (1, -1)):
+            place_ = q if lane == 0 else LINE - 1 - q
+            sent = self.dst.at[block_rows(base + (q - by * (i - 1)) * rows, rows), self.cols]
+            came = self.dst.at[block_rows(base + (q - by * i) * rows, rows), self.cols]
+            send_if = jnp.logical_and(place_ >= i - 1, place_ <= LINE - 2)
+            ways.append(
+                (
+                    send_if, functools.partial(self._remote, op, lane, sent, sent, line_peer(self.me, by)),
+                    place_ >= i, functools.partial(self._remote, op, lane, came, came, line_peer(self.me, -by)),
+                )
+            )
+        return ways
+
+    def start(self, op):
+        kind, phase, i = self.ops[op]
+        if kind == "pair":
+            self._pair(op, phase).start()
+        elif kind == "join":
+            self._join(op, phase).start()
+        elif kind == "line":
+            for cond, copy in self._line_sends(op, phase, i):
+                when(cond, lambda: copy().start())
+        else:
+            for cond, copy, _, _ in self._spread(op, phase, i):
+                when(cond, lambda: copy().start())
+
+    def end(self, op):
+        kind, phase, i = self.ops[op]
+        if kind == "pair":
+            self._pair(op, phase).wait()
+            _, _, keep, _, rows, box = self.phases[phase]
+            source, off = self._source(phase)
+            target, out = self._target(phase)
+            self._add(rows, target, keep - out, (self.box, box), (source, keep - off))
+        elif kind == "join":
+            self._join(op, phase).wait()
+        elif kind == "line":
+            self._line_end(op, phase, i)
+        else:
+            for send_if, send, recv_if, recv in self._spread(op, phase, i):
+                when(send_if, lambda: send().wait_send())
+                when(recv_if, lambda: recv().wait_recv())
 
     def gather_open(self, sem):
         region = self.dst.at[block_rows(self.base, self.size), self.cols]
         return pltpu.make_async_copy(self.own.at[:, self.cols], region, sem)
 
-    def _gather_copy(self, step):
-        bit, keep, half = self.splits[len(self.splits) - 1 - step]
-        region = self.dst.at[block_rows(keep, half), self.cols]
-        at = self.at + len(self.steps) + step
-        return remote(region, region, self.sems, at, {"wide": flip(self.me, bit)})
-
-    def gather_start(self, step):
-        self._gather_copy(step).start()
-
-    def gather_end(self, step):
-        self._gather_copy(step).wait()
-
 
 class Group:
-    def __init__(self, chains, open_sem=None, at=0, entry=0, leave=None):
-        self.chains, self.open_sem, self.at = chains, open_sem, at
-        steps, splits = len(chains[0].steps), len(chains[0].splits)
-        self.last = steps
-        self.ops = [("scatter", i) for i in range(entry, steps if leave is None else leave)]
-        if leave is None:
-            self.ops += [("gather", i) for i in range(splits)]
+    def __init__(self, chain, open_sem=None, at=0, entry=0, leave=None):
+        self.chain, self.open_sem, self.at = chain, open_sem, at
+        self.ops = list(range(entry, len(chain.ops) if leave is None else leave))
         self.pos = -1
 
     @property
@@ -184,20 +304,14 @@
             if pos >= len(self.ops):
                 return
             if pos >= 0:
-                kind, i = self.ops[pos]
-                for chain in self.chains:
-                    (chain.scatter_end if kind == "scatter" else chain.gather_end)(i)
+                self.chain.end(self.ops[pos])
             if pos + 1 >= len(self.ops):
                 return
-            kind, i = self.ops[pos + 1]
-            if kind == "gather" and i == 0:
-                opens = [c.gather_open(self.open_sem.at[self.at + j]) for j, c in enumerate(self.chains)]
-                for opened in opens:
-                    opened.start()
-                for opened in opens:
-                    opened.wait()
-            for chain in self.chains:
-                (chain.scatter_start if kind == "scatter" else chain.gather_start)(i)
+            if self.ops[pos + 1] == self.chain.scatters:
+                opened = self.chain.gather_open(self.open_sem.at[self.at])
+                opened.start()
+                opened.wait()
+            self.chain.start(self.ops[pos + 1])
 
         return tick
 
@@ -210,17 +324,18 @@
 
 
 def order_of(wide, kind):
-    steps = list(range(bits(wide)))
-    return steps if kind == 0 else [0] + steps[2:] + steps[1:2]
+    first, rest = ("pair", 0), [("pair", b) for b in range(4, bits(wide))]
+    pair, line = ("pair", 1), ("line", 2)
+    return [first, pair, line, *rest] if kind == 0 else [first, line, pair, *rest]
 
 
 def lanes_split(cols):
-    w = max(128, cols // 6 // 128 * 128)
-    return [(0, pl.ds(0, cols - w)), (1, pl.ds(cols - w, w))]
+    return [(0, pl.ds(0, cols // 2)), (1, pl.ds(cols // 2, cols // 2))]
 
 
 def wide_peers(me, wide):
-    return [{"wide": flip(me, b)} for b in range(bits(wide))]
+    pairs = [flip(me, b) for b in range(bits(wide)) if b not in (2, 3)]
+    return [{"wide": peer} for peer in pairs + [line_peer(me, by) for by in range(1, LINE)]]
 
 
 def vmem():
@@ -395,11 +510,14 @@
     )(length, q, k, v, pw)
 
 
+DOWN_ENTRY, UP_ENTRY = (2, 1), (1, 1)
+
+
 def mlp_body(
     len_ref, xf_hbm, mo_hbm, mr_hbm, pwo_hbm, pwr_hbm, pb, gain, shift, ub, up_hbm, down_hbm, cot_hbm,
-    lo_out, lo_send_out, gmix, gm_out, gup_out, down_part, gp_own, gp_other, sum_ub, sum_db, sum_g, sum_s, sum_pb,
+    lo_out, lo_send_out, gmix, gm_out, up_part, down_part, gp_own, gp_other, sum_ub, sum_db, sum_g, sum_s, sum_pb,
     xf, mo, mr, pwo, pwr, up, down, cot, cot_got, cf, lo, lo_send, mid, second, active, slope, gh,
-    gs_send, gs_got, gs_own, gdown, gup, box, gm, glow, gmix_send, load_sem, store_sem, nsend, nrecv, wsend, wrecv,
+    gs_send, gs_got, gs_own, gdown, gup, box, up_box, gm, glow, gmix_send, load_sem, store_sem, nsend, nrecv, wsend, wrecv,
     *, wide,
 ):
     n, me = lax.axis_index("narrow"), lax.axis_index("wide")
@@ -487,26 +605,6 @@
         down_load.wait()
     with scope("fwd_peer"):
         every(1 - n, forward)
-    with scope("cot_wait"):
-        cot_load.wait()
-        for j in range(each):
-            cot_copy(n, j, 0).wait()
-
-    def gs_copy(j):
-        r = block_rows(j * block, block)
-        return remote(gs_send.at[r], gs_got.at[r], narrow, 2 * each + j, peer)
-
-    def for_peer(j, carry):
-        gs_send[block_rows(j * block, block), :] = backward((1 - n) * half + j * block).astype(BF16)
-        gs_copy(j).start()
-        return carry
-
-    def for_own(j, carry):
-        gs_own[block_rows(j * block, block), :] = backward(n * half + j * block)
-        return carry
-
-    with scope("for_peer"):
-        lax.fori_loop(0, each, for_peer, 0)
     for copy in rest:
         copy.wait()
     with scope("fwd_own"):
@@ -520,6 +618,26 @@
 
     store(lo, lo_out)
     store(lo_send, lo_send_out)
+    with scope("cot_wait"):
+        cot_load.wait()
+        for j in range(each):
+            cot_copy(n, j, 0).wait()
+
+    def gs_copy(j):
+        r = block_rows(j * block, block)
+        return remote(gs_send.at[r], gs_got.at[r], narrow, 2 * each + j, peer)
+
+    def for_peer(j, carry):
+        gs_send[block_rows(j * block, block), :] = backward((1 - n) * half + j * block).astype(BF16)
+        gs_copy(j).start()
+        return carry
+
+    def for_own(j, carry):
+        gs_own[block_rows(j * block, block), :] = backward(n * half + j * block)
+        return carry
+
+    with scope("for_peer"):
+        lax.fori_loop(0, each, for_peer, 0)
     with scope("cot_wait2"):
         for j in range(each):
             cot_copy(1 - n, j, 1).wait()
@@ -534,19 +652,29 @@
 
         lax.fori_loop(0, dst.shape[0] // 256, step, 0)
 
-    chains = []
-    for kind, cols in lanes_split(d):
-        chain = Chain(me, order_of(wide, kind), f, cols, across, len(chains) * bits(wide))
-        chains.append(chain.bind(gdown, box, down_part, None))
-    reduce_down = Group(chains, leave=2)
+    used = iter(range(0, 64, 4))
+
+    def group(src, box_, part, leaves):
+        parts = []
+        for (kind, cols), leave in zip(lanes_split(src.shape[1]), leaves):
+            chain = Chain(me, order_of(wide, kind), src.shape[0], cols, across, next(used))
+            parts.append(Group(chain.bind(src, box_, part, None), leave=leave))
+        return parts
+
+    reduce_down = group(gdown, box, down_part, DOWN_ENTRY)
+    reduce_up = group(gup, up_box, up_part, UP_ENTRY)
+
+    def advance(name, *groups):
+        with scope(name):
+            for one in groups:
+                one.tick()
+
     with scope("w_down"):
         weight(gdown, active, cf)
-    reduce_down.tick()
+    advance("core_d", *reduce_down)
     with scope("w_up"):
         weight(gup, second, gh)
-    store(gup, gup_out)
-    with scope("core"):
-        reduce_down.tick()
+    advance("core_u", *reduce_down, *reduce_up)
     with scope("gs_wait"):
         for j in range(each):
             gs_copy(j).wait()
@@ -579,6 +707,7 @@
     with scope("back_norm"):
         lax.fori_loop(0, each, back_norm, 0)
     store(gm, gm_out)
+    advance("across", *reduce_up)
     with scope("proj"):
         lw = mo.shape[1]
         for src, dst in ((mr, gp_other), (mo, gp_own)):
@@ -588,8 +717,7 @@
     with scope("gmix_wait"):
         for j in range(each):
             gmix_copy(j).wait()
-    with scope("across"):
-        reduce_down.tick()
+    advance("leave", *reduce_down, *reduce_up)
     with scope("store"):
         for copy in stores:
             copy.wait()
@@ -605,33 +733,65 @@
         functools.partial(mlp_body, wide=wide),
         out_shape=(
             sd((rows, cw), F32), sd((rows, cw), BF16), sd((rows, lw), BF16), sd((half, d), F32),
-            sd((d, f), BF16), sd((f // 2, d), BF16), sd((2 * lw, cw), BF16), sd((2 * lw, cw), BF16),
+            sd((d // 2, f), BF16), sd((f // 2, d), BF16), sd((2 * lw, cw), BF16), sd((2 * lw, cw), BF16),
             sd((1, f), F32), sd((1, d), F32), sd((1, d), F32), sd((1, d), F32), sd((1, d), F32),
         ),
         in_specs=[pl.BlockSpec(memory_space=pltpu.SMEM)] + [anywhere()] * 5 + [vmem()] * 4 + [anywhere()] * 3,
-        out_specs=(anywhere(), anywhere(), vmem(), anywhere(), anywhere()) + (vmem(),) * 8,
+        out_specs=(anywhere(), anywhere(), vmem(), anywhere()) + (vmem(),) * 9,
         scratch_shapes=[
             vm((rows, d), BF16), vm((rows, lw), BF16), vm((rows, lw), BF16), vm((lw, d), BF16), vm((lw, d), BF16),
             vm((d, f), BF16), vm((f, d), BF16), vm((rows, cw), BF16), vm((rows, cw), BF16), vm((rows, d), BF16),
             vm((rows, cw), F32), vm((rows, cw), BF16), vm((rows, d), F32),
             vm((rows, d), BF16), vm((rows, f), BF16), vm((rows, f), F32), vm((rows, f), BF16),
             vm((half, d), BF16), vm((half, d), BF16), vm((half, d), F32), vm((f, d), BF16), vm((d, f), BF16),
-            vm((f - f // 4, d), BF16), vm((half, d), F32), vm((half, d), BF16), vm((half, lw), BF16),
+            vm((f, d), BF16), vm((d, f), BF16), vm((half, d), F32), vm((half, d), BF16), vm((half, lw), BF16),
         ]
-        + sems(16, 4, 4 * each, 4 * each, 2 * bits(wide), 2 * bits(wide)),
+        + sems(16, 4, 4 * each, 4 * each, 16, 16),
         compiler_params=params(collective_id=3, has_side_effects=True),
         cost_estimate=cost(2 * rows * d * (d + 6 * f), 2 * (rows * d * 8 + 2 * d * f), rows * f),
         name="mlp",
     )(length, xf, mo, mr, pwo, pwr, pb, gain, shift, ub, up, down, cot)
 
 
+HEAD_TICKS = (
+    ((0, 3), "D0"),
+    ((1, 2), "D1"),
+    ((1, 3), "U0U1Q0"),
+    ((2, 0), "D0"),
+    ((2, 1), "Q0"),
+    ((2, 2), "D1"),
+    ((2, 3), "U0"),
+    ((3, 1), "Q0P0U1"),
+    ((3, 2), "D0"),
+    ((3, 3), "D1P0D0Q1"),
+    ((4, 0), "U0"),
+    ((4, 1), "Q0Q1"),
+    ((4, 2), "D1D0"),
+    ((4, 3), "U1P0"),
+    ((5, 0), "U0"),
+    ((5, 1), "Q0Q1D0P0D1"),
+    ((5, 2), "U0Q0U1Q1"),
+    ((5, 3), "D1Q1P0Q2"),
+)
+PART_TICKS = ("Q0Q2U0Q1U1D0", "D1", "Q0D0P0", "Q2U0Q1", "")
+LAST_TICKS = (
+    "Q2U1", "norm0", "D1Q2Q0P0U0Q1D1Q2", "U0U1Q0P0Q1", "norm1", "Q0Q2U1Q2",
+    "small", "P0U1", "small", "P0Q2Q1", "small", "Q1",
+    "small", "Q2", "small", "Q2",
+)
+
+
+def pieces(names):
+    return [names[i : i + 2] for i in range(0, len(names), 2)]
+
+
 def back_body(
-    len_ref, qa_hbm, k_hbm, v_hbm, do_hbm, o_hbm, low_hbm, w_hbm, xf_hbm, gm_hbm, gain, lo_send, gup_hbm,
+    len_ref, qa_hbm, k_hbm, v_hbm, do_hbm, o_hbm, low_hbm, w_hbm, xf_hbm, gm_hbm, gain, lo_send, up_part_hbm,
     down_part_hbm, gp_own_hbm, gp_other_hbm, s_ub, s_db, s_g2, s_s2, s_pb,
     lo_got, down_out, up_out, gp_out, g0_out, g1_out, g2_out, ig, small,
-    qa, k, v, do, o, low, wp, xf, gm, gup, down_part, gp_src, gp_got,
+    qa, k, v, do, o, low, wp, xf, gm, up_part, down_part, gp_src, gp_got,
     ka, va, dk_acc, dv_acc, dqkv, gpair,
-    down_box, down_part2, down_own, up_box, up_part, up_own, gp_box, gp_part, gp_own, pair_box, pair_part, pair_own,
+    down_box, down_part2, down_own, up_box, up_part2, up_own, gp_box, gp_part, gp_own, pair_box, pair_part, pair_own,
     gn_send, gn_got, gn_own, ig_own, ig_send, sums, sums_box,
     load_sem, open_sem, nsend, nrecv, wsend, wrecv, *, bq, wide,
 ):
@@ -661,7 +821,7 @@
             + [load(qa_hbm.at[pl.ds(2 * p, 2)], qa.at[pl.ds(2 * p, 2)])]
         )
     part_load = load(down_part_hbm, down_part)
-    up_load = load(gup_hbm, gup)
+    up_load = load(up_part_hbm, up_part)
     gp_load = load(gp_own_hbm, gp_src)
     low_load = load(low_hbm, low)
     greet([peer] + wide_peers(me, wide))
@@ -676,70 +836,70 @@
     own_half = block_rows(n * half, half)
     late += [load(xf_hbm.at[own_half], xf), load(gm_hbm, gm)]
 
-    at = iter(range(0, 64 * steps, 2 * steps))
+    stride = 2 * len(Chain(0, order_of(wide, 0), d, None, None, 0).ops)
+    at = iter(range(0, 64 * stride, stride))
     opening = iter(range(32))
 
-    def group(src, box, part, own, dst, entry=0, cut=True):
+    def group(src, box, part, own, dst, entries=(0,)):
         rows_, cols_ = dst.shape
-        parts = lanes_split(cols_) if cut else [(0, pl.ds(0, cols_))]
-        chains = []
-        for kind, cols in parts:
+        made = []
+        parts = lanes_split(cols_) if len(entries) == 2 else [(0, pl.ds(0, cols_))]
+        for (kind, cols), entry in zip(parts, entries):
             chain = Chain(me, order_of(wide, kind), rows_, cols, across, next(at))
-            chains.append(chain.bind(src, box, part, own, dst, entry))
-        first = [next(opening) for _ in chains][0]
-        return Group(chains, open_sem, first, entry)
-
-    down = group(down_part, down_box, down_part2, down_own, down_out, entry=2)
-    up = group(gup, up_box, up_part, up_own, up_out)
-    proj = group(gp_src, gp_box, gp_part, gp_own, gp_out, cut=False)
-    qkv = [
-        group(gpair.at[p], pair_box.at[p], pair_part.at[p], pair_own.at[p], out, cut=False)
-        for p, out in zip(range(pairs), (g0_out, g1_out, g2_out))
-    ]
-
-    def tick(name, *groups):
-        with scope(name):
-            for g in groups:
-                g.tick()
+            made.append(Group(chain.bind(src, box, part, own, dst, entry), open_sem, next(opening), entry))
+        return made
+
+    groups = {}
+    groups["D0"], groups["D1"] = group(down_part, down_box, down_part2, down_own, down_out, DOWN_ENTRY)
+    groups["U0"], groups["U1"] = group(up_part, up_box, up_part2, up_own, up_out, UP_ENTRY)
+    groups["P0"] = group(gp_src, gp_box, gp_part, gp_own, gp_out)[0]
+    for p, out in zip(range(pairs), (g0_out, g1_out, g2_out)):
+        groups[f"Q{p}"] = group(gpair.at[p], pair_box.at[p], pair_part.at[p], pair_own.at[p], out)[0]
+
+    def tick(names):
+        with scope(names):
+            for name in pieces(names):
+                groups[name].tick()
 
     part_load.wait()
-    down.tick()
+    tick("D0D1")
     up_load.wait()
-    up.tick()
+    tick("U0U1")
 
     kpos = lax.broadcasted_iota(jnp.int32, (rows, 1), 0)
     kbias = jnp.where(kpos < len_ref[0], 0.0, -1e30)
     tri = lax.broadcasted_iota(jnp.int32, (bq, bq), 0) <= lax.broadcasted_iota(jnp.int32, (bq, bq), 1)
 
-    def plan(name, *groups):
-        ticks = [g.next() for g in groups]
+    def plan(names):
+        ticks = [groups[name].next() for name in pieces(names)]
 
         def run():
-            with scope(name):
+            with scope(names):
                 for one in ticks:
                     one()
 
         return run
 
-    def start_proj(first):
-        gp_swap.wait()
-        gp_load.wait()
-        gp_src[...] = gp_src[...] + gp_got[...]
-        first()
-
-    hooks = {
-        (0, 1): [plan("t0", up)],
-        (1, 1): [plan("t1", down, qkv[0])],
-        (2, 1): [plan("t2", down, qkv[0]), layer.start],
-        (3, 0): [plan("t3a", up)],
-        (3, 1): [plan("t3", down, *qkv[:2]), functools.partial(start_proj, proj.next())],
-        (4, 1): [plan("t4", up, down, *qkv[:2], proj)],
-        (5, 1): [plan("t5", up, *qkv[:3], proj)],
-    }
-
-    def run_hooks(head, place_):
+    def start_proj():
+        first = groups["P0"].next()
+
+        def run():
+            gp_swap.wait()
+            gp_load.wait()
+            gp_src[...] = gp_src[...] + gp_got[...]
+            first()
+
+        return run
+
+    hooks = {}
+    for at_, names in HEAD_TICKS:
+        hooks[at_] = [plan(names)]
+        if at_ == (2, 3):
+            hooks[at_] += [layer.start, start_proj()]
+
+    def run_hooks(head, block_):
         for (h, where), actions in hooks.items():
-            if where == place_:
+            if where == block_:
 
                 @pl.when(head == h)
                 def _():
@@ -787,8 +947,8 @@
                 part = dot_tn(ds, kb)
                 dqs = part if dqs is None else dqs + part
             put(0, r, dqs * HEAD**-0.5)
-            if i == rows // bq - 2:
-                run_hooks(head, 0)
+            if i < rows // bq - 1:
+                run_hooks(head, i)
         put(1, pl.ds(0, rows), dk_acc[...])
         put(2, pl.ds(0, rows), dv_acc[...])
 
@@ -801,7 +961,7 @@
             with scope("weights"):
                 gpair[pair] = dot_tn(low[...], dqkv[pair]).astype(BF16)
 
-        run_hooks(head, 1)
+        run_hooks(head, rows // bq - 1)
         return carry
 
     lax.fori_loop(0, heads, one_head, 0)
@@ -821,12 +981,14 @@
         return remote(gn_send.at[r], gn_got.at[r], narrow, 2 + j, peer)
 
     for j in range(each):
-        gn_send[j * block : (j + 1) * block, :] = gn_part((1 - n) * half + j * block).astype(BF16)
+        with scope("gn_peer"):
+            gn_send[j * block : (j + 1) * block, :] = gn_part((1 - n) * half + j * block).astype(BF16)
         gn_copy(j).start()
-        tick(f"p{j}", *qkv[::-1], proj)
+        tick(PART_TICKS[j % 2])
     for j in range(each):
-        gn_own[j * block : (j + 1) * block, :] = gn_part(n * half + j * block)
-    tick("q0", up, down)
+        with scope("gn_own"):
+            gn_own[j * block : (j + 1) * block, :] = gn_part(n * half + j * block)
+        tick(PART_TICKS[2 + j % 2])
 
     sums[...] = jnp.zeros_like(sums)
 
@@ -844,16 +1006,15 @@
     for p in range(pairs):
         put_sum(shared + fr + p, jnp.sum(dqkv[p, :, 0:pair_w].astype(F32), axis=0, keepdims=True))
         put_sum(shared + fr + lr + p, jnp.sum(dqkv[p, :, 2 * pair_w :].astype(F32), axis=0, keepdims=True))
-    tick("q1", *qkv[::-1], proj)
+    tick(PART_TICKS[4])
 
     mine, other = lane_part(n, cw), lane_part(1 - n, cw)
-    g1 = s1 = 0.0
 
     def ig_copy(j):
         r = block_rows(n * half + j * block, block)
         return remote(ig_send.at[pl.ds(j * block, block)], ig.at[r], narrow, 2 + each + j, peer)
 
-    for j in range(each):
+    def in_norm(j):
         with scope("gn_wait"):
             gn_copy(j).wait()
         rh = pl.ds(j * block, block)
@@ -867,17 +1028,13 @@
         ig_send[rh, :] = ig_own[:, other].astype(BF16)
         ig_copy(j).start()
         ig[r, :] = ig_own[:, mine].astype(BF16)
-        g1 += jnp.sum(g * xhat, axis=0, keepdims=True)
-        s1 += jnp.sum(g, axis=0, keepdims=True)
-        tick(f"r{j}", *qkv[::-1], proj, up, down)
-    put_sum(0, g1)
-    put_sum(dr, s1)
+        return jnp.sum(g * xhat, axis=0, keepdims=True), jnp.sum(g, axis=0, keepdims=True)
 
     def vec_copy(step):
         if step == 0:
             top = pl.ds(0, shared)
             return remote(sums.at[top], sums_box.at[0, top], narrow, 2 + 2 * each, peer)
-        slot = 2 * steps * 32 + step - 1
+        slot = 10 * stride + step - 1
         return remote(sums, sums_box.at[step], across, slot, {"wide": flip(me, step - 1)})
 
     def vec_end(step):
@@ -889,14 +1046,28 @@
         if step < steps:
             vec_copy(step + 1).start()
 
-    vec_copy(0).start()
-    todo = [*qkv[::-1], proj, up, down]
-    step = 0
-    while step <= steps or not all(g.done for g in todo):
-        tick(f"s{step}", *todo)
-        if step <= steps:
-            vec_end(step)
-        step += 1
+    small_step, sums1 = 0, []
+    for names in LAST_TICKS:
+        if names in ("norm0", "norm1"):
+            todo = range(each - 1) if names == "norm0" else range(each - 1, each)
+            sums1 += [in_norm(j) for j in todo]
+            if names == "norm1":
+                put_sum(0, sum(a for a, _ in sums1))
+                put_sum(dr, sum(b for _, b in sums1))
+                vec_copy(0).start()
+        elif names == "small":
+            if small_step <= steps:
+                with scope("small"):
+                    vec_end(small_step)
+            small_step += 1
+        else:
+            tick(names)
+    while small_step <= steps or not all(g.done for g in groups.values()):
+        for name in groups:
+            tick(name)
+        if small_step <= steps:
+            vec_end(small_step)
+        small_step += 1
     small[...] = sums[...]
     with scope("end"):
         layer.wait()
@@ -905,17 +1076,20 @@
 
 
 def back_call(
-    length, qa, k, v, do, o, low, w, xf, gm, gain, lo_send, gup, down_part, gp_own, gp_other,
+    length, qa, k, v, do, o, low, w, xf, gm, gain, lo_send, up_part, down_part, gp_own, gp_other,
     s_ub, s_db, s_g2, s_s2, s_pb, wide, bq=256,
 ):
     heads, rows, pair = qa.shape
-    d, f, lw = gain.shape[0], gup.shape[1], k.shape[1]
+    d, f, lw = gain.shape[0], up_part.shape[1], k.shape[1]
     cw, half = d // 2, rows // 2
     block = min(256, half)
     each, steps, pairs = half // block, bits(wide), heads // 2
     sd, vm = jax.ShapeDtypeStruct, pltpu.VMEM
     shape = lambda r: Chain(0, order_of(wide, 0), r, None, None, 0)
+    stride = 2 * len(shape(d).ops)
     c_down, c_up, c_gp = shape(f), shape(d), shape(2 * lw)
+    other = lambda r: Chain(0, order_of(wide, 1), r, None, None, 0).box_rows
+    down_rows, up_rows = max(c_down.box_rows, other(f)), max(c_up.box_rows, other(d))
     vec_rows = -(-6 * d // 1024) * 8 + -(-(f + 2 * lw) // 1024) * 8
     work = 2 * heads * rows * rows * HEAD
     return pl.pallas_call(
@@ -927,23 +1101,23 @@
         scratch_shapes=[
             vm(qa.shape, BF16), vm((rows, lw), BF16), vm((rows, lw), BF16), vm((rows, lw), BF16), vm((rows, lw), BF16),
             vm((rows, d), BF16), vm((pairs, d, 3 * pair), BF16), vm((half, d), BF16), vm((half, d), F32),
-            vm((d, f), BF16), vm((f // 2, d), BF16), vm((2 * lw, cw), BF16), vm((2 * lw, cw), BF16),
+            vm((d // 2, f), BF16), vm((f // 2, d), BF16), vm((2 * lw, cw), BF16), vm((2 * lw, cw), BF16),
             vm((rows, pair), BF16), vm((rows, pair), BF16), vm((rows, pair), F32), vm((rows, pair), F32),
             vm((pairs, rows, 3 * pair), BF16), vm((pairs, d, 3 * pair), BF16),
-            vm((c_down.box_rows, d), BF16), vm((f // 2, d), BF16), vm((c_down.size, d), BF16),
-            vm((c_up.box_rows, f), BF16), vm((d // 2, f), BF16), vm((c_up.size, f), BF16),
+            vm((down_rows, d), BF16), vm((f // 2, d), BF16), vm((c_down.size, d), BF16),
+            vm((up_rows, f), BF16), vm((d // 2, f), BF16), vm((c_up.size, f), BF16),
             vm((c_gp.box_rows, cw), BF16), vm((lw, cw), BF16), vm((c_gp.size, cw), BF16),
             vm((pairs, c_up.box_rows, 3 * pair), BF16), vm((pairs, d // 2, 3 * pair), BF16),
             vm((pairs, c_up.size, 3 * pair), BF16),
             vm((half, d), BF16), vm((half, d), BF16), vm((half, d), F32), vm((block, d), F32), vm((half, cw), BF16),
             vm((vec_rows, 128), F32), vm((steps + 1, vec_rows, 128), F32),
         ]
-        + sems(64, 32, 3 + 2 * each, 3 + 2 * each, 65 * steps, 65 * steps),
+        + sems(64, 32, 3 + 2 * each, 3 + 2 * each, 11 * stride, 11 * stride),
         compiler_params=params(collective_id=4, has_side_effects=True),
         cost_estimate=cost(10 * work + 4 * rows * d * 3 * lw, 2 * rows * d * 20, work // 256),
         name="back",
     )(
-        length, qa, k, v, do, o, low, w, xf, gm, gain, lo_send, gup, down_part, gp_own, gp_other,
+        length, qa, k, v, do, o, low, w, xf, gm, gain, lo_send, up_part, down_part, gp_own, gp_other,
         s_ub, s_db, s_g2, s_s2, s_pb,
     )
 
@@ -1024,12 +1198,12 @@
 
     xf, low, q, k, v = qkv_call(tokens, w3, qv_bias, first_gain, first_shift)
     mixed, qa, mixed_got, proj_got = attend_forward(lengths, q, k, v, proj_weight)
-    lo, lo_send, gmix, gm, gup, down_part, gp_own, gp_other, s_ub, s_db, s_g2, s_s2, s_pb = mlp_call(
+    lo, lo_send, gmix, gm, up_part, down_part, gp_own, gp_other, s_ub, s_db, s_g2, s_s2, s_pb = mlp_call(
         lengths, xf, mixed, mixed_got, proj_weight, proj_got, proj_bias, second_gain, second_shift,
         up_weight, up_bias, down_weight, cotangent, wide,
     )
     lo_got, gdown, gup, gp, g0, g1, g2, ig, small = back_call(
-        lengths, qa, k, v, gmix, mixed, low, w3, xf, gm, first_gain, lo_send, gup, down_part, gp_own, gp_other,
+        lengths, qa, k, v, gmix, mixed, low, w3, xf, gm, first_gain, lo_send, up_part, down_part, gp_own, gp_other,
         s_ub, s_db, s_g2, s_s2, s_pb, wide,
     )
     out, ig, o_qkv, o_qvb, o_proj, *rest = finish_call(

time: 237 us -> 217 us (0.916)
  Pallas kernels: 234 us -> 214 us
    pallas_call x1, Pallas kernels: 119 us -> 98.2 us  [back_call(): pl.pallas_call(functools.partial(back_body, bq=bq, wide=wide), out_shape=...]
where the time goes in v6:
time: 217 us
  Pallas kernels  214 us (99%)
    pallas_call x1, Pallas kernels, back_call(): pl.pallas_call(functools.partial(back_body, bq=bq, wide=wide), out_shape=...  98.2 us
    pallas_call x1, Pallas kernels, mlp_call(): pl.pallas_call(functools.partial(mlp_body, wide=wide), out_shape=(sd((row...  51.7 us
    pallas_call x1, Pallas kernels, attend_forward(): pl.pallas_call(functools.partial(fwd_body, bq=bq), out_shape=(sd((rows, w...  28.8 us
    pallas_call x1, Pallas kernels, qkv_call(): pl.pallas_call(qkv_body, out_shape=(sd((rows, d), BF16), sd((rows, d), BF...  24.2 us
    pallas_call x1, Pallas kernels, finish_call(): pl.pallas_call(functools.partial(finish_body, factor=factor, dr=dr, share...  10.9 us

profile of v6, /device:TPU:0, one launch (start us, length us, event | category | flops | bytes accessed | tf_op | source)
XLA Modules:
  0.0 216.6 jit_solution(4636002480317687513)
XLA Ops:
  1.3 1.3 reshape.64.bias
  2.6 24.2 %norm_qkv.1 = (bf16[1024,768]{1,0:T(8,128)(2,1)}, bf16[1024,768]{1,0:T(8,128)(2,1)}, bf16[1024,384]{1,0:T(8,128)(2,1)}, bf16[1024,384]{1,0:T(8,128)(2,1)}, bf16[1024,384]{1,0:T(8,128)(2,1)}) custom-call(bf16[1024,384]{1,0:T(8,128)(2,1)} %own.1, bf16[1024,384]{1,0:T(8,128)(2,1)} %own.1, bf16[3,768,384]{2,1,0:T(8,128)(2,1)} %bitcast.10, bf16[2,384]{1,0:T(2,128)(2,1)} %bias.1, ...), custom_call_target="tpu_custom_call" | custom-call | flops 1811939328 | bytes 9633792 | tf_op jit(solution)/shard_map/norm_qkv/pallas_call | solution.py:385
  26.7 28.8 %attend_fwd.1 = (bf16[1024,384]{1,0:T(8,128)(2,1)}, bf16[6,1024,128]{2,1,0:T(8,128)(2,1)}, bf16[1024,384]{1,0:T(8,128)(2,1)}, bf16[384,768]{1,0:T(8,128)(2,1)}) custom-call(s32[1]{0:T(128)S(6)} %copy.29.len_ref, bf16[1024,384]{1,0:T(8,128)(2,1)} %get-tuple-element.60.q, bf16[1024,384]{1,0:T(8,128)(2,1)} %get-tuple-element.61.k.k_hbm, ...), custom_call_target="tpu_custom_call" | custom-call | flops 3221225472 | bytes 4718592 | tf_op jit(solution)/shard_map/attend_fwd/pallas_call | solution.py:495
  55.6 51.7 %mlp.1 = (f32[1024,384]{1,0:T(8,128)}, bf16[1024,384]{1,0:T(8,128)(2,1)}, bf16[1024,384]{1,0:T(8,128)(2,1)}, f32[512,768]{1,0:T(8,128)}, bf16[384,1536]{1,0:T(8,...) custom-call(s32[1]{0:T(128)S(6)} %copy.29.len_ref, ...), custom_call_target="tpu_custom_call" | custom-call | flops 15703474176 | bytes 17301504 | tf_op jit(solution)/shard_map/mlp/pallas_call | solution.py:732
  107.3 98.2 %back.1 = (bf16[1024,384]{1,0:T(8,128)(2,1)}, bf16[1536,768]{1,0:T(8,128)(2,1)}, bf16[768,1536]{1,0:T(8,128)(2,1)}, bf16[768,384]{1,0:T(8,128)(2,1)}, bf16[768,3...) custom-call(s32[1]{0:T(128)S(6)} %copy.29.len_ref, ...), custom_call_target="tpu_custom_call" | custom-call | flops 11676942336 | bytes 31457280 | tf_op jit(solution)/shard_map/back/pallas_call | solution.py:1095
  205.5 10.9 %finish.1 = (bf16[1024,384]{1,0:T(8,128)(2,1)}, bf16[1024,384]{1,0:T(8,128)(2,1)}, f32[3,768,384]{2,1,0:T(8,128)}, f32[2,384]{1,0:T(2,128)}, f32[384,768]{1,0:T(...) custom-call(f32[1024,384]{1,0:T(8,128)} %get-tuple-element.66.lo, ...), custom_call_target="tpu_custom_call" | custom-call | flops 9437184 | bytes 28311552 | tf_op jit(solution)/shard_map/finish/pallas_call | solution.py:1177

commit v7 on v6

--- a/solution.py
+++ b/solution.py
@@ -80,9 +80,9 @@
     pl.semaphore_wait(barrier, len(peers))
 
 
-def remote(src, dst, sems, at, peer):
+def remote(src, dst, sems, at, peer, send_at=None):
     return pltpu.make_async_remote_copy(
-        src_ref=src, dst_ref=dst, send_sem=sems[0].at[at], recv_sem=sems[1].at[at],
+        src_ref=src, dst_ref=dst, send_sem=sems[0].at[at if send_at is None else send_at], recv_sem=sems[1].at[at],
         device_id=peer, device_id_type=MESH,
     )
 
@@ -91,7 +91,7 @@
     return pl.ds(start if isinstance(start, int) else pl.multiple_of(start, unit), size)
 
 
-LINE = 4
+LINE, CHIPS = 4, 8
 
 
 def when(cond, action):
@@ -106,14 +106,20 @@
 
 
 class Chain:
-    def __init__(self, me, order, rows, cols, sems, at):
-        self.me, self.cols, self.sems, self.at = me, cols, sems, at
+    def __init__(self, me, order, rows, cols, sems, send_at, recv_at):
+        self.me, self.cols, self.sems, self.send_at = me, cols, sems, send_at
         self.phases, self.ops, back = [], [], []
         base, size, box = 0, rows, 0
         for kind, bit in order:
             if kind == "line" and size % (16 * LINE):
                 raise ValueError(rows)
-            if kind == "line":
+            if kind == "all":
+                ways = CHIPS >> (bit - 1)
+                part = size // ways
+                keep, give, boxes = base + (me // (1 << bit)) % ways * part, None, (ways - 1) * part
+                self.ops.append(("send", len(self.phases), ways))
+                back = [("share", len(self.phases), ways)] + back
+            elif kind == "line":
                 part = size // LINE
                 keep, give, boxes = base + (me // 4) % LINE * part, None, 2 * (LINE - 1) * part
                 self.ops += [("line", len(self.phases), i) for i in range(1, LINE)]
@@ -132,6 +138,12 @@
         self.scatters = len(self.ops)
         self.ops += back
         self.base, self.size, self.box_rows = base, size, box
+        self.recv_at, widest = [], 1
+        for kind, _, i in self.ops:
+            width = {"line": 2, "spread": 2, "send": i - 1, "share": i - 1}.get(kind, 1)
+            self.recv_at.append(recv_at)
+            recv_at, widest = recv_at + width, max(widest, width)
+        self.recv_next, self.send_next = recv_at, send_at + widest
 
     def bind(self, src, box, part, own, dst=None, entry=0):
         self.src, self.box, self.part, self.own, self.dst = src, box, part, own, dst
@@ -148,7 +160,7 @@
         return self.part, self.phases[0][2]
 
     def _remote(self, op, lane, src, dst, to):
-        return remote(src, dst, self.sems, self.at + 2 * op + lane, {"wide": to})
+        return remote(src, dst, self.sems, self.recv_at[op] + lane, {"wide": to}, self.send_at + lane)
 
     def _add(self, rows, target, first, *terms):
         unit = next(u for u in (96, 64, 48, 32, 16) if rows % u == 0)
@@ -157,8 +169,9 @@
             total = None
             for ref, start in terms:
                 value = ref[block_rows(start + i * unit, unit), self.cols]
+                value = value.astype(F32) if len(terms) > 2 else value
                 total = value if total is None else total + value
-            target[block_rows(first + i * unit, unit), self.cols] = total
+            target[block_rows(first + i * unit, unit), self.cols] = total.astype(BF16)
             return carry
 
         lax.fori_loop(0, rows // unit, add, 0)
@@ -174,6 +187,25 @@
         bit, _, keep, _, rows, _ = self.phases[phase]
         region = self.dst.at[block_rows(keep, rows), self.cols]
         return self._remote(op, 0, region, region, flip(self.me, bit))
+
+
+    def _others(self, bit, ways):
+        for m in range(1, ways):
+            yield m - 1, flip_all(self.me, bit, m)
+
+    def _sends(self, op, phase, ways):
+        bit, base, _, _, rows, box = self.phases[phase]
+        source, off = self._source(phase)
+        for m, to in self._others(bit, ways):
+            src = source.at[block_rows(base - off + (to // (1 << bit)) % ways * rows, rows), self.cols]
+            yield self._remote(op, m, src, self.box.at[pl.ds(box + m * rows, rows), self.cols], to)
+
+    def _shares(self, op, phase, ways, came):
+        bit, base, keep, _, rows, _ = self.phases[phase]
+        for m, to in self._others(bit, ways):
+            at = base + (to // (1 << bit)) % ways * rows if came else keep
+            region = self.dst.at[block_rows(at, rows), self.cols]
+            yield self._remote(op, m, region, region, to)
 
 
     def _slot(self, phase, lane, i):
@@ -257,6 +289,12 @@
             self._pair(op, phase).start()
         elif kind == "join":
             self._join(op, phase).start()
+        elif kind == "send":
+            for copy in self._sends(op, phase, i):
+                copy.start()
+        elif kind == "share":
+            for copy in self._shares(op, phase, i, False):
+                copy.start()
         elif kind == "line":
             for cond, copy in self._line_sends(op, phase, i):
                 when(cond, lambda: copy().start())
@@ -274,6 +312,19 @@
             self._add(rows, target, keep - out, (self.box, box), (source, keep - off))
         elif kind == "join":
             self._join(op, phase).wait()
+        elif kind == "send":
+            for copy in self._sends(op, phase, i):
+                copy.wait()
+            _, _, keep, _, rows, box = self.phases[phase]
+            source, off = self._source(phase)
+            target, out = self._target(phase)
+            terms = [(self.box, box + m * rows) for m in range(i - 1)]
+            self._add(rows, target, keep - out, (source, keep - off), *terms)
+        elif kind == "share":
+            for copy in self._shares(op, phase, i, False):
+                copy.wait_send()
+            for copy in self._shares(op, phase, i, True):
+                copy.wait_recv()
         elif kind == "line":
             self._line_end(op, phase, i)
         else:
@@ -281,14 +332,13 @@
                 when(send_if, lambda: send().wait_send())
                 when(recv_if, lambda: recv().wait_recv())
 
-    def gather_open(self, sem):
-        region = self.dst.at[block_rows(self.base, self.size), self.cols]
-        return pltpu.make_async_copy(self.own.at[:, self.cols], region, sem)
+    def gather_open(self):
+        self._add(self.size, self.dst, self.base, (self.own, 0))
 
 
 class Group:
-    def __init__(self, chain, open_sem=None, at=0, entry=0, leave=None):
-        self.chain, self.open_sem, self.at = chain, open_sem, at
+    def __init__(self, chain, entry=0, leave=None, out=None):
+        self.chain, self.out = chain, out
         self.ops = list(range(entry, len(chain.ops) if leave is None else leave))
         self.pos = -1
 
@@ -306,17 +356,21 @@
             if pos >= 0:
                 self.chain.end(self.ops[pos])
             if pos + 1 >= len(self.ops):
+                if self.out is not None:
+                    self.store().start()
                 return
             if self.ops[pos + 1] == self.chain.scatters:
-                opened = self.chain.gather_open(self.open_sem.at[self.at])
-                opened.start()
-                opened.wait()
+                self.chain.gather_open()
             self.chain.start(self.ops[pos + 1])
 
         return tick
 
     def tick(self):
         self.next()()
+
+    def store(self):
+        out, sem = self.out
+        return pltpu.make_async_copy(self.chain.dst.at[:, self.chain.cols], out.at[:, self.chain.cols], sem)
 
 
 def bits(wide):
@@ -326,16 +380,75 @@
 def order_of(wide, kind):
     first, rest = ("pair", 0), [("pair", b) for b in range(4, bits(wide))]
     pair, line = ("pair", 1), ("line", 2)
-    return [first, pair, line, *rest] if kind == 0 else [first, line, pair, *rest]
-
-
-def lanes_split(cols):
-    return [(0, pl.ds(0, cols // 2)), (1, pl.ds(cols // 2, cols // 2))]
+    return {
+        0: [first, pair, line, *rest], 1: [first, line, pair, *rest], 2: [first, ("all", 1), *rest],
+        3: [first, pair, ("all", 2), *rest],
+    }[kind]
+
+
+def lanes_split(cols, kinds):
+    w = cols // len(kinds)
+    return [(kind, pl.ds(i * w, w)) for i, kind in enumerate(kinds)]
+
+
+def flip_all(me, bit, mask):
+    to = me
+    for i in range(3):
+        if mask >> i & 1:
+            to = to + (flip(me, bit + i) - me)
+    return to
+
+
+def chip_peers(me):
+    return [flip_all(me, 1, m) for m in range(1, CHIPS)]
 
 
 def wide_peers(me, wide):
-    pairs = [flip(me, b) for b in range(bits(wide)) if b not in (2, 3)]
-    return [{"wide": peer} for peer in pairs + [line_peer(me, by) for by in range(1, LINE)]]
+    pairs = [flip(me, b) for b in range(bits(wide)) if b not in (1, 2, 3)]
+    return [{"wide": peer} for peer in pairs + chip_peers(me)]
+
+
+class Small:
+    def __init__(self, me, n, wide, total, box, shared, narrow, across, narrow_at, send_at, recv_at):
+        self.me, self.n, self.total, self.box, self.shared = me, n, total, box, shared
+        self.narrow, self.across = narrow, across
+        self.narrow_at, self.send_at, self.recv_at = narrow_at, send_at, recv_at
+        self.ops = ["narrow", 0, "chips"] + list(range(4, bits(wide)))
+        self.scatters, self.dst = None, None
+        self.send_next = send_at + CHIPS - 1
+        self.recv_next = recv_at + len(self.ops) + CHIPS - 1
+
+    def _copies(self, op):
+        kind = self.ops[op]
+        if kind == "narrow":
+            top = pl.ds(0, self.shared)
+            return [remote(self.total.at[top], self.box.at[0, top], self.narrow, self.narrow_at, {"narrow": 1 - self.n})]
+        if kind == "chips":
+            return [
+                remote(
+                    self.total, self.box.at[2 + i], self.across, self.recv_at + len(self.ops) + i, {"wide": to},
+                    self.send_at + i,
+                )
+                for i, to in enumerate(chip_peers(self.me))
+            ]
+        slot = 1 if kind == 0 else CHIPS + 1 + kind - 4
+        peer = {"wide": flip(self.me, kind)}
+        return [remote(self.total, self.box.at[slot], self.across, self.recv_at + op, peer, self.send_at)]
+
+    def start(self, op):
+        for copy in self._copies(op):
+            copy.start()
+
+    def end(self, op):
+        for copy in self._copies(op):
+            copy.wait()
+        kind = self.ops[op]
+        if kind == "narrow":
+            self.total[0 : self.shared, :] += self.box[0, 0 : self.shared, :]
+        elif kind == "chips":
+            self.total[...] += sum(self.box[2 + i] for i in range(CHIPS - 1))
+        else:
+            self.total[...] += self.box[1 if kind == 0 else CHIPS + 1 + kind - 4]
 
 
 def vmem():
@@ -510,7 +623,8 @@
     )(length, q, k, v, pw)
 
 
-DOWN_ENTRY, UP_ENTRY = (2, 1), (1, 1)
+DOWN_ENTRY, UP_ENTRY = (2, 2), (1, 1)
+DOWN_KINDS, UP_KINDS = (0, 0), (0, 1)
 
 
 def mlp_body(
@@ -652,17 +766,18 @@
 
         lax.fori_loop(0, dst.shape[0] // 256, step, 0)
 
-    used = iter(range(0, 64, 4))
-
-    def group(src, box_, part, leaves):
+    used = iter(range(16))
+
+    def group(src, box_, part, kinds, leaves):
         parts = []
-        for (kind, cols), leave in zip(lanes_split(src.shape[1]), leaves):
-            chain = Chain(me, order_of(wide, kind), src.shape[0], cols, across, next(used))
+        for (kind, cols), leave in zip(lanes_split(src.shape[1], kinds), leaves):
+            a = next(used)
+            chain = Chain(me, order_of(wide, kind), src.shape[0], cols, across, 2 * a, 2 * a)
             parts.append(Group(chain.bind(src, box_, part, None), leave=leave))
         return parts
 
-    reduce_down = group(gdown, box, down_part, DOWN_ENTRY)
-    reduce_up = group(gup, up_box, up_part, UP_ENTRY)
+    reduce_down = group(gdown, box, down_part, DOWN_KINDS, DOWN_ENTRY)
+    reduce_up = group(gup, up_box, up_part, UP_KINDS, UP_ENTRY)
 
     def advance(name, *groups):
         with scope(name):
@@ -746,7 +861,7 @@
             vm((half, d), BF16), vm((half, d), BF16), vm((half, d), F32), vm((f, d), BF16), vm((d, f), BF16),
             vm((f, d), BF16), vm((d, f), BF16), vm((half, d), F32), vm((half, d), BF16), vm((half, lw), BF16),
         ]
-        + sems(16, 4, 4 * each, 4 * each, 16, 16),
+        + sems(12, 4, 4 * each, 4 * each, 8, 8),
         compiler_params=params(collective_id=3, has_side_effects=True),
         cost_estimate=cost(2 * rows * d * (d + 6 * f), 2 * (rows * d * 8 + 2 * d * f), rows * f),
         name="mlp",
@@ -754,30 +869,23 @@
 
 
 HEAD_TICKS = (
-    ((0, 3), "D0"),
-    ((1, 2), "D1"),
-    ((1, 3), "U0U1Q0"),
-    ((2, 0), "D0"),
-    ((2, 1), "Q0"),
-    ((2, 2), "D1"),
-    ((2, 3), "U0"),
-    ((3, 1), "Q0P0U1"),
-    ((3, 2), "D0"),
-    ((3, 3), "D1P0D0Q1"),
-    ((4, 0), "U0"),
-    ((4, 1), "Q0Q1"),
-    ((4, 2), "D1D0"),
-    ((4, 3), "U1P0"),
-    ((5, 0), "U0"),
-    ((5, 1), "Q0Q1D0P0D1"),
-    ((5, 2), "U0Q0U1Q1"),
-    ((5, 3), "D1Q1P0Q2"),
+    ((1, 2), "U1"),
+    ((1, 3), "D1U0D0Q0"),
+    ((2, 2), "Q0U1"),
+    ((2, 3), "D1"),
+    ((3, 1), "U0SA"),
+    ((3, 2), "D0P0"),
+    ((3, 3), "SAQ0U1Q1"),
+    ((4, 1), "D1"),
+    ((4, 2), "U0Q1"),
+    ((4, 3), "D0"),
+    ((5, 0), "P0"),
+    ((5, 3), "Q0D1U1Q2"),
 )
-PART_TICKS = ("Q0Q2U0Q1U1D0", "D1", "Q0D0P0", "Q2U0Q1", "")
+PART_TICKS = ("U0D0SAQ1P0Q2", "Q0D1U1", "Q1U0", "D0P0", "Q0Q2")
 LAST_TICKS = (
-    "Q2U1", "norm0", "D1Q2Q0P0U0Q1D1Q2", "U0U1Q0P0Q1", "norm1", "Q0Q2U1Q2",
-    "small", "P0U1", "small", "P0Q2Q1", "small", "Q1",
-    "small", "Q2", "small", "Q2",
+    "D1Q1P0U1Q2Q1", "norm0", "U0Q2D0Q0D1Q2P0U1", "D1Q1U0", "norm1", "Q0Q2P0D0D0U1Q1Q0",
+    "U1Q2SBU0SBP0Q1U0", "Q2Q0Q0P0SBQ1P0Q1", "Q2Q2",
 )
 
 
@@ -788,11 +896,12 @@
 def back_body(
     len_ref, qa_hbm, k_hbm, v_hbm, do_hbm, o_hbm, low_hbm, w_hbm, xf_hbm, gm_hbm, gain, lo_send, up_part_hbm,
     down_part_hbm, gp_own_hbm, gp_other_hbm, s_ub, s_db, s_g2, s_s2, s_pb,
-    lo_got, down_out, up_out, gp_out, g0_out, g1_out, g2_out, ig, small,
+    lo_got, down_out, up_out, gp_out, g0_out, g1_out, g2_out, ig, small_a, small_b,
     qa, k, v, do, o, low, wp, xf, gm, up_part, down_part, gp_src, gp_got,
     ka, va, dk_acc, dv_acc, dqkv, gpair,
     down_box, down_part2, down_own, up_box, up_part2, up_own, gp_box, gp_part, gp_own, pair_box, pair_part, pair_own,
-    gn_send, gn_got, gn_own, ig_own, ig_send, sums, sums_box,
+    down_sum, up_sum, gp_sum, pair_sum,
+    gn_send, gn_got, gn_own, ig_own, ig_send, early, early_box, late_sums, late_box,
     load_sem, open_sem, nsend, nrecv, wsend, wrecv, *, bq, wide,
 ):
     n, me = lax.axis_index("narrow"), lax.axis_index("wide")
@@ -836,35 +945,53 @@
     own_half = block_rows(n * half, half)
     late += [load(xf_hbm.at[own_half], xf), load(gm_hbm, gm)]
 
-    stride = 2 * len(Chain(0, order_of(wide, 0), d, None, None, 0).ops)
-    at = iter(range(0, 64 * stride, stride))
-    opening = iter(range(32))
-
-    def group(src, box, part, own, dst, entries=(0,)):
+    at = [0, 0]
+    opening = iter(range(16))
+
+    def group(src, box, part, own, dst, out, kinds=(0,), entries=(0,)):
         rows_, cols_ = dst.shape
         made = []
-        parts = lanes_split(cols_) if len(entries) == 2 else [(0, pl.ds(0, cols_))]
-        for (kind, cols), entry in zip(parts, entries):
-            chain = Chain(me, order_of(wide, kind), rows_, cols, across, next(at))
-            made.append(Group(chain.bind(src, box, part, own, dst, entry), open_sem, next(opening), entry))
+        for (kind, cols), entry in zip(lanes_split(cols_, kinds), entries):
+            chain = Chain(me, order_of(wide, kind), rows_, cols, across, *at)
+            at[:] = chain.send_next, chain.recv_next
+            made.append(Group(chain.bind(src, box, part, own, dst, entry), entry, out=(out, open_sem.at[next(opening)])))
         return made
 
     groups = {}
-    groups["D0"], groups["D1"] = group(down_part, down_box, down_part2, down_own, down_out, DOWN_ENTRY)
-    groups["U0"], groups["U1"] = group(up_part, up_box, up_part2, up_own, up_out, UP_ENTRY)
-    groups["P0"] = group(gp_src, gp_box, gp_part, gp_own, gp_out)[0]
+    groups["D0"], groups["D1"] = group(down_part, down_box, down_part2, down_own, down_sum, down_out, DOWN_KINDS, DOWN_ENTRY)
+    groups["U0"], groups["U1"] = group(up_part, up_box, up_part2, up_own, up_sum, up_out, UP_KINDS, UP_ENTRY)
+    groups["P0"] = group(gp_src, gp_box, gp_part, gp_own, gp_sum, gp_out, kinds=(1,))[0]
     for p, out in zip(range(pairs), (g0_out, g1_out, g2_out)):
-        groups[f"Q{p}"] = group(gpair.at[p], pair_box.at[p], pair_part.at[p], pair_own.at[p], out)[0]
+        groups[f"Q{p}"] = group(
+            gpair.at[p], pair_box.at[p], pair_part.at[p], pair_own.at[p], pair_sum.at[p], out,
+        )[0]
+
+    dr, fr, lr = d // 128, s_ub.shape[1] // 128, lw // 128
+    for i, (name, total, box, shared) in enumerate(
+        (("SA", early, early_box, 4 * dr), ("SB", late_sums, late_box, -(-2 * dr // 8) * 8))
+    ):
+        one = Small(me, n, wide, total, box, shared, narrow, across, 2 + 2 * each + i, *at)
+        at[:] = one.send_next, one.recv_next
+        groups[name] = Group(one)
+
+    def put_sum(ref, start, value):
+        for i in range(value.shape[1] // 128):
+            ref[start + i : start + i + 1, :] = value[:, i * 128 : (i + 1) * 128]
+
+    early[...] = jnp.zeros_like(early)
+    late_sums[...] = jnp.zeros_like(late_sums)
+    for i, ref in enumerate((s_g2, s_s2, s_pb, s_db, s_ub)):
+        put_sum(early, i * dr, ref[...])
 
     def tick(names):
-        with scope(names):
-            for name in pieces(names):
+        for name in pieces(names):
+            with scope(name):
                 groups[name].tick()
 
     part_load.wait()
     tick("D0D1")
     up_load.wait()
-    tick("U0U1")
+    tick("U0U1SA")
 
     kpos = lax.broadcasted_iota(jnp.int32, (rows, 1), 0)
     kbias = jnp.where(kpos < len_ref[0], 0.0, -1e30)
@@ -874,8 +1001,8 @@
         ticks = [groups[name].next() for name in pieces(names)]
 
         def run():
-            with scope(names):
-                for one in ticks:
+            for name, one in zip(pieces(names), ticks):
+                with scope(name):
                     one()
 
         return run
@@ -990,22 +1117,10 @@
             gn_own[j * block : (j + 1) * block, :] = gn_part(n * half + j * block)
         tick(PART_TICKS[2 + j % 2])
 
-    sums[...] = jnp.zeros_like(sums)
-
-    def put_sum(start, value):
-        for i in range(value.shape[1] // 128):
-            sums[start + i : start + i + 1, :] = value[:, i * 128 : (i + 1) * 128]
-
-    dr, fr, lr = d // 128, s_ub.shape[1] // 128, lw // 128
-    shared = -(-6 * dr // 8) * 8
-    put_sum(2 * dr, s_g2[...])
-    put_sum(3 * dr, s_s2[...])
-    put_sum(4 * dr, s_pb[...])
-    put_sum(5 * dr, s_db[...])
-    put_sum(shared, s_ub[...])
+    shared = -(-2 * dr // 8) * 8
     for p in range(pairs):
-        put_sum(shared + fr + p, jnp.sum(dqkv[p, :, 0:pair_w].astype(F32), axis=0, keepdims=True))
-        put_sum(shared + fr + lr + p, jnp.sum(dqkv[p, :, 2 * pair_w :].astype(F32), axis=0, keepdims=True))
+        put_sum(late_sums, shared + p, jnp.sum(dqkv[p, :, 0:pair_w].astype(F32), axis=0, keepdims=True))
+        put_sum(late_sums, shared + lr + p, jnp.sum(dqkv[p, :, 2 * pair_w :].astype(F32), axis=0, keepdims=True))
     tick(PART_TICKS[4])
 
     mine, other = lane_part(n, cw), lane_part(1 - n, cw)
@@ -1030,46 +1145,26 @@
         ig[r, :] = ig_own[:, mine].astype(BF16)
         return jnp.sum(g * xhat, axis=0, keepdims=True), jnp.sum(g, axis=0, keepdims=True)
 
-    def vec_copy(step):
-        if step == 0:
-            top = pl.ds(0, shared)
-            return remote(sums.at[top], sums_box.at[0, top], narrow, 2 + 2 * each, peer)
-        slot = 10 * stride + step - 1
-        return remote(sums, sums_box.at[step], across, slot, {"wide": flip(me, step - 1)})
-
-    def vec_end(step):
-        vec_copy(step).wait()
-        if step == 0:
-            sums[0:shared, :] += sums_box[0, 0:shared, :]
-        else:
-            sums[...] += sums_box[step]
-        if step < steps:
-            vec_copy(step + 1).start()
-
-    small_step, sums1 = 0, []
+    sums1 = []
     for names in LAST_TICKS:
         if names in ("norm0", "norm1"):
             todo = range(each - 1) if names == "norm0" else range(each - 1, each)
             sums1 += [in_norm(j) for j in todo]
             if names == "norm1":
-                put_sum(0, sum(a for a, _ in sums1))
-                put_sum(dr, sum(b for _, b in sums1))
-                vec_copy(0).start()
-        elif names == "small":
-            if small_step <= steps:
-                with scope("small"):
-                    vec_end(small_step)
-            small_step += 1
+                put_sum(late_sums, 0, sum(a for a, _ in sums1))
+                put_sum(late_sums, dr, sum(b for _, b in sums1))
+                tick("SB")
         else:
             tick(names)
-    while small_step <= steps or not all(g.done for g in groups.values()):
+    while not all(g.done for g in groups.values()):
         for name in groups:
             tick(name)
-        if small_step <= steps:
-            vec_end(small_step)
-        small_step += 1
-    small[...] = sums[...]
+    small_a[...] = early[...]
+    small_b[...] = late_sums[...]
     with scope("end"):
+        for one in groups.values():
+            if one.out is not None:
+                one.store().wait()
         layer.wait()
         for j in range(each):
             ig_copy(j).wait()
@@ -1085,19 +1180,22 @@
     block = min(256, half)
     each, steps, pairs = half // block, bits(wide), heads // 2
     sd, vm = jax.ShapeDtypeStruct, pltpu.VMEM
-    shape = lambda r: Chain(0, order_of(wide, 0), r, None, None, 0)
-    stride = 2 * len(shape(d).ops)
+    shape = lambda r, kind=0: Chain(0, order_of(wide, kind), r, None, None, 0, 0)
     c_down, c_up, c_gp = shape(f), shape(d), shape(2 * lw)
-    other = lambda r: Chain(0, order_of(wide, 1), r, None, None, 0).box_rows
-    down_rows, up_rows = max(c_down.box_rows, other(f)), max(c_up.box_rows, other(d))
-    vec_rows = -(-6 * d // 1024) * 8 + -(-(f + 2 * lw) // 1024) * 8
+    down_rows, up_rows, pair_rows = (max(shape(r, k).box_rows for k in range(4)) for r in (f, d, d))
+    small = lambda shared, rest: -(-(shared + rest) // 8) * 8
+    rows_a = small(4 * d // 128, f // 128)
+    rows_b = small(-(-2 * d // 1024) * 8, 2 * lw // 128)
+    slots = CHIPS + 1 + max(0, bits(wide) - 4)
+    semaphores = (len(DOWN_KINDS) + len(UP_KINDS) + 1 + pairs) * shape(d).recv_next + 2 * (bits(wide) + CHIPS)
     work = 2 * heads * rows * rows * HEAD
     return pl.pallas_call(
         functools.partial(back_body, bq=bq, wide=wide),
         out_shape=(sd((rows, cw), BF16), sd((f, d), BF16), sd((d, f), BF16), sd((2 * lw, cw), BF16))
-        + (sd((d, 3 * pair), BF16),) * 3 + (sd((rows, cw), BF16), sd((vec_rows, 128), F32)),
+        + (sd((d, 3 * pair), BF16),) * 3
+        + (sd((rows, cw), BF16), sd((rows_a, 128), F32), sd((rows_b, 128), F32)),
         in_specs=[pl.BlockSpec(memory_space=pltpu.SMEM)] + [anywhere()] * 9 + [vmem()] + [anywhere()] * 5 + [vmem()] * 5,
-        out_specs=(anywhere(),) * 7 + (vmem(), vmem()),
+        out_specs=(anywhere(),) * 7 + (vmem(), vmem(), vmem()),
         scratch_shapes=[
             vm(qa.shape, BF16), vm((rows, lw), BF16), vm((rows, lw), BF16), vm((rows, lw), BF16), vm((rows, lw), BF16),
             vm((rows, d), BF16), vm((pairs, d, 3 * pair), BF16), vm((half, d), BF16), vm((half, d), F32),
@@ -1106,13 +1204,14 @@
             vm((pairs, rows, 3 * pair), BF16), vm((pairs, d, 3 * pair), BF16),
             vm((down_rows, d), BF16), vm((f // 2, d), BF16), vm((c_down.size, d), BF16),
             vm((up_rows, f), BF16), vm((d // 2, f), BF16), vm((c_up.size, f), BF16),
-            vm((c_gp.box_rows, cw), BF16), vm((lw, cw), BF16), vm((c_gp.size, cw), BF16),
-            vm((pairs, c_up.box_rows, 3 * pair), BF16), vm((pairs, d // 2, 3 * pair), BF16),
+            vm((pair_rows, cw), BF16), vm((lw, cw), BF16), vm((c_gp.size, cw), BF16),
+            vm((pairs, pair_rows, 3 * pair), BF16), vm((pairs, d // 2, 3 * pair), BF16),
             vm((pairs, c_up.size, 3 * pair), BF16),
+            vm((f, d), BF16), vm((d, f), BF16), vm((2 * lw, cw), BF16), vm((pairs, d, 3 * pair), BF16),
             vm((half, d), BF16), vm((half, d), BF16), vm((half, d), F32), vm((block, d), F32), vm((half, cw), BF16),
-            vm((vec_rows, 128), F32), vm((steps + 1, vec_rows, 128), F32),
+            vm((rows_a, 128), F32), vm((slots, rows_a, 128), F32), vm((rows_b, 128), F32), vm((slots, rows_b, 128), F32),
         ]
-        + sems(64, 32, 3 + 2 * each, 3 + 2 * each, 11 * stride, 11 * stride),
+        + sems(8 * pairs + 8, 8, 4 + 2 * each, 4 + 2 * each, 17 + 3 * CHIPS, semaphores),
         compiler_params=params(collective_id=4, has_side_effects=True),
         cost_estimate=cost(10 * work + 4 * rows * d * 3 * lw, 2 * rows * d * 20, work // 256),
         name="back",
@@ -1123,9 +1222,9 @@
 
 
 def finish_body(
-    lo, lo_got, bias, ig, up, down, q, k, v, p0, p1, small,
+    lo, lo_got, bias, ig, up, down, q, k, v, p0, p1, small_a, small_b,
     out, ig_out, o_qkv, o_qvb, o_proj, o_pb, o_up, o_ub, o_down, o_db, o_g1, o_s1, o_g2, o_s2,
-    *, factor, dr, shared,
+    *, factor,
 ):
     n = lax.axis_index("narrow")
     cw = lo.shape[1]
@@ -1142,23 +1241,23 @@
 
     @pl.when(pl.program_id(0) == 0)
     def _():
-        for i, ref in enumerate((o_g1, o_s1, o_g2, o_s2, o_pb, o_db)):
-            ref[...] = small[i * dr : (i + 1) * dr, :] * factor
-        fr = o_ub.shape[0]
-        o_ub[...] = small[shared : shared + fr, :] * factor
-        lr = o_qvb.shape[1] // 128
+        dr, fr = o_g1.shape[0], o_ub.shape[0]
+        for i, ref in enumerate((o_g2, o_s2, o_pb, o_db)):
+            ref[...] = small_a[i * dr : (i + 1) * dr, :] * factor
+        o_ub[...] = small_a[4 * dr : 4 * dr + fr, :] * factor
+        o_g1[...] = small_b[0:dr, :] * factor
+        o_s1[...] = small_b[dr : 2 * dr, :] * factor
+        lr, shared = o_qvb.shape[1] // 128, -(-2 * dr // 8) * 8
         for c in range(2):
             for i in range(lr):
-                at = shared + fr + c * lr + i
-                o_qvb[c : c + 1, i * 128 : (i + 1) * 128] = small[at : at + 1, :] * factor
-
-
-def finish_call(lo, lo_got, bias, ig, up, down, q, k, v, p, small, factor, grid=8):
+                at = shared + c * lr + i
+                o_qvb[c : c + 1, i * 128 : (i + 1) * 128] = small_b[at : at + 1, :] * factor
+
+
+def finish_call(lo, lo_got, bias, ig, up, down, q, k, v, p, small_a, small_b, factor, grid=8):
     rows, cw = lo.shape
     (d, f), lw = up.shape, q.shape[1]
-    dr, shared = d // 128, -(-6 * d // 1024) * 8
-    sd = jax.ShapeDtypeStruct
-    tiny = [sd((dr, 128), F32)] * 2
+    dr, sd = d // 128, jax.ShapeDtypeStruct
     shapes = (
         [sd((rows, cw), BF16), sd((rows, cw), BF16), sd((3, d, lw), F32), sd((2, lw), F32), sd((lw, d), F32)]
         + [sd((dr, 128), F32), sd((d, f), F32), sd((f // 128, 128), F32), sd((f, d), F32)]
@@ -1175,16 +1274,16 @@
         else:
             specs.append(whole_spec(s.shape))
     return pl.pallas_call(
-        functools.partial(finish_body, factor=factor, dr=dr, shared=shared),
+        functools.partial(finish_body, factor=factor),
         out_shape=tuple(shapes),
         grid=(grid,),
         in_specs=[big(lo), big(lo_got), whole_spec(bias.shape), big(ig), big(up), big(down), big(q), big(k), big(v)]
-        + [rows_spec(pb, cw), rows_spec(pb, cw, grid), whole_spec(small.shape)],
+        + [rows_spec(pb, cw), rows_spec(pb, cw, grid), whole_spec(small_a.shape), whole_spec(small_b.shape)],
         out_specs=tuple(specs),
         compiler_params=params(),
         cost_estimate=cost(up.size * 8, up.size * 24),
         name="finish",
-    )(lo, lo_got, bias, ig, up, down, q, k, v, p, p, small)
+    )(lo, lo_got, bias, ig, up, down, q, k, v, p, p, small_a, small_b)
 
 
 def on_device(
@@ -1202,12 +1301,12 @@
         lengths, xf, mixed, mixed_got, proj_weight, proj_got, proj_bias, second_gain, second_shift,
         up_weight, up_bias, down_weight, cotangent, wide,
     )
-    lo_got, gdown, gup, gp, g0, g1, g2, ig, small = back_call(
+    lo_got, gdown, gup, gp, g0, g1, g2, ig, small_a, small_b = back_call(
         lengths, qa, k, v, gmix, mixed, low, w3, xf, gm, first_gain, lo_send, up_part, down_part, gp_own, gp_other,
         s_ub, s_db, s_g2, s_s2, s_pb, wide,
     )
     out, ig, o_qkv, o_qvb, o_proj, *rest = finish_call(
-        lo, lo_got, down_bias.astype(F32).reshape(1, -1), ig, gup, gdown, g0, g1, g2, gp, small,
+        lo, lo_got, down_bias.astype(F32).reshape(1, -1), ig, gup, gdown, g0, g1, g2, gp, small_a, small_b,
         1.0 / (lengths.shape[0] * wide),
     )
     pb, up, ubs, down, dbs, g1, s1, g2, s2 = rest

time: 217 us -> 204 us (0.940)
  Pallas kernels: 214 us -> 201 us
    pallas_call x1, Pallas kernels: 98.2 us -> 84.1 us  [back_call(): pl.pallas_call(functools.partial(back_body, bq=bq, wide=wide), out_shape=...]
where the time goes in v7:
time: 204 us; the launch traced here: 203 us
  Pallas kernels  201 us (99%)
    pallas_call x1, Pallas kernels, back_call(): pl.pallas_call(functools.partial(back_body, bq=bq, wide=wide), out_shape=...  84.1 us
    pallas_call x1, Pallas kernels, mlp_call(): pl.pallas_call(functools.partial(mlp_body, wide=wide), out_shape=(sd((row...  52.6 us
    pallas_call x1, Pallas kernels, attend_forward(): pl.pallas_call(functools.partial(fwd_body, bq=bq), out_shape=(sd((rows, w...  28.8 us
    pallas_call x1, Pallas kernels, qkv_call(): pl.pallas_call(qkv_body, out_shape=(sd((rows, d), BF16), sd((rows, d), BF...  24.2 us
    pallas_call x1, Pallas kernels, finish_call(): pl.pallas_call(functools.partial(finish_body, factor=factor), out_shape=t...  10.9 us

profile of v7, /device:TPU:0, one launch (start us, length us, event | category | flops | bytes accessed | tf_op | source)
XLA Modules:
  0.0 203.4 jit_solution(14856721260595603049)
XLA Ops:
  1.3 1.3 reshape.64.bias
  2.6 24.2 %norm_qkv.1 = (bf16[1024,768]{1,0:T(8,128)(2,1)}, bf16[1024,768]{1,0:T(8,128)(2,1)}, bf16[1024,384]{1,0:T(8,128)(2,1)}, bf16[1024,384]{1,0:T(8,128)(2,1)}, bf16[1024,384]{1,0:T(8,128)(2,1)}) custom-call(bf16[1024,384]{1,0:T(8,128)(2,1)} %own.1, bf16[1024,384]{1,0:T(8,128)(2,1)} %own.1, bf16[3,768,384]{2,1,0:T(8,128)(2,1)} %bitcast.10, bf16[2,384]{1,0:T(2,128)(2,1)} %bias.1, ...), custom_call_target="tpu_custom_call" | custom-call | flops 1811939328 | bytes 9633792 | tf_op jit(solution)/shard_map/norm_qkv/pallas_call | solution.py:498
  26.7 28.8 %attend_fwd.1 = (bf16[1024,384]{1,0:T(8,128)(2,1)}, bf16[6,1024,128]{2,1,0:T(8,128)(2,1)}, bf16[1024,384]{1,0:T(8,128)(2,1)}, bf16[384,768]{1,0:T(8,128)(2,1)}) custom-call(s32[1]{0:T(128)S(6)} %copy.29.len_ref, bf16[1024,384]{1,0:T(8,128)(2,1)} %get-tuple-element.61.q, bf16[1024,384]{1,0:T(8,128)(2,1)} %get-tuple-element.62.k.k_hbm, ...), custom_call_target="tpu_custom_call" | custom-call | flops 3221225472 | bytes 4718592 | tf_op jit(solution)/shard_map/attend_fwd/pallas_call | solution.py:608
  55.6 52.6 %mlp.1 = (f32[1024,384]{1,0:T(8,128)}, bf16[1024,384]{1,0:T(8,128)(2,1)}, bf16[1024,384]{1,0:T(8,128)(2,1)}, f32[512,768]{1,0:T(8,128)}, bf16[384,1536]{1,0:T(8,...) custom-call(s32[1]{0:T(128)S(6)} %copy.29.len_ref, ...), custom_call_target="tpu_custom_call" | custom-call | flops 15703474176 | bytes 17301504 | tf_op jit(solution)/shard_map/mlp/pallas_call | solution.py:847
  108.2 84.1 %back.1 = (bf16[1024,384]{1,0:T(8,128)(2,1)}, bf16[1536,768]{1,0:T(8,128)(2,1)}, bf16[768,1536]{1,0:T(8,128)(2,1)}, bf16[768,384]{1,0:T(8,128)(2,1)}, bf16[768,3...) custom-call(s32[1]{0:T(128)S(6)} %copy.29.len_ref, ...), custom_call_target="tpu_custom_call" | custom-call | flops 11676942336 | bytes 31457280 | tf_op jit(solution)/shard_map/back/pallas_call | solution.py:1192
  192.3 10.9 %finish.1 = (bf16[1024,384]{1,0:T(8,128)(2,1)}, bf16[1024,384]{1,0:T(8,128)(2,1)}, f32[3,768,384]{2,1,0:T(8,128)}, f32[2,384]{1,0:T(2,128)}, f32[384,768]{1,0:T(...) custom-call(f32[1024,384]{1,0:T(8,128)} %get-tuple-element.67.lo, ...), custom_call_target="tpu_custom_call" | custom-call | flops 9437184 | bytes 28311552 | tf_op jit(solution)/shard_map/finish/pallas_call | solution.py:1276

commit v8 on v7

--- a/solution.py
+++ b/solution.py
@@ -463,54 +463,6 @@
     return [pltpu.SemaphoreType.DMA((c,)) for c in counts]
 
 
-def qkv_body(own_hbm, own, w, bias, gain, shift, xf, low, q, k, v, got, send_sem, recv_sem):
-    n = lax.axis_index("narrow")
-    i = pl.program_id(0)
-    rows, cw = own.shape
-    peer = {"narrow": 1 - n}
-
-    def copy(at):
-        block = block_rows(at * rows, rows)
-        return remote(own_hbm.at[block], got.at[block], (send_sem, recv_sem), at, peer)
-
-    @pl.when(i == 0)
-    def _():
-        greet([peer])
-        for at in range(got.shape[0] // rows):
-            copy(at).start()
-
-    xf[:, lane_part(n, cw)] = own[...]
-    with scope("wait"):
-        copy(i).wait()
-    xf[:, lane_part(1 - n, cw)] = got[block_rows(i * rows, rows), :]
-    xhat, _ = norm_rows(xf[...].astype(F32))
-    y = (xhat * vec(gain) + vec(shift)).astype(BF16)
-    low[...] = y
-    q[...] = (dot(y, w[0]) + bias[0:1, :].astype(F32)).astype(BF16) * jnp.asarray(HEAD**-0.5, BF16)
-    k[...] = dot(y, w[1]).astype(BF16)
-    v[...] = (dot(y, w[2]) + bias[1:2, :].astype(F32)).astype(BF16)
-
-
-def qkv_call(own, w, bias, gain, shift, block=256):
-    rows, cw = own.shape
-    d, lw = w.shape[1], w.shape[2]
-    sd = jax.ShapeDtypeStruct
-    return pl.pallas_call(
-        qkv_body,
-        out_shape=(sd((rows, d), BF16), sd((rows, d), BF16)) + (sd((rows, lw), BF16),) * 3,
-        grid_spec=pltpu.PrefetchScalarGridSpec(
-            num_scalar_prefetch=0,
-            grid=(rows // block,),
-            in_specs=[anywhere(), rows_spec(block, cw)] + [whole_spec(a.shape) for a in (w, bias, gain, shift)],
-            out_specs=[rows_spec(block, d)] * 2 + [rows_spec(block, lw)] * 3,
-            scratch_shapes=[pltpu.VMEM((rows, cw), BF16)] + sems(rows // block, rows // block),
-        ),
-        compiler_params=params(collective_id=1, has_side_effects=True),
-        cost_estimate=cost(2 * rows * d * 3 * lw, 2 * (rows * d * 5 + w.size)),
-        name="norm_qkv",
-    )(own, own, w, bias, gain, shift)
-
-
 def three(x):
     hi = x.astype(BF16).astype(F32)
     mid = (x - hi).astype(BF16).astype(F32)
@@ -530,97 +482,143 @@
     return out
 
 
-def fwd_body(
-    len_ref, q, k, v, pw, o, qa_out, o_got, pw_got, ka, va, send_sem, recv_sem, *, bq
+def front_body(
+    len_ref, tokens, w_hbm, bias, gain, shift, pw,
+    xf_out, low_out, k_out, v_out, o_out, qa_out, o_got, pw_got,
+    own, got, w, xf, low, q, k, v, o, qa, ka, va, load_sem, store_sem, send_sem, recv_sem, *, bq,
 ):
-    head = pl.program_id(0)
-    par, pair = head % 2, head // 2
-    lane, mine, at = lanes_of(par)
     n, me = lax.axis_index("narrow"), lax.axis_index("wide")
     peer, core = {"narrow": 1 - n}, {"wide": flip(me, 0)}
-    pairs = pl.num_programs(0) // 2
     both = (send_sem, recv_sem)
-    cols = lane_part(pair, 2 * HEAD)
+    rows, cw = own.shape
+    pair_w, heads = 2 * HEAD, qa.shape[0]
+    blocks = rows // bq
+    loads = [pltpu.make_async_copy(a, b, load_sem.at[i]) for i, (a, b) in enumerate(((tokens, own), (w_hbm, w)))]
+    for load in loads:
+        load.start()
+    greet([peer, core])
+
+    def token_copy(i):
+        r = block_rows(i * bq, bq)
+        return remote(tokens.at[r], got.at[r], both, i, peer)
+
+    for i in range(blocks):
+        token_copy(i).start()
     part = block_rows((me % 2) * (pw.shape[0] // 2), pw.shape[0] // 2)
-    npairs = o.shape[1] // (2 * HEAD)
-    weights = remote(pw.at[part], pw_got.at[part], both, npairs, peer)
-    shared = remote(pw_got.at[part], pw_got.at[part], both, npairs + 1, core)
-
-    @pl.when(head == 0)
-    def _():
-        greet([peer, core])
-        weights.start()
-
-    keys = k.shape[0]
-    kpos = lax.broadcasted_iota(jnp.int32, (keys, 1), 0)
+    used = blocks + blocks * (heads // 2)
+    weights = remote(pw.at[part], pw_got.at[part], both, used, peer)
+    shared = remote(pw_got.at[part], pw_got.at[part], both, used + 1, core)
+    weights.start()
+    for load in loads:
+        load.wait()
+
+    def project(i, carry):
+        r = block_rows(i * bq, bq)
+        xf[r, lane_part(n, cw)] = own[r, :]
+        with scope("wait"):
+            token_copy(i).wait()
+        xf[r, lane_part(1 - n, cw)] = got[r, :]
+        xhat, _ = norm_rows(xf[r, :].astype(F32))
+        y = (xhat * vec(gain) + vec(shift)).astype(BF16)
+        low[r, :] = y
+        q[r, :] = (dot(y, w[0]) + bias[0:1, :].astype(F32)).astype(BF16) * jnp.asarray(HEAD**-0.5, BF16)
+        k[r, :] = dot(y, w[1]).astype(BF16)
+        v[r, :] = (dot(y, w[2]) + bias[1:2, :].astype(F32)).astype(BF16)
+        return carry
+
+    lax.fori_loop(0, blocks, project, 0)
+    stores = [
+        pltpu.make_async_copy(a, b, store_sem.at[i])
+        for i, (a, b) in enumerate(((xf, xf_out), (low, low_out), (k, k_out), (v, v_out)))
+    ]
+    for store in stores:
+        store.start()
+
+    kpos = lax.broadcasted_iota(jnp.int32, (rows, 1), 0)
     kbias = jnp.where(kpos < len_ref[0], 0.0, -1e30)
-    ka[...] = place(lane, mine, at, k[...].astype(F32), [kbias]).astype(BF16)
-    va[...] = place(lane, mine, at, v[...].astype(F32), [1.0]).astype(BF16)
     tri = lax.broadcasted_iota(jnp.int32, (bq, bq), 1) <= lax.broadcasted_iota(jnp.int32, (bq, bq), 0)
-    for i in range(q.shape[0] // bq):
-        nk = (i + 1) * bq
-        rows = pl.ds(i * bq, bq)
-        qf = q[rows, :].astype(F32)
-        qa = place(lane, mine, at, qf, [1.0])
-        s = dot_nt(qa.astype(BF16), ka[0:nk, :])
-        edge = jnp.where(tri, s[:, nk - bq :], -1e30)
-        m = jnp.max(edge, axis=1, keepdims=True)
-        if nk > bq:
-            m = jnp.maximum(m, jnp.max(s[:, : nk - bq], axis=1, keepdims=True))
-        pv = dot(jnp.exp(edge - m).astype(BF16), va[nk - bq : nk, :])
-        if nk > bq:
-            pv += dot(jnp.exp(s[:, : nk - bq] - m).astype(BF16), va[0 : nk - bq, :])
-        total = jnp.sum(jnp.where(lane == at, pv, 0.0), axis=1, keepdims=True)
-        out = (pv / total).astype(BF16).astype(F32)
-        old = o[rows, cols].astype(F32)
-        o[rows, cols] = jnp.where(mine, out, jnp.where(par == 0, 0.0, old)).astype(BF16)
-        lse = m + jnp.log(total)
-        qa_out[0, rows, :] = place(lane, mine, at, qf, [1.0, *three(lse)]).astype(BF16)
-
-    def mixed(j):
-        c = pl.ds(j * 2 * HEAD, 2 * HEAD)
-        return remote(o.at[:, c], o_got.at[:, c], both, j, peer)
-
-    for j in range(npairs):
-
-        @pl.when(head == 2 * j + 1)
+
+    def mixed(pair, i):
+        r, c = pl.ds(i * bq, bq), lane_part(pair, pair_w)
+        return remote(o.at[r, c], o_got.at[r, c], both, blocks + pair * blocks + i, peer)
+
+    def mixed_store(pair):
+        c = lane_part(pair, pair_w)
+        return pltpu.make_async_copy(o.at[:, c], o_out.at[:, c], store_sem.at[4 + pair])
+
+    def qa_store(head):
+        return pltpu.make_async_copy(qa.at[head], qa_out.at[head], store_sem.at[4 + heads // 2 + head])
+
+    def one_head(head, carry):
+        par, pair = head % 2, head // 2
+        lane, mine, at = lanes_of(par)
+        cols = lane_part(pair, pair_w)
+        ka[...] = place(lane, mine, at, k[:, cols].astype(F32), [kbias]).astype(BF16)
+        va[...] = place(lane, mine, at, v[:, cols].astype(F32), [1.0]).astype(BF16)
+        for i in range(blocks):
+            nk = (i + 1) * bq
+            r = pl.ds(i * bq, bq)
+            qf = q[r, cols].astype(F32)
+            s = dot_nt(place(lane, mine, at, qf, [1.0]).astype(BF16), ka[0:nk, :])
+            edge = jnp.where(tri, s[:, nk - bq :], -1e30)
+            m = jnp.max(edge, axis=1, keepdims=True)
+            if nk > bq:
+                m = jnp.maximum(m, jnp.max(s[:, : nk - bq], axis=1, keepdims=True))
+            pv = dot(jnp.exp(edge - m).astype(BF16), va[nk - bq : nk, :])
+            if nk > bq:
+                pv += dot(jnp.exp(s[:, : nk - bq] - m).astype(BF16), va[0 : nk - bq, :])
+            total = jnp.sum(jnp.where(lane == at, pv, 0.0), axis=1, keepdims=True)
+            out = (pv / total).astype(BF16).astype(F32)
+            old = o[r, cols].astype(F32)
+            o[r, cols] = jnp.where(mine, out, jnp.where(par == 0, 0.0, old)).astype(BF16)
+            lse = m + jnp.log(total)
+            qa[head, r, :] = place(lane, mine, at, qf, [1.0, *three(lse)]).astype(BF16)
+            when(par == 1, lambda: mixed(pair, i).start())
+        when(par == 1, lambda: mixed_store(pair).start())
+        qa_store(head).start()
+
+        @pl.when(head == 3)
         def _():
-            mixed(j).start()
-
-    @pl.when(head == 3)
-    def _():
-        weights.wait()
-        shared.start()
-
-    @pl.when(head == 2 * npairs - 1)
-    def _():
-        shared.wait()
-        for j in range(npairs):
-            mixed(j).wait()
-
-
-def attend_forward(length, q, k, v, pw, bq=256):
-    rows, width = q.shape
-    heads, pair = width // HEAD, 2 * HEAD
-    half = lambda h, *_: (0, h // 2)
-    sd = jax.ShapeDtypeStruct
+            weights.wait()
+            shared.start()
+
+        return carry
+
+    with scope("heads"):
+        lax.fori_loop(0, heads, one_head, 0)
+    for store in stores:
+        store.wait()
+    for head in range(heads):
+        qa_store(head).wait()
+    shared.wait()
+    with scope("mixed"):
+        for pair in range(heads // 2):
+            mixed_store(pair).wait()
+            for i in range(blocks):
+                mixed(pair, i).wait()
+
+
+def front_call(length, own, w, bias, gain, shift, pw, bq=256):
+    rows, cw = own.shape
+    d, lw = w.shape[1], w.shape[2]
+    heads, pair = lw // HEAD, 2 * HEAD
+    sd, vm = jax.ShapeDtypeStruct, pltpu.VMEM
+    copies = rows // bq * (1 + heads // 2) + 2
+    shapes = [(rows, d), (rows, d), (rows, lw), (rows, lw), (rows, lw), (heads, rows, pair), (rows, lw), pw.shape]
+    scratch = [(rows, cw), (rows, cw), w.shape, (rows, d), (rows, d)] + [(rows, lw)] * 4
     work = 2 * heads * rows * rows * HEAD
     return pl.pallas_call(
-        functools.partial(fwd_body, bq=bq),
-        out_shape=(
-            sd((rows, width), BF16), sd((heads, rows, pair), BF16), sd((rows, width), BF16), sd(pw.shape, BF16),
-        ),
-        grid_spec=pltpu.PrefetchScalarGridSpec(
-            num_scalar_prefetch=1,
-            grid=(heads,),
-            in_specs=[pl.BlockSpec((rows, pair), half)] * 3 + [anywhere()],
-            out_specs=[vmem(), pl.BlockSpec((1, rows, pair), lambda h, *_: (h, 0, 0)), anywhere(), anywhere()],
-            scratch_shapes=[pltpu.VMEM((rows, pair), BF16)] * 2 + sems(heads // 2 + 2, heads // 2 + 2),
-        ),
-        compiler_params=params(collective_id=2, has_side_effects=True),
-        cost_estimate=cost(4 * work, 2 * rows * width * 6, work // 256),
-        name="attend_fwd",
-    )(length, q, k, v, pw)
+        functools.partial(front_body, bq=bq),
+        out_shape=tuple(sd(a, BF16) for a in shapes),
+        in_specs=[pl.BlockSpec(memory_space=pltpu.SMEM), anywhere(), anywhere(), vmem(), vmem(), vmem(), anywhere()],
+        out_specs=(anywhere(),) * 8,
+        scratch_shapes=[vm(a, BF16) for a in scratch]
+        + [vm((heads, rows, pair), BF16), vm((rows, pair), BF16), vm((rows, pair), BF16)]
+        + sems(2, 4 + heads // 2 + heads, copies, copies),
+        compiler_params=params(collective_id=1, has_side_effects=True),
+        cost_estimate=cost(2 * rows * d * 3 * lw + 4 * work, 2 * rows * d * 8, work // 256),
+        name="front",
+    )(length, own, w, bias, gain, shift, pw)
 
 
 DOWN_ENTRY, UP_ENTRY = (2, 2), (1, 1)
@@ -898,7 +896,7 @@
     down_part_hbm, gp_own_hbm, gp_other_hbm, s_ub, s_db, s_g2, s_s2, s_pb,
     lo_got, down_out, up_out, gp_out, g0_out, g1_out, g2_out, ig, small_a, small_b,
     qa, k, v, do, o, low, wp, xf, gm, up_part, down_part, gp_src, gp_got,
-    ka, va, dk_acc, dv_acc, dqkv, gpair,
+    ka, va, kt, dk_acc, dv_acc, dqkv, gpair,
     down_box, down_part2, down_own, up_box, up_part2, up_own, gp_box, gp_part, gp_own, pair_box, pair_part, pair_own,
     down_sum, up_sum, gp_sum, pair_sum,
     gn_send, gn_got, gn_own, ig_own, ig_send, early, early_box, late_sums, late_box,
@@ -1046,6 +1044,7 @@
 
         ka[...] = place(lane, mine, extra, k[:, cols].astype(F32), [kbias, -1.0, -1.0, -1.0]).astype(BF16)
         va[...] = place(lane, mine, extra, v[:, cols].astype(F32), [-1.0, -1.0, -1.0]).astype(BF16)
+        kt[...] = ka[...].T
         dk_acc[...] = jnp.zeros_like(dk_acc)
         dv_acc[...] = jnp.zeros_like(dv_acc)
 
@@ -1061,19 +1060,20 @@
             delta = jnp.sum(jnp.where(mine, df * o[r, cols].astype(F32), 0.0), axis=1, keepdims=True)
             db = place(lane, mine, extra, df, three(delta)).astype(BF16)
             dqs = None
-            for j in range(i + 1):
-                c = pl.ds(j * bq, bq)
+            chunks = [(0, i * bq), (i * bq, bq)] if i else [(0, bq)]
+            for start, size in chunks:
+                c = pl.ds(start, size)
                 kb, vb = ka[c, :], va[c, :]
                 s = dot_nt(kb, qb)
-                if j == i:
+                if start == i * bq:
                     s = jnp.where(tri, s, -1e30)
                 p = jnp.exp(s)
                 ds = (p * dot_nt(vb, db)).astype(BF16)
                 dv_acc[c, :] += dot(p.astype(BF16), db)
                 dk_acc[c, :] += dot(ds, qb)
-                part = dot_tn(ds, kb)
+                part = dot(kt[:, c], ds)
                 dqs = part if dqs is None else dqs + part
-            put(0, r, dqs * HEAD**-0.5)
+            put(0, r, dqs.T * HEAD**-0.5)
             if i < rows // bq - 1:
                 run_hooks(head, i)
         put(1, pl.ds(0, rows), dk_acc[...])
@@ -1200,7 +1200,7 @@
             vm(qa.shape, BF16), vm((rows, lw), BF16), vm((rows, lw), BF16), vm((rows, lw), BF16), vm((rows, lw), BF16),
             vm((rows, d), BF16), vm((pairs, d, 3 * pair), BF16), vm((half, d), BF16), vm((half, d), F32),
             vm((d // 2, f), BF16), vm((f // 2, d), BF16), vm((2 * lw, cw), BF16), vm((2 * lw, cw), BF16),
-            vm((rows, pair), BF16), vm((rows, pair), BF16), vm((rows, pair), F32), vm((rows, pair), F32),
+            vm((rows, pair), BF16), vm((rows, pair), BF16), vm((pair, rows), BF16), vm((rows, pair), F32), vm((rows, pair), F32),
             vm((pairs, rows, 3 * pair), BF16), vm((pairs, d, 3 * pair), BF16),
             vm((down_rows, d), BF16), vm((f // 2, d), BF16), vm((c_down.size, d), BF16),
             vm((up_rows, f), BF16), vm((d // 2, f), BF16), vm((c_up.size, f), BF16),
@@ -1228,7 +1228,8 @@
 ):
     n = lax.axis_index("narrow")
     cw = lo.shape[1]
-    out[...] = (lo[...] + lo_got[...].astype(F32) + bias[:, lane_part(n, cw)]).astype(BF16)
+    b = vec(bias)
+    out[...] = (lo[...] + lo_got[...].astype(F32) + jnp.where(n == 0, b[:, :cw], b[:, cw:])).astype(BF16)
     ig_out[...] = ig[...]
     for p, ref in enumerate((q, k, v)):
         for c in range(3):
@@ -1295,8 +1296,9 @@
     wide = lax.axis_size("wide")
     w3 = jnp.transpose(qkv_weight, (1, 0, 2))
 
-    xf, low, q, k, v = qkv_call(tokens, w3, qv_bias, first_gain, first_shift)
-    mixed, qa, mixed_got, proj_got = attend_forward(lengths, q, k, v, proj_weight)
+    xf, low, k, v, mixed, qa, mixed_got, proj_got = front_call(
+        lengths, tokens, w3, qv_bias, first_gain, first_shift, proj_weight
+    )
     lo, lo_send, gmix, gm, up_part, down_part, gp_own, gp_other, s_ub, s_db, s_g2, s_s2, s_pb = mlp_call(
         lengths, xf, mixed, mixed_got, proj_weight, proj_got, proj_bias, second_gain, second_shift,
         up_weight, up_bias, down_weight, cotangent, wide,
@@ -1306,7 +1308,7 @@
         s_ub, s_db, s_g2, s_s2, s_pb, wide,
     )
     out, ig, o_qkv, o_qvb, o_proj, *rest = finish_call(
-        lo, lo_got, down_bias.astype(F32).reshape(1, -1), ig, gup, gdown, g0, g1, g2, gp, small_a, small_b,
+        lo, lo_got, down_bias, ig, gup, gdown, g0, g1, g2, gp, small_a, small_b,
         1.0 / (lengths.shape[0] * wide),
     )
     pb, up, ubs, down, dbs, g1, s1, g2, s2 = rest

time: 204 us -> 194 us (0.951)
  Pallas kernels: 201 us -> 192 us
    pallas_call x2 -> x1, Pallas kernels: 53 us -> 45.9 us  [front_call(): pl.pallas_call(functools.partial(front_body, bq=bq), out_shape=tuple((sd(...]
where the time goes in v8:
time: 194 us; the launch traced here: 193 us
  Pallas kernels  192 us (99%)
    pallas_call x1, Pallas kernels, back_call(): pl.pallas_call(functools.partial(back_body, bq=bq, wide=wide), out_shape=...  83.7 us
    pallas_call x1, Pallas kernels, mlp_call(): pl.pallas_call(functools.partial(mlp_body, wide=wide), out_shape=(sd((row...  51.1 us
    pallas_call x1, Pallas kernels, front_call(): pl.pallas_call(functools.partial(front_body, bq=bq), out_shape=tuple((sd(...  45.9 us
    pallas_call x1, Pallas kernels, finish_call(): pl.pallas_call(functools.partial(finish_body, factor=factor), out_shape=t...  10.9 us

profile of v8, /device:TPU:0, one launch (start us, length us, event | category | flops | bytes accessed | tf_op | source)
XLA Modules:
  0.0 193.1 jit_solution(7536134850794591322)
XLA Ops:
  1.3 45.9 %front.1 = (bf16[1024,768]{1,0:T(8,128)(2,1)}, bf16[1024,768]{1,0:T(8,128)(2,1)}, bf16[1024,384]{1,0:T(8,128)(2,1)}, bf16[1024,384]{1,0:T(8,128)(2,1)}, bf16[102...) custom-call(s32[1]{0:T(128)S(6)} %copy.29.len_ref, ...), custom_call_target="tpu_custom_call" | custom-call | flops 5033164800 | bytes 12582912 | tf_op jit(solution)/shard_map/front/pallas_call | solution.py:610
  47.2 51.1 %mlp.1 = (f32[1024,384]{1,0:T(8,128)}, bf16[1024,384]{1,0:T(8,128)(2,1)}, bf16[1024,384]{1,0:T(8,128)(2,1)}, f32[512,768]{1,0:T(8,128)}, bf16[384,1536]{1,0:T(8,...) custom-call(s32[1]{0:T(128)S(6)} %copy.29.len_ref, ...), custom_call_target="tpu_custom_call" | custom-call | flops 15703474176 | bytes 17301504 | tf_op jit(solution)/shard_map/mlp/pallas_call | solution.py:845
  98.2 83.7 %back.1 = (bf16[1024,384]{1,0:T(8,128)(2,1)}, bf16[1536,768]{1,0:T(8,128)(2,1)}, bf16[768,1536]{1,0:T(8,128)(2,1)}, bf16[768,384]{1,0:T(8,128)(2,1)}, bf16[768,3...) custom-call(s32[1]{0:T(128)S(6)} %copy.29.len_ref, ...), custom_call_target="tpu_custom_call" | custom-call | flops 11676942336 | bytes 31457280 | tf_op jit(solution)/shard_map/back/pallas_call | solution.py:1192
  182.0 10.9 %finish.1 = (bf16[1024,384]{1,0:T(8,128)(2,1)}, bf16[1024,384]{1,0:T(8,128)(2,1)}, f32[3,768,384]{2,1,0:T(8,128)}, f32[2,384]{1,0:T(2,128)}, f32[384,768]{1,0:T(...) custom-call(f32[1024,384]{1,0:T(8,128)} %get-tuple-element.63.lo, ...), custom_call_target="tpu_custom_call" | custom-call | flops 9437184 | bytes 28311552 | tf_op jit(solution)/shard_map/finish/pallas_call | solution.py:1277

commit v9 on v8

--- a/solution.py
+++ b/solution.py
@@ -483,8 +483,8 @@
 
 
 def front_body(
-    len_ref, tokens, w_hbm, bias, gain, shift, pw,
-    xf_out, low_out, k_out, v_out, o_out, qa_out, o_got, pw_got,
+    len_ref, tokens, w_hbm, bias, gain, shift, pw, cot,
+    xf_out, low_out, k_out, v_out, o_out, qa_out, o_got, pw_got, cot_head,
     own, got, w, xf, low, q, k, v, o, qa, ka, va, load_sem, store_sem, send_sem, recv_sem, *, bq,
 ):
     n, me = lax.axis_index("narrow"), lax.axis_index("wide")
@@ -496,7 +496,7 @@
     loads = [pltpu.make_async_copy(a, b, load_sem.at[i]) for i, (a, b) in enumerate(((tokens, own), (w_hbm, w)))]
     for load in loads:
         load.start()
-    greet([peer, core])
+    greet([peer, core] + [{"wide": to} for to in chip_peers(me)])
 
     def token_copy(i):
         r = block_rows(i * bq, bq)
@@ -504,11 +504,25 @@
 
     for i in range(blocks):
         token_copy(i).start()
-    part = block_rows((me % 2) * (pw.shape[0] // 2), pw.shape[0] // 2)
     used = blocks + blocks * (heads // 2)
-    weights = remote(pw.at[part], pw_got.at[part], both, used, peer)
-    shared = remote(pw_got.at[part], pw_got.at[part], both, used + 1, core)
+    slab, mine_lanes = pw.shape[0] // CHIPS, lane_part(me % 2, pw.shape[1] // 2)
+
+    def slab_of(device):
+        return pw_got.at[block_rows((device // 2) % CHIPS * slab, slab), mine_lanes]
+
+    source = pw.at[block_rows((me // 2) % CHIPS * slab, slab), mine_lanes]
+    weights = remote(source, slab_of(me), both, used, peer)
+    core_share = remote(pw_got.at[:, mine_lanes], pw_got.at[:, mine_lanes], both, used + 1, core)
+    head_copy = remote(cot.at[block_rows(n * (rows // 2), bq)], cot_head, both, used + 2, peer)
+
+    def chip_shares(came):
+        return [
+            remote(slab_of(to if came else me), slab_of(to if came else me), both, used + 3 + i, {"wide": to})
+            for i, to in enumerate(chip_peers(me))
+        ]
+
     weights.start()
+    head_copy.start()
     for load in loads:
         load.wait()
 
@@ -577,10 +591,19 @@
         when(par == 1, lambda: mixed_store(pair).start())
         qa_store(head).start()
 
+        @pl.when(head == 0)
+        def _():
+            weights.wait()
+            for share in chip_shares(False):
+                share.start()
+
         @pl.when(head == 3)
         def _():
-            weights.wait()
-            shared.start()
+            for share in chip_shares(False):
+                share.wait_send()
+            for share in chip_shares(True):
+                share.wait_recv()
+            core_share.start()
 
         return carry
 
@@ -590,7 +613,8 @@
         store.wait()
     for head in range(heads):
         qa_store(head).wait()
-    shared.wait()
+    core_share.wait()
+    head_copy.wait()
     with scope("mixed"):
         for pair in range(heads // 2):
             mixed_store(pair).wait()
@@ -598,35 +622,35 @@
                 mixed(pair, i).wait()
 
 
-def front_call(length, own, w, bias, gain, shift, pw, bq=256):
+def front_call(length, own, w, bias, gain, shift, pw, cot, bq=256):
     rows, cw = own.shape
     d, lw = w.shape[1], w.shape[2]
     heads, pair = lw // HEAD, 2 * HEAD
     sd, vm = jax.ShapeDtypeStruct, pltpu.VMEM
-    copies = rows // bq * (1 + heads // 2) + 2
-    shapes = [(rows, d), (rows, d), (rows, lw), (rows, lw), (rows, lw), (heads, rows, pair), (rows, lw), pw.shape]
+    copies = rows // bq * (1 + heads // 2) + 3 + CHIPS
+    shapes = [(rows, d), (rows, d), (rows, lw), (rows, lw), (rows, lw), (heads, rows, pair), (rows, lw), pw.shape, (bq, cw)]
     scratch = [(rows, cw), (rows, cw), w.shape, (rows, d), (rows, d)] + [(rows, lw)] * 4
     work = 2 * heads * rows * rows * HEAD
     return pl.pallas_call(
         functools.partial(front_body, bq=bq),
         out_shape=tuple(sd(a, BF16) for a in shapes),
-        in_specs=[pl.BlockSpec(memory_space=pltpu.SMEM), anywhere(), anywhere(), vmem(), vmem(), vmem(), anywhere()],
-        out_specs=(anywhere(),) * 8,
+        in_specs=[pl.BlockSpec(memory_space=pltpu.SMEM), anywhere(), anywhere(), vmem(), vmem(), vmem(), anywhere(), anywhere()],
+        out_specs=(anywhere(),) * 9,
         scratch_shapes=[vm(a, BF16) for a in scratch]
         + [vm((heads, rows, pair), BF16), vm((rows, pair), BF16), vm((rows, pair), BF16)]
         + sems(2, 4 + heads // 2 + heads, copies, copies),
         compiler_params=params(collective_id=1, has_side_effects=True),
         cost_estimate=cost(2 * rows * d * 3 * lw + 4 * work, 2 * rows * d * 8, work // 256),
         name="front",
-    )(length, own, w, bias, gain, shift, pw)
+    )(length, own, w, bias, gain, shift, pw, cot)
 
 
 DOWN_ENTRY, UP_ENTRY = (2, 2), (1, 1)
-DOWN_KINDS, UP_KINDS = (0, 0), (0, 1)
+DOWN_KINDS, UP_KINDS, PAIR_KINDS = (0, 0), (0, 1), (0, 0, 3)
 
 
 def mlp_body(
-    len_ref, xf_hbm, mo_hbm, mr_hbm, pwo_hbm, pwr_hbm, pb, gain, shift, ub, up_hbm, down_hbm, cot_hbm,
+    len_ref, xf_hbm, mo_hbm, mr_hbm, pwo_hbm, pwr_hbm, pb, gain, shift, ub, up_hbm, down_hbm, cot_hbm, cot_head,
     lo_out, lo_send_out, gmix, gm_out, up_part, down_part, gp_own, gp_other, sum_ub, sum_db, sum_g, sum_s, sum_pb,
     xf, mo, mr, pwo, pwr, up, down, cot, cot_got, cf, lo, lo_send, mid, second, active, slope, gh,
     gs_send, gs_got, gs_own, gdown, gup, box, up_box, gm, glow, gmix_send, load_sem, store_sem, nsend, nrecv, wsend, wrecv,
@@ -659,7 +683,9 @@
 
     for a, side in enumerate((n, 1 - n)):
         for j in range(each):
-            cot_copy(side, j, a).start()
+            if (a, j) != (0, 0):
+                cot_copy(side, j, a).start()
+    head_load = load(cot_head, cot_got.at[block_rows((1 - n) * half, block)])
     down_load = load(down_hbm, down)
     cot_load = load(cot_hbm, cot)
     rest = [load(a.at[own], b.at[own]) for a, b in ((xf_hbm, xf), (mo_hbm, mo), (mr_hbm, mr))]
@@ -717,6 +743,27 @@
         down_load.wait()
     with scope("fwd_peer"):
         every(1 - n, forward)
+    with scope("cot_wait"):
+        cot_load.wait()
+        head_load.wait()
+        for j in range(1, each):
+            cot_copy(n, j, 0).wait()
+
+    def gs_copy(j):
+        r = block_rows(j * block, block)
+        return remote(gs_send.at[r], gs_got.at[r], narrow, 2 * each + j, peer)
+
+    def for_peer(j, carry):
+        gs_send[block_rows(j * block, block), :] = backward((1 - n) * half + j * block).astype(BF16)
+        gs_copy(j).start()
+        return carry
+
+    def for_own(j, carry):
+        gs_own[block_rows(j * block, block), :] = backward(n * half + j * block)
+        return carry
+
+    with scope("for_peer"):
+        lax.fori_loop(0, each, for_peer, 0)
     for copy in rest:
         copy.wait()
     with scope("fwd_own"):
@@ -730,26 +777,6 @@
 
     store(lo, lo_out)
     store(lo_send, lo_send_out)
-    with scope("cot_wait"):
-        cot_load.wait()
-        for j in range(each):
-            cot_copy(n, j, 0).wait()
-
-    def gs_copy(j):
-        r = block_rows(j * block, block)
-        return remote(gs_send.at[r], gs_got.at[r], narrow, 2 * each + j, peer)
-
-    def for_peer(j, carry):
-        gs_send[block_rows(j * block, block), :] = backward((1 - n) * half + j * block).astype(BF16)
-        gs_copy(j).start()
-        return carry
-
-    def for_own(j, carry):
-        gs_own[block_rows(j * block, block), :] = backward(n * half + j * block)
-        return carry
-
-    with scope("for_peer"):
-        lax.fori_loop(0, each, for_peer, 0)
     with scope("cot_wait2"):
         for j in range(each):
             cot_copy(1 - n, j, 1).wait()
@@ -836,7 +863,7 @@
             copy.wait()
 
 
-def mlp_call(length, xf, mo, mr, pwo, pwr, pb, gain, shift, up, ub, down, cot, wide):
+def mlp_call(length, xf, mo, mr, pwo, pwr, pb, gain, shift, up, ub, down, cot, cot_head, wide):
     rows, d = xf.shape
     f, lw, cw = up.shape[1], mo.shape[1], cot.shape[1]
     half = rows // 2
@@ -849,7 +876,7 @@
             sd((d // 2, f), BF16), sd((f // 2, d), BF16), sd((2 * lw, cw), BF16), sd((2 * lw, cw), BF16),
             sd((1, f), F32), sd((1, d), F32), sd((1, d), F32), sd((1, d), F32), sd((1, d), F32),
         ),
-        in_specs=[pl.BlockSpec(memory_space=pltpu.SMEM)] + [anywhere()] * 5 + [vmem()] * 4 + [anywhere()] * 3,
+        in_specs=[pl.BlockSpec(memory_space=pltpu.SMEM)] + [anywhere()] * 5 + [vmem()] * 4 + [anywhere()] * 4,
         out_specs=(anywhere(), anywhere(), vmem(), anywhere()) + (vmem(),) * 9,
         scratch_shapes=[
             vm((rows, d), BF16), vm((rows, lw), BF16), vm((rows, lw), BF16), vm((lw, d), BF16), vm((lw, d), BF16),
@@ -863,27 +890,30 @@
         compiler_params=params(collective_id=3, has_side_effects=True),
         cost_estimate=cost(2 * rows * d * (d + 6 * f), 2 * (rows * d * 8 + 2 * d * f), rows * f),
         name="mlp",
-    )(length, xf, mo, mr, pwo, pwr, pb, gain, shift, ub, up, down, cot)
-
-
+    )(length, xf, mo, mr, pwo, pwr, pb, gain, shift, ub, up, down, cot, cot_head)
+
+
+START_TICKS = "U0D1D0U1"
 HEAD_TICKS = (
-    ((1, 2), "U1"),
-    ((1, 3), "D1U0D0Q0"),
-    ((2, 2), "Q0U1"),
-    ((2, 3), "D1"),
-    ((3, 1), "U0SA"),
-    ((3, 2), "D0P0"),
-    ((3, 3), "SAQ0U1Q1"),
-    ((4, 1), "D1"),
-    ((4, 2), "U0Q1"),
-    ((4, 3), "D0"),
-    ((5, 0), "P0"),
-    ((5, 3), "Q0D1U1Q2"),
+    ((0, 3), "SA"),
+    ((1, 2), "D1"),
+    ((1, 3), "D0Q0"),
+    ((2, 0), "U0U1"),
+    ((2, 2), "D1Q0"),
+    ((2, 3), ""),
+    ((3, 0), "D0"),
+    ((3, 1), "SA"),
+    ((3, 2), "P0U0"),
+    ((3, 3), "Q0SAD1U1Q1"),
+    ((4, 1), "D0"),
+    ((4, 2), "P0Q1"),
+    ((4, 3), "U0Q0"),
+    ((5, 3), "D1Q1SAQ2"),
 )
-PART_TICKS = ("U0D0SAQ1P0Q2", "Q0D1U1", "Q1U0", "D0P0", "Q0Q2")
+PART_TICKS = ("D0U1P0", "Q2U0", "Q1Q0D1", "", "D0P0U1")
 LAST_TICKS = (
-    "D1Q1P0U1Q2Q1", "norm0", "U0Q2D0Q0D1Q2P0U1", "D1Q1U0", "norm1", "Q0Q2P0D0D0U1Q1Q0",
-    "U1Q2SBU0SBP0Q1U0", "Q2Q0Q0P0SBQ1P0Q1", "Q2Q2",
+    "U0Q1Q2Q0D1P0D0", "norm0", "Q1U1U0Q0Q2Q1D1P0", "norm1", "U1D1U0Q0D0Q1Q2SB", "D0P0SBU1U0Q0Q1U0",
+    "P0Q2Q2Q0SBU1Q0P0", "Q1U1P0Q1",
 )
 
 
@@ -962,6 +992,7 @@
     for p, out in zip(range(pairs), (g0_out, g1_out, g2_out)):
         groups[f"Q{p}"] = group(
             gpair.at[p], pair_box.at[p], pair_part.at[p], pair_own.at[p], pair_sum.at[p], out,
+            kinds=(PAIR_KINDS[p],),
         )[0]
 
     dr, fr, lr = d // 128, s_ub.shape[1] // 128, lw // 128
@@ -987,9 +1018,8 @@
                 groups[name].tick()
 
     part_load.wait()
-    tick("D0D1")
     up_load.wait()
-    tick("U0U1SA")
+    tick(START_TICKS)
 
     kpos = lax.broadcasted_iota(jnp.int32, (rows, 1), 0)
     kbias = jnp.where(kpos < len_ref[0], 0.0, -1e30)
@@ -1296,12 +1326,12 @@
     wide = lax.axis_size("wide")
     w3 = jnp.transpose(qkv_weight, (1, 0, 2))
 
-    xf, low, k, v, mixed, qa, mixed_got, proj_got = front_call(
-        lengths, tokens, w3, qv_bias, first_gain, first_shift, proj_weight
+    xf, low, k, v, mixed, qa, mixed_got, proj_got, cot_head = front_call(
+        lengths, tokens, w3, qv_bias, first_gain, first_shift, proj_weight, cotangent
     )
     lo, lo_send, gmix, gm, up_part, down_part, gp_own, gp_other, s_ub, s_db, s_g2, s_s2, s_pb = mlp_call(
         lengths, xf, mixed, mixed_got, proj_weight, proj_got, proj_bias, second_gain, second_shift,
-        up_weight, up_bias, down_weight, cotangent, wide,
+        up_weight, up_bias, down_weight, cotangent, cot_head, wide,
     )
     lo_got, gdown, gup, gp, g0, g1, g2, ig, small_a, small_b = back_call(
         lengths, qa, k, v, gmix, mixed, low, w3, xf, gm, first_gain, lo_send, up_part, down_part, gp_own, gp_other,

time: 194 us -> 188 us (0.969)
  Pallas kernels: 192 us -> 186 us
    pallas_call x1, Pallas kernels: 51.1 us -> 45.2 us  [mlp_call(): pl.pallas_call(functools.partial(mlp_body, wide=wide), out_shape=(sd((row...]
    pallas_call x1, Pallas kernels: 45.9 us -> 48.3 us  [front_call(): pl.pallas_call(functools.partial(front_body, bq=bq), out_shape=tuple((sd(...]
    pallas_call x1, Pallas kernels: 83.7 us -> 81.5 us  [back_call(): pl.pallas_call(functools.partial(back_body, bq=bq, wide=wide), out_shape=...]
where the time goes in v9:
time: 188 us; the launch traced here: 187 us
  Pallas kernels  186 us (99%)
    pallas_call x1, Pallas kernels, back_call(): pl.pallas_call(functools.partial(back_body, bq=bq, wide=wide), out_shape=...  81.5 us
    pallas_call x1, Pallas kernels, front_call(): pl.pallas_call(functools.partial(front_body, bq=bq), out_shape=tuple((sd(...  48.3 us
    pallas_call x1, Pallas kernels, mlp_call(): pl.pallas_call(functools.partial(mlp_body, wide=wide), out_shape=(sd((row...  45.2 us
    pallas_call x1, Pallas kernels, finish_call(): pl.pallas_call(functools.partial(finish_body, factor=factor), out_shape=t...  10.9 us

profile of v9, /device:TPU:0, one launch (start us, length us, event | category | flops | bytes accessed | tf_op | source)
XLA Modules:
  0.0 187.5 jit_solution(15566911161591919417)
XLA Ops:
  1.3 48.3 %front.1 = (bf16[1024,768]{1,0:T(8,128)(2,1)}, bf16[1024,768]{1,0:T(8,128)(2,1)}, bf16[1024,384]{1,0:T(8,128)(2,1)}, bf16[1024,384]{1,0:T(8,128)(2,1)}, bf16[102...) custom-call(s32[1]{0:T(128)S(6)} %copy.29.len_ref, ...), custom_call_target="tpu_custom_call" | custom-call | flops 5033164800 | bytes 12582912 | tf_op jit(solution)/shard_map/front/pallas_call | solution.py:634
  49.6 45.2 %mlp.1 = (f32[1024,384]{1,0:T(8,128)}, bf16[1024,384]{1,0:T(8,128)(2,1)}, bf16[1024,384]{1,0:T(8,128)(2,1)}, f32[512,768]{1,0:T(8,128)}, bf16[384,1536]{1,0:T(8,...) custom-call(s32[1]{0:T(128)S(6)} %copy.29.len_ref, ...), custom_call_target="tpu_custom_call" | custom-call | flops 15703474176 | bytes 17301504 | tf_op jit(solution)/shard_map/mlp/pallas_call | solution.py:872
  94.9 81.5 %back.1 = (bf16[1024,384]{1,0:T(8,128)(2,1)}, bf16[1536,768]{1,0:T(8,128)(2,1)}, bf16[768,1536]{1,0:T(8,128)(2,1)}, bf16[768,384]{1,0:T(8,128)(2,1)}, bf16[768,3...) custom-call(s32[1]{0:T(128)S(6)} %copy.29.len_ref, ...), custom_call_target="tpu_custom_call" | custom-call | flops 11676942336 | bytes 31457280 | tf_op jit(solution)/shard_map/back/pallas_call | solution.py:1222
  176.4 10.9 %finish.1 = (bf16[1024,384]{1,0:T(8,128)(2,1)}, bf16[1024,384]{1,0:T(8,128)(2,1)}, f32[3,768,384]{2,1,0:T(8,128)}, f32[2,384]{1,0:T(2,128)}, f32[384,768]{1,0:T(...) custom-call(f32[1024,384]{1,0:T(8,128)} %get-tuple-element.65.lo, ...), custom_call_target="tpu_custom_call" | custom-call | flops 9437184 | bytes 28311552 | tf_op jit(solution)/shard_map/finish/pallas_call | solution.py:1307

commit v10 on v9

--- a/solution.py
+++ b/solution.py
@@ -819,12 +819,14 @@
         for j in range(each):
             gs_copy(j).wait()
 
+    fine = min(128, half)
+
     def gmix_copy(j):
-        r = block_rows(n * half + j * block, block)
-        return remote(gmix_send.at[block_rows(j * block, block)], gmix.at[r], narrow, 3 * each + j, peer)
+        r = block_rows(n * half + j * fine, fine)
+        return remote(gmix_send.at[block_rows(j * fine, fine)], gmix.at[r], narrow, 3 * each + j, peer)
 
     def back_norm(j, carry):
-        r, rh = block_rows(n * half + j * block, block), block_rows(j * block, block)
+        r, rh = block_rows(n * half + j * fine, fine), block_rows(j * fine, fine)
         g = gs_own[rh, :] + gs_got[rh, :].astype(F32)
         xhat, scale = norm_rows(mid[r, :])
         gg = g * vec(gain)
@@ -845,7 +847,7 @@
         return carry
 
     with scope("back_norm"):
-        lax.fori_loop(0, each, back_norm, 0)
+        lax.fori_loop(0, half // fine, back_norm, 0)
     store(gm, gm_out)
     advance("across", *reduce_up)
     with scope("proj"):
@@ -855,7 +857,7 @@
             dst[0:lw, :] = total[:, :cw]
             dst[lw : 2 * lw, :] = total[:, cw:]
     with scope("gmix_wait"):
-        for j in range(each):
+        for j in range(half // fine):
             gmix_copy(j).wait()
     advance("leave", *reduce_down, *reduce_up)
     with scope("store"):
@@ -886,7 +888,7 @@
             vm((half, d), BF16), vm((half, d), BF16), vm((half, d), F32), vm((f, d), BF16), vm((d, f), BF16),
             vm((f, d), BF16), vm((d, f), BF16), vm((half, d), F32), vm((half, d), BF16), vm((half, lw), BF16),
         ]
-        + sems(12, 4, 4 * each, 4 * each, 8, 8),
+        + sems(12, 4, 3 * each + half // min(128, half), 3 * each + half // min(128, half), 8, 8),
         compiler_params=params(collective_id=3, has_side_effects=True),
         cost_estimate=cost(2 * rows * d * (d + 6 * f), 2 * (rows * d * 8 + 2 * d * f), rows * f),
         name="mlp",
@@ -1241,7 +1243,7 @@
             vm((half, d), BF16), vm((half, d), BF16), vm((half, d), F32), vm((block, d), F32), vm((half, cw), BF16),
             vm((rows_a, 128), F32), vm((slots, rows_a, 128), F32), vm((rows_b, 128), F32), vm((slots, rows_b, 128), F32),
         ]
-        + sems(8 * pairs + 8, 8, 4 + 2 * each, 4 + 2 * each, 17 + 3 * CHIPS, semaphores),
+        + sems(8 * pairs + 8, 8, 4 + 2 * each, 4 + 2 * each, 9 + 3 * CHIPS, semaphores),
         compiler_params=params(collective_id=4, has_side_effects=True),
         cost_estimate=cost(10 * work + 4 * rows * d * 3 * lw, 2 * rows * d * 20, work // 256),
         name="back",

time: 188 us -> 188 us (level)
  no operation moved by 1% of the time
where the time goes in v10:
time: 188 us; the launch traced here: 187 us
  Pallas kernels  186 us (99%)
    pallas_call x1, Pallas kernels, back_call(): pl.pallas_call(functools.partial(back_body, bq=bq, wide=wide), out_shape=...  81.7 us
    pallas_call x1, Pallas kernels, front_call(): pl.pallas_call(functools.partial(front_body, bq=bq), out_shape=tuple((sd(...  48.3 us
    pallas_call x1, Pallas kernels, mlp_call(): pl.pallas_call(functools.partial(mlp_body, wide=wide), out_shape=(sd((row...  45 us
    pallas_call x1, Pallas kernels, finish_call(): pl.pallas_call(functools.partial(finish_body, factor=factor), out_shape=t...  10.9 us

profile of v10, /device:TPU:0, one launch (start us, length us, event | category | flops | bytes accessed | tf_op | source)
XLA Modules:
  0.0 187.5 jit_solution(4302938573045813167)
XLA Ops:
  1.3 48.3 %front.1 = (bf16[1024,768]{1,0:T(8,128)(2,1)}, bf16[1024,768]{1,0:T(8,128)(2,1)}, bf16[1024,384]{1,0:T(8,128)(2,1)}, bf16[1024,384]{1,0:T(8,128)(2,1)}, bf16[102...) custom-call(s32[1]{0:T(128)S(6)} %copy.29.len_ref, ...), custom_call_target="tpu_custom_call" | custom-call | flops 5033164800 | bytes 12582912 | tf_op jit(solution)/shard_map/front/pallas_call | solution.py:634
  49.6 45.0 %mlp.1 = (f32[1024,384]{1,0:T(8,128)}, bf16[1024,384]{1,0:T(8,128)(2,1)}, bf16[1024,384]{1,0:T(8,128)(2,1)}, f32[512,768]{1,0:T(8,128)}, bf16[384,1536]{1,0:T(8,...) custom-call(s32[1]{0:T(128)S(6)} %copy.29.len_ref, ...), custom_call_target="tpu_custom_call" | custom-call | flops 15703474176 | bytes 17301504 | tf_op jit(solution)/shard_map/mlp/pallas_call | solution.py:874
  94.7 81.7 %back.1 = (bf16[1024,384]{1,0:T(8,128)(2,1)}, bf16[1536,768]{1,0:T(8,128)(2,1)}, bf16[768,1536]{1,0:T(8,128)(2,1)}, bf16[768,384]{1,0:T(8,128)(2,1)}, bf16[768,3...) custom-call(s32[1]{0:T(128)S(6)} %copy.29.len_ref, ...), custom_call_target="tpu_custom_call" | custom-call | flops 11676942336 | bytes 31457280 | tf_op jit(solution)/shard_map/back/pallas_call | solution.py:1224
  176.4 10.9 %finish.1 = (bf16[1024,384]{1,0:T(8,128)(2,1)}, bf16[1024,384]{1,0:T(8,128)(2,1)}, f32[3,768,384]{2,1,0:T(8,128)}, f32[2,384]{1,0:T(2,128)}, f32[384,768]{1,0:T(...) custom-call(f32[1024,384]{1,0:T(8,128)} %get-tuple-element.65.lo, ...), custom_call_target="tpu_custom_call" | custom-call | flops 9437184 | bytes 28311552 | tf_op jit(solution)/shard_map/finish/pallas_call | solution.py:1309
